TPU v7x, 256 devices: a whole 4x4x8 slice. The times are simulated.
256 devices in a mesh: row: 16 (over z, core), col: 16 (over x, y).
Axes of the slice: x: 4, y: 4, z: 8, core: 2. Of those that a mesh axis runs over, the one named last changes fastest.
Arguments:
- features: bfloat16 [16, 16, 1024, 602], P('row', 'col'), may hold values from -6 to 6
- local_mask: int32 [16, 16, 1024, 1024], P('row', 'col'), may hold values 0 or 1
- halo_mask: int32 [16, 16, 1024, 512], P('row', 'col'), may hold values 0 or 1
- boundary_index: int32 [16, 16, 512], P('row', 'col'), may hold values from 0 to 1023
- labels: int32 [16, 16, 1024], P('row', 'col'), may hold values from 0 to 40
- halo_first: bfloat16 [16, 16, 512, 602], P('row', 'col'), may hold values from -6 to 6
- halo_second: bfloat16 [16, 16, 512, 256], P('row', 'col'), may hold values from -4 to 4
- halo_third: bfloat16 [16, 16, 512, 256], P('row', 'col'), may hold values from -4 to 4
- return_second: bfloat16 [16, 16, 512, 256], P('row', 'col'), may hold values from -0.0059814453 to 0.0059814453
- return_third: bfloat16 [16, 16, 512, 256], P('row', 'col'), may hold values from -0.0059814453 to 0.0059814453
- weight_first: bfloat16 [602, 256], replicated, may hold values from -1 to 1
- weight_second: bfloat16 [256, 256], replicated, may hold values from -1.5 to 1.5
- weight_third: bfloat16 [256, 41], replicated, may hold values from -1.5 to 1.5
Outputs:
- grad_first: float32 [602, 256], replicated
- grad_second: float32 [256, 256], replicated
- grad_third: float32 [256, 41], replicated
- next_second: bfloat16 [16, 16, 512, 256], P('row', 'col')
- next_third: bfloat16 [16, 16, 512, 256], P('row', 'col')
- back_second: bfloat16 [16, 16, 512, 256], P('row', 'col')
- back_third: bfloat16 [16, 16, 512, 256], P('row', 'col')
All inputs are finite; a program needn't handle non-finite values. No bound on the sum of `local_mask` or of `halo_mask` on one device may be relied on, other than what follows from the above.
Results may differ from a plain program's by a relative error of at most 0.007.
Values may be sent and summed in bfloat16 or wider, within the bound.
No kernel may reach another device: no remote copies, remote signals or barrier semaphores. Data moves between devices by JAX's collectives and lax.ppermute only.
A program may use at most 64 MiB of HBM per device.

v0:
```python
import jax
import jax.numpy as jnp
from jax import lax
from jax.sharding import Mesh
from jax.sharding import PartitionSpec as P

ROW = ("row_0", "row_1")
COL = ("col_0", "col_1")


def padded(shard, sides, width, wrap):
    for axis, dim in sides:
        size, length = (lax.axis_size(axis), shard.shape[dim])
        up = [(i, (i + 1) % size) for i in range(size if wrap else size - 1)]
        down = [(j, i) for i, j in up]
        last = lax.slice_in_dim(shard, length - width, length, axis=dim)
        initial = lax.slice_in_dim(shard, 0, width, axis=dim)
        before = lax.ppermute(last, axis, up)
        after = lax.ppermute(initial, axis, down)
        shard = jnp.concatenate([before, shard, after], axis=dim)
    return shard


def filled_up(lines, size):
    spare = -len(lines) % size
    return jnp.pad(lines, [(0, spare)] + [(0, 0)] * (lines.ndim - 1))


def copy_for_each(shard, axis):
    size = lax.axis_size(axis)
    return lax.all_to_all(
        jnp.broadcast_to(shard[None], (size, *shard.shape)), axis, 0, 0, tiled=True
    )


def joined_along(pieces, dim):
    pieces = jnp.moveaxis(pieces, 0, dim)
    lengths = pieces.shape
    return pieces.reshape(*lengths[:dim], lengths[dim] * lengths[dim + 1], *lengths[dim + 2 :])


def gather_axes(shard, axes, dim):
    far, near = axes
    pieces = copy_for_each(copy_for_each(shard, far), near)
    return joined_along(pieces.swapaxes(0, 1).reshape(-1, *shard.shape), dim)


def cut_along(shard, dim, size):
    lengths = shard.shape
    pieces = shard.reshape(*lengths[:dim], size, lengths[dim] // size, *lengths[dim + 1 :])
    return jnp.moveaxis(pieces, dim, 0)


def sum_at_owner(shard, axis, dim):
    size = lax.axis_size(axis)
    pieces = lax.all_to_all(cut_along(shard, dim, size), axis, 0, 0, tiled=True)
    return jnp.sum(pieces, axis=0)


def sum_in_two_steps(shard, axes, dim):
    far, near = axes
    own = sum_at_owner(cut_along(shard, dim, lax.axis_size(far)), near, dim + 1)
    return jnp.sum(lax.all_to_all(own, far, 0, 0, tiled=True), axis=0)


def nested_sum(shard, axes):
    padded = filled_up(shard, lax.axis_size(axes[0]) * lax.axis_size(axes[1]))
    whole = gather_axes(sum_in_two_steps(padded, axes, 0), axes, 0)
    return lax.slice_in_dim(whole, 0, len(shard)).reshape(shard.shape)


def in_one(arrays, axis):
    ravelled, at, gathered = (jnp.concatenate([a.reshape(-1) for a in arrays]), 0, [])
    total = nested_sum(ravelled, axis)
    for a in arrays:
        gathered.append(total[at : at + a.size].reshape(a.shape))
        at += a.size
    return tuple(gathered)


def slope(pre):
    sigma = jax.nn.sigmoid(pre)
    return sigma * (1.0 + pre * (1.0 - sigma))


def spread(local_bf, halo_bf, inverse, values, remote):
    summed = jnp.dot(local_bf, values, preferred_element_type=jnp.float32)
    summed = summed + values.astype(jnp.float32)
    summed = summed + jnp.dot(halo_bf, remote, preferred_element_type=jnp.float32)
    return (summed * inverse).astype(jnp.bfloat16)


def retract(local_bf, halo_bf, inverse, upstream, weight, hits, returned):
    across = jnp.dot(upstream, weight.T, preferred_element_type=jnp.float32)
    scaled = (across * inverse).astype(jnp.bfloat16)
    carried = jnp.dot(local_bf.T, scaled, preferred_element_type=jnp.float32) + scaled.astype(
        jnp.float32
    )
    carried = carried + jnp.dot(hits, returned, preferred_element_type=jnp.float32)
    outgoing = jnp.dot(halo_bf.T, scaled, preferred_element_type=jnp.float32).astype(jnp.bfloat16)
    return (carried, outgoing)


def arrange(vertical, lateral, shape):
    joined = jnp.concatenate([vertical[0:1], vertical[3:4], lateral[0:1], lateral[3:4]], axis=0)
    return joined.reshape(shape)[None, None]


def trade_features(sent):
    parted = sent.reshape((4, sent.shape[0] // 4, sent.shape[1]))
    vertical = padded(parted[0:2], ((ROW, 0),), 1, False)
    lateral = padded(parted[2:4], ((COL, 0),), 1, False)
    return arrange(vertical, lateral, sent.shape)


def trade_gradients(sent):
    parted = sent.reshape((4, sent.shape[0] // 4, sent.shape[1]))
    vertical = padded(parted[0:2], ((ROW, 0),), 1, False)
    lateral = padded(parted[2:4], ((COL, 0),), 1, False)
    return arrange(vertical, lateral, sent.shape)


def per_device(
    features,
    local_mask,
    halo_mask,
    boundary_index,
    labels,
    halo_first,
    halo_second,
    halo_third,
    return_second,
    return_third,
    weight_first,
    weight_second,
    weight_third,
):
    features = features[0, 0]
    local_mask = local_mask[0, 0]
    halo_mask = halo_mask[0, 0]
    boundary_index = boundary_index[0, 0]
    labels = labels[0, 0]
    local_bf = local_mask.astype(jnp.bfloat16)
    halo_bf = halo_mask.astype(jnp.bfloat16)
    degree = (
        1.0
        + jnp.sum(local_mask, axis=1).astype(jnp.float32)
        + jnp.sum(halo_mask, axis=1).astype(jnp.float32)
    )
    inverse = (1.0 / degree)[:, None]
    node_rows = features.shape[0]
    hits = (jnp.arange(node_rows, dtype=jnp.int32)[:, None] == boundary_index[None, :]).astype(
        jnp.bfloat16
    )
    mixed_one = spread(local_bf, halo_bf, inverse, features, halo_first[0, 0])
    pre_one = jnp.dot(mixed_one, weight_first, preferred_element_type=jnp.float32)
    hidden_one = jax.nn.silu(pre_one).astype(jnp.bfloat16)
    next_second = trade_features(jnp.take(hidden_one, boundary_index, axis=0))
    mixed_two = spread(local_bf, halo_bf, inverse, hidden_one, halo_second[0, 0])
    pre_two = jnp.dot(mixed_two, weight_second, preferred_element_type=jnp.float32)
    hidden_two = jax.nn.silu(pre_two).astype(jnp.bfloat16)
    next_third = trade_features(jnp.take(hidden_two, boundary_index, axis=0))
    mixed_three = spread(local_bf, halo_bf, inverse, hidden_two, halo_third[0, 0])
    logits = jnp.dot(mixed_three, weight_third, preferred_element_type=jnp.float32)
    expo = jnp.exp(logits)
    probs = expo / jnp.sum(expo, axis=1, keepdims=True)
    target = (labels[:, None] == jnp.arange(logits.shape[1], dtype=jnp.int32)[None, :]).astype(
        jnp.float32
    )
    upstream_three = ((probs - target) / node_rows).astype(jnp.bfloat16)
    grad_three = jnp.dot(mixed_three.T, upstream_three, preferred_element_type=jnp.float32)
    carried_two, outgoing_three = retract(
        local_bf, halo_bf, inverse, upstream_three, weight_third, hits, return_third[0, 0]
    )
    back_third = trade_gradients(outgoing_three)
    upstream_two = (carried_two * slope(pre_two)).astype(jnp.bfloat16)
    grad_two = jnp.dot(mixed_two.T, upstream_two, preferred_element_type=jnp.float32)
    carried_one, outgoing_two = retract(
        local_bf, halo_bf, inverse, upstream_two, weight_second, hits, return_second[0, 0]
    )
    back_second = trade_gradients(outgoing_two)
    upstream_one = (carried_one * slope(pre_one)).astype(jnp.bfloat16)
    grad_one = jnp.dot(mixed_one.T, upstream_one, preferred_element_type=jnp.float32)
    grad_one, grad_two, grad_three = in_one(
        (grad_one, grad_two, grad_three), (("row_0", "row_1", "col_0"), "col_1")
    )
    return (grad_one, grad_two, grad_three, next_second, next_third, back_second, back_third)


def solution(mesh):
    torus = Mesh(mesh.devices.reshape(8, 2, 4, 4), ("row_0", "row_1", "col_0", "col_1"))
    in_specs = (
        P(ROW, COL, None, None),
        P(ROW, COL, None, None),
        P(ROW, COL, None, None),
        P(ROW, COL, None),
        P(ROW, COL, None),
        P(ROW, COL, None, None),
        P(ROW, COL, None, None),
        P(ROW, COL, None, None),
        P(ROW, COL, None, None),
        P(ROW, COL, None, None),
        P(),
        P(),
        P(),
    )
    out_specs = (
        P(),
        P(),
        P(),
        P(ROW, COL, None, None),
        P(ROW, COL, None, None),
        P(ROW, COL, None, None),
        P(ROW, COL, None, None),
    )
    return jax.shard_map(
        per_device, mesh=torus, in_specs=in_specs, out_specs=out_specs, check_vma=False
    )
```

profile of v0, /device:TPU:25, one launch (start us, length us, event | category | flops | bytes accessed | tf_op | source)
XLA Modules:
  0.0 165.8 jit_solution(1159538102248271119)
XLA Ops:
  0.6 2.7 %fusion.74 = (bf16[1,1,1024,512]{3,2,1,0:T(8,128)(2,1)S(1)}, s32[1024]{0:T(1024)S(1)}) fusion(s32[1,1,1024,512]{3,2,1,0:T(8,128)} %param.17), kind=kLoop, calls=%fused_computation.102 | loop fusion | flops 1047552 | bytes 3149824 | tf_op jit(solution)/shard_map/convert_element_type | solution.py:144
  3.3 4.3 %fusion.73 = (s32[1024]{0:T(1024)S(1)}, bf16[1,1,1024,1024]{3,2,1,0:T(8,128)(2,1)S(1)}) fusion(s32[1,1,1024,1024]{3,2,1,0:T(8,128)} %param.16), kind=kLoop, calls=%fused_computation.101 | loop fusion | flops 2096128 | bytes 6295552 | tf_op jit(solution)/shard_map/reduce_sum | solution.py:147
  20.3 3.5 %fusion.30 = f32[1024,256]{1,0:T(8,128)} fusion(bf16[1024,256]{1,0:T(8,128)(2,1)S(1)} %fusion.47, bf16[1,1,1024,1024]{3,2,1,0:T(8,128)(2,1)} %copy-done.1), kind=kOutput, calls=%fused_computation.30 | convolution fusion | flops 537395200 | bytes 3670016 | tf_op jit(solution)/shard_map/dot_general | solution.py:96
  23.9 4.1 %fusion.49 = f32[602,256]{1,0:T(8,128)} fusion(bf16[1024,602]{0,1:T(8,128)(2,1)} %copy-done.3, f32[1024,256]{1,0:T(8,128)} %fusion.30, f32[1024,256]{1,0:T(8,128)} %get-tuple-element.52, s32[512]{0:T(512)S(1)} %bitcast.152, bf16[1,1,512,256]{3,2,1,0:T(8,128)(2,1)} %param.23), kind=kOutput, calls=%fused_computation.41 | convolution fusion | flops 587202560 | bytes 4210688 | tf_op jit(solution)/shard_map/dot_general | solution.py:183
  31.2 3.2 %reshape_reshape.6 = f32[64,4,899]{2,1,0:T(4,128)} reshape(f32[230144]{0:T(1024)} %pad_maximum_fusion) | data formatting | bytes 1841152 | tf_op jit(solution)/shard_map/reshape;reshape | solution.py:50
  34.4 2.8 %copy.43 = f32[4,64,899]{2,1,0:T(8,128)} copy(f32[4,64,899]{2,0,1:T(4,128)} %bitcast.144) | data formatting | bytes 1841152 | tf_op jit(solution)/shard_map/transpose | solution.py:51
  37.2 4.2 %all-to-all-start = ((f32[4,64,899]{2,1,0:T(8,128)}), f32[4,64,899]{2,1,0:T(8,128)}, u32[]{:S(2)}, u32[]{:S(2)}) async-start(f32[4,64,899]{2,1,0:T(8,128)} %copy.43), calls=%async_computation | async-start | bytes 2097152 | tf_op jit(solution)/shard_map/all_to_all | solution.py:56
  41.5 2.0 %gather_fusion = bf16[512,256]{1,0:T(8,128)(2,1)S(1)} fusion(bf16[1024,256]{1,0:T(8,128)(2,1)S(1)} %get-tuple-element.51, s32[1024]{0:T(1024)S(1)} %pad_clamp_fusion), kind=kCustom, calls=%fused_computation.clone | custom fusion | bytes 526336 | tf_op jit(solution)/shard_map/jit(_take)/gather | solution.py:158
  43.4 2.0 %gather_fusion.1 = bf16[512,256]{1,0:T(8,128)(2,1)S(1)} fusion(bf16[1024,256]{1,0:T(8,128)(2,1)S(1)} %get-tuple-element.53, s32[1024]{0:T(1024)S(1)} %pad_clamp_fusion), kind=kCustom, calls=%fused_computation.1.clone | custom fusion | bytes 526336 | tf_op jit(solution)/shard_map/jit(_take)/gather | solution.py:162
  45.6 4.5 %collective-permute-start.4 = (bf16[1,128,256]{2,1,0:T(8,128)(2,1)S(1)}, bf16[1,128,256]{2,1,0:T(8,128)(2,1)S(1)}, u32[]{:S(2)}, u32[]{:S(2)}) collective-permute-start(bf16[1,128,256]{2,1,0:T(8,128)(2,1)S(1)} %get-tuple-element.41), channel_id=1, source_target_pairs={{0,16},{16,32},{32,48},{48,64},{64,80},{80,96},{96,112},{112,128},... | collective-permute-start | bytes 196616 | tf_op jit(solution)/shard_map/ppermute | solution.py:18
  50.1 2.0 %all-to-all-done = f32[4,64,899]{2,1,0:T(8,128)} async-done(((f32[4,64,899]{2,1,0:T(8,128)}), f32[4,64,899]{2,1,0:T(8,128)}, u32[]{:S(2)}, u32[]{:S(2)}) %all-to-all-start) | async-done | bytes 920608 | tf_op jit(solution)/shard_map/all_to_all | solution.py:56
  54.4 15.0 %all-to-all-start.1 = ((f32[64,1,899]{2,1,0:T(1,128)}), f32[64,1,899]{2,1,0:T(1,128)S(1)}, u32[]{:S(2)}, u32[]{:S(2)}) async-start(f32[64,1,899]{2,1,0:T(1,128)} %all_to_all.17), calls=%async_computation.1 | async-start | bytes 524288 | tf_op jit(solution)/shard_map/all_to_all | solution.py:63
  71.7 3.5 %collective-permute-start.12 = (bf16[1,128,256]{1,2,0:T(8,128)(2,1)}, bf16[1,128,256]{1,2,0:T(8,128)(2,1)S(1)}, u32[]{:S(2)}, u32[]{:S(2)}) collective-permute-start(bf16[1,128,256]{1,2,0:T(8,128)(2,1)} %get-tuple-element.33), channel_id=1, source_target_pairs={{0,16},{16,32},{32,48},{48,64},{64,80},{80,96},{96,112},{112,128},... | collective-permute-start | bytes 196616 | tf_op jit(solution)/shard_map/ppermute | solution.py:18
  75.2 1.9 %collective-permute-start.15 = (bf16[1,128,256]{1,2,0:T(8,128)(2,1)}, bf16[1,128,256]{1,2,0:T(8,128)(2,1)S(1)}, u32[]{:S(2)}, u32[]{:S(2)}) collective-permute-start(bf16[1,128,256]{1,2,0:T(8,128)(2,1)} %get-tuple-element.34), channel_id=1, source_target_pairs={{1,0},{2,1},{3,2},{4,3},{5,4},{6,5},{7,6},{8,7},{9,8},{10,9},{11,1... | collective-permute-start | bytes 196616 | tf_op jit(solution)/shard_map/ppermute | solution.py:19
  77.1 5.5 %collective-permute-start.14 = (bf16[1,128,256]{1,2,0:T(8,128)(2,1)}, bf16[1,128,256]{1,2,0:T(8,128)(2,1)}, u32[]{:S(2)}, u32[]{:S(2)}) collective-permute-start(bf16[1,128,256]{1,2,0:T(8,128)(2,1)} %get-tuple-element.35), channel_id=1, source_target_pairs={{0,1},{1,2},{2,3},{3,4},{4,5},{5,6},{6,7},{7,8},{8,9},{9,10},{10,1... | collective-permute-start | bytes 196616 | tf_op jit(solution)/shard_map/ppermute | solution.py:18
  82.6 1.9 %collective-permute-start.13 = (bf16[1,128,256]{1,2,0:T(8,128)(2,1)S(1)}, bf16[1,128,256]{1,2,0:T(8,128)(2,1)}, u32[]{:S(2)}, u32[]{:S(2)}) collective-permute-start(bf16[1,128,256]{1,2,0:T(8,128)(2,1)S(1)} %get-tuple-element.36), channel_id=1, source_target_pairs={{16,0},{32,16},{48,32},{64,48},{80,64},{96,80},{112,96},{128,112},... | collective-permute-start | bytes 196616 | tf_op jit(solution)/shard_map/ppermute | solution.py:19
  85.6 11.6 %all-to-all-start.2 = ((f32[64,1,899]{2,1,0:T(1,128)}), f32[64,1,899]{2,1,0:T(1,128)S(1)}, u32[]{:S(2)}, u32[]{:S(2)}) async-start(f32[64,1,899]{2,1,0:T(1,128)} %broadcast_in_dim.15), calls=%async_computation.2 | async-start | bytes 524288 | tf_op jit(solution)/shard_map/all_to_all | solution.py:31
  97.7 11.8 %all-to-all-done.2 = f32[64,1,899]{2,1,0:T(1,128)S(1)} async-done(((f32[64,1,899]{2,1,0:T(1,128)}), f32[64,1,899]{2,1,0:T(1,128)S(1)}, u32[]{:S(2)}, u32[]{:S(2)}) %all-to-all-start.2) | async-done | bytes 230176 | tf_op jit(solution)/shard_map/all_to_all | solution.py:31
  110.6 3.9 %all-to-all-start.3 = ((f32[4,64,899]{2,1,0:T(8,128)}), f32[4,64,899]{2,1,0:T(8,128)S(1)}, u32[]{:S(2)}, u32[]{:S(2)}) async-start(f32[4,64,899]{2,1,0:T(8,128)} %broadcast_in_dim.17), calls=%async_computation.3 | async-start | bytes 2097152 | tf_op jit(solution)/shard_map/all_to_all | solution.py:31
  114.6 5.0 %collective-permute-start.8 = (bf16[1,128,256]{1,2,0:T(8,128)(2,1)S(1)}, bf16[1,128,256]{1,2,0:T(8,128)(2,1)S(1)}, u32[]{:S(2)}, u32[]{:S(2)}) collective-permute-start(bf16[1,128,256]{1,2,0:T(8,128)(2,1)S(1)} %get-tuple-element.37), channel_id=1, source_target_pairs={{0,16},{16,32},{32,48},{48,64},{64,80},{80,96},{96,112},{112,128},... | collective-permute-start | bytes 196616 | tf_op jit(solution)/shard_map/ppermute | solution.py:18
  119.6 2.5 %collective-permute-start.11 = (bf16[1,128,256]{1,2,0:T(8,128)(2,1)S(1)}, bf16[1,128,256]{1,2,0:T(8,128)(2,1)S(1)}, u32[]{:S(2)}, u32[]{:S(2)}) collective-permute-start(bf16[1,128,256]{1,2,0:T(8,128)(2,1)S(1)} %get-tuple-element.38), channel_id=1, source_target_pairs={{1,0},{2,1},{3,2},{4,3},{5,4},{6,5},{7,6},{8,7},{9,8},{10,9},{11,1... | collective-permute-start | bytes 196616 | tf_op jit(solution)/shard_map/ppermute | solution.py:19
  122.1 4.9 %collective-permute-start.10 = (bf16[1,128,256]{1,2,0:T(8,128)(2,1)S(1)}, bf16[1,128,256]{1,2,0:T(8,128)(2,1)S(1)}, u32[]{:S(2)}, u32[]{:S(2)}) collective-permute-start(bf16[1,128,256]{1,2,0:T(8,128)(2,1)S(1)} %get-tuple-element.39), channel_id=1, source_target_pairs={{0,1},{1,2},{2,3},{3,4},{4,5},{5,6},{6,7},{7,8},{8,9},{9,10},{10,1... | collective-permute-start | bytes 196616 | tf_op jit(solution)/shard_map/ppermute | solution.py:18
  127.1 1.9 %collective-permute-start.9 = (bf16[1,128,256]{1,2,0:T(8,128)(2,1)S(1)}, bf16[1,128,256]{1,2,0:T(8,128)(2,1)S(1)}, u32[]{:S(2)}, u32[]{:S(2)}) collective-permute-start(bf16[1,128,256]{1,2,0:T(8,128)(2,1)S(1)} %get-tuple-element.40), channel_id=1, source_target_pairs={{16,0},{32,16},{48,32},{64,48},{80,64},{96,80},{112,96},{128,112},... | collective-permute-start | bytes 196616 | tf_op jit(solution)/shard_map/ppermute | solution.py:19
  130.8 1.9 %collective-permute-start.7 = (bf16[1,128,256]{2,1,0:T(8,128)(2,1)S(1)}, bf16[1,128,256]{2,1,0:T(8,128)(2,1)S(1)}, u32[]{:S(2)}, u32[]{:S(2)}) collective-permute-start(bf16[1,128,256]{2,1,0:T(8,128)(2,1)S(1)} %get-tuple-element.42), channel_id=1, source_target_pairs={{1,0},{2,1},{3,2},{4,3},{5,4},{6,5},{7,6},{8,7},{9,8},{10,9},{11,1... | collective-permute-start | bytes 196616 | tf_op jit(solution)/shard_map/ppermute | solution.py:19
  132.7 5.5 %collective-permute-start.6 = (bf16[1,128,256]{2,1,0:T(8,128)(2,1)S(1)}, bf16[1,128,256]{2,1,0:T(8,128)(2,1)S(1)}, u32[]{:S(2)}, u32[]{:S(2)}) collective-permute-start(bf16[1,128,256]{2,1,0:T(8,128)(2,1)S(1)} %get-tuple-element.43), channel_id=1, source_target_pairs={{0,1},{1,2},{2,3},{3,4},{4,5},{5,6},{6,7},{7,8},{8,9},{9,10},{10,1... | collective-permute-start | bytes 196616 | tf_op jit(solution)/shard_map/ppermute | solution.py:18
  138.2 1.9 %collective-permute-start.5 = (bf16[1,128,256]{2,1,0:T(8,128)(2,1)S(1)}, bf16[1,128,256]{2,1,0:T(8,128)(2,1)S(1)}, u32[]{:S(2)}, u32[]{:S(2)}) collective-permute-start(bf16[1,128,256]{2,1,0:T(8,128)(2,1)S(1)} %get-tuple-element.44), channel_id=1, source_target_pairs={{16,0},{32,16},{48,32},{64,48},{80,64},{96,80},{112,96},{128,112},... | collective-permute-start | bytes 196616 | tf_op jit(solution)/shard_map/ppermute | solution.py:19
  140.1 4.2 %collective-permute-start = (bf16[1,128,256]{2,1,0:T(8,128)(2,1)S(1)}, bf16[1,128,256]{2,1,0:T(8,128)(2,1)S(1)}, u32[]{:S(2)}, u32[]{:S(2)}) collective-permute-start(bf16[1,128,256]{2,1,0:T(8,128)(2,1)S(1)} %get-tuple-element.45), channel_id=1, source_target_pairs={{0,16},{16,32},{32,48},{48,64},{64,80},{80,96},{96,112},{112,128},... | collective-permute-start | bytes 196616 | tf_op jit(solution)/shard_map/ppermute | solution.py:18
  145.2 1.9 %collective-permute-start.3 = (bf16[1,128,256]{2,1,0:T(8,128)(2,1)S(1)}, bf16[1,128,256]{2,1,0:T(8,128)(2,1)S(1)}, u32[]{:S(2)}, u32[]{:S(2)}) collective-permute-start(bf16[1,128,256]{2,1,0:T(8,128)(2,1)S(1)} %get-tuple-element.46), channel_id=1, source_target_pairs={{1,0},{2,1},{3,2},{4,3},{5,4},{6,5},{7,6},{8,7},{9,8},{10,9},{11,1... | collective-permute-start | bytes 196616 | tf_op jit(solution)/shard_map/ppermute | solution.py:19
  147.2 5.5 %collective-permute-start.2 = (bf16[1,128,256]{2,1,0:T(8,128)(2,1)S(1)}, bf16[1,128,256]{2,1,0:T(8,128)(2,1)S(1)}, u32[]{:S(2)}, u32[]{:S(2)}) collective-permute-start(bf16[1,128,256]{2,1,0:T(8,128)(2,1)S(1)} %get-tuple-element.47), channel_id=1, source_target_pairs={{0,1},{1,2},{2,3},{3,4},{4,5},{5,6},{6,7},{7,8},{8,9},{9,10},{10,1... | collective-permute-start | bytes 196616 | tf_op jit(solution)/shard_map/ppermute | solution.py:18
  152.6 1.9 %collective-permute-start.1 = (bf16[1,128,256]{2,1,0:T(8,128)(2,1)S(1)}, bf16[1,128,256]{2,1,0:T(8,128)(2,1)S(1)}, u32[]{:S(2)}, u32[]{:S(2)}) collective-permute-start(bf16[1,128,256]{2,1,0:T(8,128)(2,1)S(1)} %get-tuple-element.48), channel_id=1, source_target_pairs={{16,0},{32,16},{48,32},{64,48},{80,64},{96,80},{112,96},{128,112},... | collective-permute-start | bytes 196616 | tf_op jit(solution)/shard_map/ppermute | solution.py:19
  155.3 2.9 %collective-permute-done.1 = bf16[1,128,256]{2,1,0:T(8,128)(2,1)S(1)} collective-permute-done((bf16[1,128,256]{2,1,0:T(8,128)(2,1)S(1)}, bf16[1,128,256]{2,1,0:T(8,128)(2,1)S(1)}, u32[]{:S(2)}, u32[]{:S(2)}) %collective-permute-start.1) | collective-permute-done | bytes 65568 | tf_op jit(solution)/shard_map/ppermute | solution.py:19
  159.7 1.7 %reshape_reshape.7 = f32[230144]{0:T(1024)} reshape(f32[64,4,899]{2,1,0:T(4,128)S(1)} %copy.44) | data formatting | bytes 1841152 | tf_op jit(solution)/shard_map/reshape;reshape | solution.py:39
  (96 shorter events, 32.3 us)
Async XLA Ops:
  0.6 8.5 %copy-start = (bf16[1,1,512,602]{2,3,1,0:T(8,128)(2,1)S(1)}, bf16[1,1,512,602]{2,3,1,0:T(8,128)(2,1)}, u32[]{:S(2)}) copy-start(bf16[1,1,512,602]{2,3,1,0:T(8,128)(2,1)} %param.20) | copy-start | bytes 1849348
  3.3 4.3 %copy-start.2 = (bf16[1,1,1024,602]{2,3,1,0:T(8,128)(2,1)S(1)}, bf16[1,1,1024,602]{2,3,1,0:T(8,128)(2,1)}, u32[]{:S(2)}) copy-start(bf16[1,1,1024,602]{2,3,1,0:T(8,128)(2,1)} %param.15) | copy-start | bytes 3698692
  7.6 9.1 %copy-start.1 = (bf16[1,1,1024,1024]{3,2,1,0:T(8,128)(2,1)}, bf16[1,1,1024,1024]{3,2,1,0:T(8,128)(2,1)S(1)}, u32[]{:S(2)}) copy-start(bf16[1,1,1024,1024]{3,2,1,0:T(8,128)(2,1)S(1)} %get-tuple-element.30) | copy-start | bytes 6291460
  9.2 1.0 copy-start.11
  10.2 1.6 copy-start.3
  14.1 1.0 copy-start.7
  15.0 1.0 copy-start.13
  16.8 1.9 %copy-start.14 = (bf16[1024,256]{1,0:T(8,128)(2,1)}, bf16[1024,256]{1,0:T(8,128)(2,1)S(1)}, u32[]{:S(2)}) copy-start(bf16[1024,256]{1,0:T(8,128)(2,1)S(1)} %fusion.42) | copy-start | bytes 1572868
  16.8 1.0 copy-start.10
  16.8 1.1 copy-start.12
  20.1 3.8 %copy-start.4 = (bf16[1024,256]{1,0:T(8,128)(2,1)}, bf16[1024,256]{1,0:T(8,128)(2,1)S(1)}, u32[]{:S(2)}) copy-start(bf16[1024,256]{1,0:T(8,128)(2,1)S(1)} %fusion.47) | copy-start | bytes 1572868
  37.2 15.0 %all-to-all-start = ((f32[4,64,899]{2,1,0:T(8,128)}), f32[4,64,899]{2,1,0:T(8,128)}, u32[]{:S(2)}, u32[]{:S(2)}) async-start(f32[4,64,899]{2,1,0:T(8,128)} %copy.43), calls=%async_computation | async-start | bytes 2097152 | tf_op jit(solution)/shard_map/all_to_all | solution.py:56
  45.6 99.7 %collective-permute-start.4 = (bf16[1,128,256]{2,1,0:T(8,128)(2,1)S(1)}, bf16[1,128,256]{2,1,0:T(8,128)(2,1)S(1)}, u32[]{:S(2)}, u32[]{:S(2)}) collective-permute-start(bf16[1,128,256]{2,1,0:T(8,128)(2,1)S(1)} %get-tuple-element.41), channel_id=1, source_target_pairs={{0,16},{16,32},{32,48},{48,64},{64,80},{80,96},{96,112},{112,128},... | collective-permute-start | bytes 196616 | tf_op jit(solution)/shard_map/ppermute | solution.py:18
  54.4 30.2 %all-to-all-start.1 = ((f32[64,1,899]{2,1,0:T(1,128)}), f32[64,1,899]{2,1,0:T(1,128)S(1)}, u32[]{:S(2)}, u32[]{:S(2)}) async-start(f32[64,1,899]{2,1,0:T(1,128)} %all_to_all.17), calls=%async_computation.1 | async-start | bytes 524288 | tf_op jit(solution)/shard_map/all_to_all | solution.py:63
  69.4 27.8 %copy-start.5 = (bf16[1024,256]{1,0:T(8,128)(2,1)S(1)}, bf16[1024,256]{1,0:T(8,128)(2,1)}, u32[]{:S(2)}) copy-start(bf16[1024,256]{1,0:T(8,128)(2,1)} %copy-done.4) | copy-start | bytes 1572868
  71.7 42.9 %collective-permute-start.12 = (bf16[1,128,256]{1,2,0:T(8,128)(2,1)}, bf16[1,128,256]{1,2,0:T(8,128)(2,1)S(1)}, u32[]{:S(2)}, u32[]{:S(2)}) collective-permute-start(bf16[1,128,256]{1,2,0:T(8,128)(2,1)} %get-tuple-element.33), channel_id=1, source_target_pairs={{0,16},{16,32},{32,48},{48,64},{64,80},{80,96},{96,112},{112,128},... | collective-permute-start | bytes 196616 | tf_op jit(solution)/shard_map/ppermute | solution.py:18
  75.2 44.4 %collective-permute-start.15 = (bf16[1,128,256]{1,2,0:T(8,128)(2,1)}, bf16[1,128,256]{1,2,0:T(8,128)(2,1)S(1)}, u32[]{:S(2)}, u32[]{:S(2)}) collective-permute-start(bf16[1,128,256]{1,2,0:T(8,128)(2,1)} %get-tuple-element.34), channel_id=1, source_target_pairs={{1,0},{2,1},{3,2},{4,3},{5,4},{6,5},{7,6},{8,7},{9,8},{10,9},{11,1... | collective-permute-start | bytes 196616 | tf_op jit(solution)/shard_map/ppermute | solution.py:19
  77.1 45.0 %collective-permute-start.14 = (bf16[1,128,256]{1,2,0:T(8,128)(2,1)}, bf16[1,128,256]{1,2,0:T(8,128)(2,1)}, u32[]{:S(2)}, u32[]{:S(2)}) collective-permute-start(bf16[1,128,256]{1,2,0:T(8,128)(2,1)} %get-tuple-element.35), channel_id=1, source_target_pairs={{0,1},{1,2},{2,3},{3,4},{4,5},{5,6},{6,7},{7,8},{8,9},{9,10},{10,1... | collective-permute-start | bytes 196616 | tf_op jit(solution)/shard_map/ppermute | solution.py:18
  82.6 44.5 %collective-permute-start.13 = (bf16[1,128,256]{1,2,0:T(8,128)(2,1)S(1)}, bf16[1,128,256]{1,2,0:T(8,128)(2,1)}, u32[]{:S(2)}, u32[]{:S(2)}) collective-permute-start(bf16[1,128,256]{1,2,0:T(8,128)(2,1)S(1)} %get-tuple-element.36), channel_id=1, source_target_pairs={{16,0},{32,16},{48,32},{64,48},{80,64},{96,80},{112,96},{128,112},... | collective-permute-start | bytes 196616 | tf_op jit(solution)/shard_map/ppermute | solution.py:19
  85.6 23.9 %all-to-all-start.2 = ((f32[64,1,899]{2,1,0:T(1,128)}), f32[64,1,899]{2,1,0:T(1,128)S(1)}, u32[]{:S(2)}, u32[]{:S(2)}) async-start(f32[64,1,899]{2,1,0:T(1,128)} %broadcast_in_dim.15), calls=%async_computation.2 | async-start | bytes 524288 | tf_op jit(solution)/shard_map/all_to_all | solution.py:31
  110.6 48.4 %all-to-all-start.3 = ((f32[4,64,899]{2,1,0:T(8,128)}), f32[4,64,899]{2,1,0:T(8,128)S(1)}, u32[]{:S(2)}, u32[]{:S(2)}) async-start(f32[4,64,899]{2,1,0:T(8,128)} %broadcast_in_dim.17), calls=%async_computation.3 | async-start | bytes 2097152 | tf_op jit(solution)/shard_map/all_to_all | solution.py:31
  114.6 16.2 %collective-permute-start.8 = (bf16[1,128,256]{1,2,0:T(8,128)(2,1)S(1)}, bf16[1,128,256]{1,2,0:T(8,128)(2,1)S(1)}, u32[]{:S(2)}, u32[]{:S(2)}) collective-permute-start(bf16[1,128,256]{1,2,0:T(8,128)(2,1)S(1)} %get-tuple-element.37), channel_id=1, source_target_pairs={{0,16},{16,32},{32,48},{48,64},{64,80},{80,96},{96,112},{112,128},... | collective-permute-start | bytes 196616 | tf_op jit(solution)/shard_map/ppermute | solution.py:18
  119.6 13.0 %collective-permute-start.11 = (bf16[1,128,256]{1,2,0:T(8,128)(2,1)S(1)}, bf16[1,128,256]{1,2,0:T(8,128)(2,1)S(1)}, u32[]{:S(2)}, u32[]{:S(2)}) collective-permute-start(bf16[1,128,256]{1,2,0:T(8,128)(2,1)S(1)} %get-tuple-element.38), channel_id=1, source_target_pairs={{1,0},{2,1},{3,2},{4,3},{5,4},{6,5},{7,6},{8,7},{9,8},{10,9},{11,1... | collective-permute-start | bytes 196616 | tf_op jit(solution)/shard_map/ppermute | solution.py:19
  122.1 16.0 %collective-permute-start.10 = (bf16[1,128,256]{1,2,0:T(8,128)(2,1)S(1)}, bf16[1,128,256]{1,2,0:T(8,128)(2,1)S(1)}, u32[]{:S(2)}, u32[]{:S(2)}) collective-permute-start(bf16[1,128,256]{1,2,0:T(8,128)(2,1)S(1)} %get-tuple-element.39), channel_id=1, source_target_pairs={{0,1},{1,2},{2,3},{3,4},{4,5},{5,6},{6,7},{7,8},{8,9},{9,10},{10,1... | collective-permute-start | bytes 196616 | tf_op jit(solution)/shard_map/ppermute | solution.py:18
  127.1 13.0 %collective-permute-start.9 = (bf16[1,128,256]{1,2,0:T(8,128)(2,1)S(1)}, bf16[1,128,256]{1,2,0:T(8,128)(2,1)S(1)}, u32[]{:S(2)}, u32[]{:S(2)}) collective-permute-start(bf16[1,128,256]{1,2,0:T(8,128)(2,1)S(1)} %get-tuple-element.40), channel_id=1, source_target_pairs={{16,0},{32,16},{48,32},{64,48},{80,64},{96,80},{112,96},{128,112},... | collective-permute-start | bytes 196616 | tf_op jit(solution)/shard_map/ppermute | solution.py:19
  130.8 16.4 %collective-permute-start.7 = (bf16[1,128,256]{2,1,0:T(8,128)(2,1)S(1)}, bf16[1,128,256]{2,1,0:T(8,128)(2,1)S(1)}, u32[]{:S(2)}, u32[]{:S(2)}) collective-permute-start(bf16[1,128,256]{2,1,0:T(8,128)(2,1)S(1)} %get-tuple-element.42), channel_id=1, source_target_pairs={{1,0},{2,1},{3,2},{4,3},{5,4},{6,5},{7,6},{8,7},{9,8},{10,9},{11,1... | collective-permute-start | bytes 196616 | tf_op jit(solution)/shard_map/ppermute | solution.py:19
  132.7 19.9 %collective-permute-start.6 = (bf16[1,128,256]{2,1,0:T(8,128)(2,1)S(1)}, bf16[1,128,256]{2,1,0:T(8,128)(2,1)S(1)}, u32[]{:S(2)}, u32[]{:S(2)}) collective-permute-start(bf16[1,128,256]{2,1,0:T(8,128)(2,1)S(1)} %get-tuple-element.43), channel_id=1, source_target_pairs={{0,1},{1,2},{2,3},{3,4},{4,5},{5,6},{6,7},{7,8},{8,9},{9,10},{10,1... | collective-permute-start | bytes 196616 | tf_op jit(solution)/shard_map/ppermute | solution.py:18
  138.2 16.4 %collective-permute-start.5 = (bf16[1,128,256]{2,1,0:T(8,128)(2,1)S(1)}, bf16[1,128,256]{2,1,0:T(8,128)(2,1)S(1)}, u32[]{:S(2)}, u32[]{:S(2)}) collective-permute-start(bf16[1,128,256]{2,1,0:T(8,128)(2,1)S(1)} %get-tuple-element.44), channel_id=1, source_target_pairs={{16,0},{32,16},{48,32},{64,48},{80,64},{96,80},{112,96},{128,112},... | collective-permute-start | bytes 196616 | tf_op jit(solution)/shard_map/ppermute | solution.py:19
  140.1 15.2 %collective-permute-start = (bf16[1,128,256]{2,1,0:T(8,128)(2,1)S(1)}, bf16[1,128,256]{2,1,0:T(8,128)(2,1)S(1)}, u32[]{:S(2)}, u32[]{:S(2)}) collective-permute-start(bf16[1,128,256]{2,1,0:T(8,128)(2,1)S(1)} %get-tuple-element.45), channel_id=1, source_target_pairs={{0,16},{16,32},{32,48},{48,64},{64,80},{80,96},{96,112},{112,128},... | collective-permute-start | bytes 196616 | tf_op jit(solution)/shard_map/ppermute | solution.py:18
  145.2 10.1 %collective-permute-start.3 = (bf16[1,128,256]{2,1,0:T(8,128)(2,1)S(1)}, bf16[1,128,256]{2,1,0:T(8,128)(2,1)S(1)}, u32[]{:S(2)}, u32[]{:S(2)}) collective-permute-start(bf16[1,128,256]{2,1,0:T(8,128)(2,1)S(1)} %get-tuple-element.46), channel_id=1, source_target_pairs={{1,0},{2,1},{3,2},{4,3},{5,4},{6,5},{7,6},{8,7},{9,8},{10,9},{11,1... | collective-permute-start | bytes 196616 | tf_op jit(solution)/shard_map/ppermute | solution.py:19
  147.2 8.2 %collective-permute-start.2 = (bf16[1,128,256]{2,1,0:T(8,128)(2,1)S(1)}, bf16[1,128,256]{2,1,0:T(8,128)(2,1)S(1)}, u32[]{:S(2)}, u32[]{:S(2)}) collective-permute-start(bf16[1,128,256]{2,1,0:T(8,128)(2,1)S(1)} %get-tuple-element.47), channel_id=1, source_target_pairs={{0,1},{1,2},{2,3},{3,4},{4,5},{5,6},{6,7},{7,8},{8,9},{9,10},{10,1... | collective-permute-start | bytes 196616 | tf_op jit(solution)/shard_map/ppermute | solution.py:18
  152.6 5.6 %collective-permute-start.1 = (bf16[1,128,256]{2,1,0:T(8,128)(2,1)S(1)}, bf16[1,128,256]{2,1,0:T(8,128)(2,1)S(1)}, u32[]{:S(2)}, u32[]{:S(2)}) collective-permute-start(bf16[1,128,256]{2,1,0:T(8,128)(2,1)S(1)} %get-tuple-element.48), channel_id=1, source_target_pairs={{16,0},{32,16},{48,32},{64,48},{80,64},{96,80},{112,96},{128,112},... | collective-permute-start | bytes 196616 | tf_op jit(solution)/shard_map/ppermute | solution.py:19
  (3 other events, 2.6 us)
where the time goes:
time: 167 us; the launch traced here: 166 us
  starting transfers between devices  89.3 us (53%)
  local copies, waits for them, and re-layouts  26 us (16%)
  matrix products  20.5 us (12%)
  waiting for transfers between devices  16.8 us (10%)
  other arithmetic  12 us (7%)
    ppermute x8, starting transfers between devices, padded(): before = lax.ppermute(last, axis, up)  38.6 us
    ppermute x8, starting transfers between devices, padded(): after = lax.ppermute(initial, axis, down)  15.9 us
    all_to_all x2, starting transfers between devices, copy_for_each(): lax.all_to_all(jnp.broadcast_to(shard[None], (size, *shard.shape)), axis,...  15.5 us
    all_to_all x1, starting transfers between devices, sum_in_two_steps(): return jnp.sum(lax.all_to_all(own, far, 0, 0, tiled=True), axis=0)  15 us
    all_to_all x2, waiting for transfers between devices, copy_for_each(): lax.all_to_all(jnp.broadcast_to(shard[None], (size, *shard.shape)), axis,...  11.8 us
    dot_general x2, matrix products, retract(): jnp.dot(local_bf.T, scaled, preferred_element_type=jnp.float32)  4.49 us
    reduce_sum x1, other arithmetic, per_device(): jnp.sum(local_mask, axis=1).astype(jnp.float32)  4.3 us
    all_to_all x1, starting transfers between devices, sum_at_owner(): pieces = lax.all_to_all(cut_along(shard, dim, size), axis, 0, 0, tiled=True)  4.24 us
  transfers between devices with their start and end apart: 20, of which 3 were waited for; matrix products, arithmetic and copies ran while one was open for 9% of the time, Pallas kernels for 0%

commit v1 on v0

v1 whole, which is shorter than its diff:
```python
import jax
import jax.numpy as jnp
from jax import lax
from jax.sharding import Mesh
from jax.sharding import PartitionSpec as P

ROW = ("row_0", "row_1")
COL = ("col_0", "col_1")


def slope(pre):
    sigma = jax.nn.sigmoid(pre)
    return sigma * (1.0 + pre * (1.0 - sigma))


def spread(local_bf, halo_bf, inverse, values, remote):
    summed = jnp.dot(local_bf, values, preferred_element_type=jnp.float32)
    summed = summed + values.astype(jnp.float32)
    summed = summed + jnp.dot(halo_bf, remote, preferred_element_type=jnp.float32)
    return (summed * inverse).astype(jnp.bfloat16)


def retract(local_bf, halo_bf, inverse, upstream, weight, hits, returned):
    across = jnp.dot(upstream, weight.T, preferred_element_type=jnp.float32)
    scaled = (across * inverse).astype(jnp.bfloat16)
    carried = jnp.dot(local_bf.T, scaled, preferred_element_type=jnp.float32) + scaled.astype(
        jnp.float32
    )
    carried = carried + jnp.dot(hits, returned, preferred_element_type=jnp.float32)
    outgoing = jnp.dot(halo_bf.T, scaled, preferred_element_type=jnp.float32).astype(jnp.bfloat16)
    return (carried, outgoing)


GROUP = ("row_1", "col_0", "col_1")
FAR = ("row_0",)
ROWS = 1024


def shares(axes):
    size = 1
    for axis in axes:
        size *= lax.axis_size(axis)
    return size


def copies(piece, axes):
    size = shares(axes)
    return lax.all_to_all(jnp.broadcast_to(piece[None], (size, *piece.shape)), axes, 0, 0, tiled=True)


def summed(pieces):
    return jnp.sum(pieces.astype(jnp.float32), axis=0).astype(jnp.bfloat16)


def total_of(packed):
    size = shares(GROUP)
    pieces = packed.reshape(size, packed.shape[0] // size, packed.shape[1])
    own = summed(lax.all_to_all(pieces, GROUP, 0, 0, tiled=True))
    own = summed(copies(own, FAR))
    return copies(own, GROUP).reshape(packed.shape)


def shifted(block, axis, step):
    size = lax.axis_size(axis)
    pairs = [(i, i + step) for i in range(size) if 0 <= i + step < size]
    return lax.ppermute(block, axis, pairs)


def traded(arrays):
    blocks = jnp.stack([a.reshape(4, a.shape[0] // 4, a.shape[1]) for a in arrays], axis=1)
    got = [
        shifted(blocks[1], ROW, 1),
        shifted(blocks[0], ROW, -1),
        shifted(blocks[3], COL, 1),
        shifted(blocks[2], COL, -1),
    ]
    return [jnp.concatenate([g[n] for g in got], axis=0)[None, None] for n in range(len(arrays))]


def per_device(
    features,
    local_mask,
    halo_mask,
    boundary_index,
    labels,
    halo_first,
    halo_second,
    halo_third,
    return_second,
    return_third,
    weight_first,
    weight_second,
    weight_third,
):
    features = features[0, 0]
    local_mask = local_mask[0, 0]
    halo_mask = halo_mask[0, 0]
    boundary_index = boundary_index[0, 0]
    labels = labels[0, 0]
    local_bf = local_mask.astype(jnp.bfloat16)
    halo_bf = halo_mask.astype(jnp.bfloat16)
    degree = (
        1.0
        + jnp.sum(local_mask, axis=1).astype(jnp.float32)
        + jnp.sum(halo_mask, axis=1).astype(jnp.float32)
    )
    inverse = (1.0 / degree)[:, None]
    node_rows = features.shape[0]
    hits = (jnp.arange(node_rows, dtype=jnp.int32)[:, None] == boundary_index[None, :]).astype(
        jnp.bfloat16
    )
    mixed_one = spread(local_bf, halo_bf, inverse, features, halo_first[0, 0])
    pre_one = jnp.dot(mixed_one, weight_first, preferred_element_type=jnp.float32)
    hidden_one = jax.nn.silu(pre_one).astype(jnp.bfloat16)
    mixed_two = spread(local_bf, halo_bf, inverse, hidden_one, halo_second[0, 0])
    pre_two = jnp.dot(mixed_two, weight_second, preferred_element_type=jnp.float32)
    hidden_two = jax.nn.silu(pre_two).astype(jnp.bfloat16)
    mixed_three = spread(local_bf, halo_bf, inverse, hidden_two, halo_third[0, 0])
    logits = jnp.dot(mixed_three, weight_third, preferred_element_type=jnp.float32)
    expo = jnp.exp(logits)
    probs = expo / jnp.sum(expo, axis=1, keepdims=True)
    target = (labels[:, None] == jnp.arange(logits.shape[1], dtype=jnp.int32)[None, :]).astype(
        jnp.float32
    )
    upstream_three = ((probs - target) / node_rows).astype(jnp.bfloat16)
    grad_three = jnp.dot(upstream_three.T, mixed_three, preferred_element_type=jnp.float32)
    carried_two, outgoing_three = retract(
        local_bf, halo_bf, inverse, upstream_three, weight_third, hits, return_third[0, 0]
    )
    upstream_two = (carried_two * slope(pre_two)).astype(jnp.bfloat16)
    grad_two = jnp.dot(mixed_two.T, upstream_two, preferred_element_type=jnp.float32)
    carried_one, outgoing_two = retract(
        local_bf, halo_bf, inverse, upstream_two, weight_second, hits, return_second[0, 0]
    )
    upstream_one = (carried_one * slope(pre_one)).astype(jnp.bfloat16)
    grad_one = jnp.dot(mixed_one.T, upstream_one, preferred_element_type=jnp.float32)
    hidden = jnp.concatenate([hidden_one, hidden_two], axis=1)
    sent = jnp.dot(hits.T, hidden, preferred_element_type=jnp.float32).astype(jnp.bfloat16)
    width = hidden_one.shape[1]
    next_second, next_third, back_second, back_third = traded(
        (sent[:, :width], sent[:, width:], outgoing_two, outgoing_three)
    )
    one, two, three = grad_one.shape[0], grad_two.shape[0], grad_three.shape[0]
    third_at = two + one + (-one) % 8
    packed = jnp.concatenate(
        [
            grad_two.astype(jnp.bfloat16),
            jnp.pad(grad_one.astype(jnp.bfloat16), [(0, (-one) % 8), (0, 0)]),
            jnp.pad(grad_three.astype(jnp.bfloat16), [(0, ROWS - third_at - three), (0, 0)]),
        ],
        axis=0,
    )
    total = total_of(packed).astype(jnp.float32)
    grad_two = total[:two]
    grad_one = total[two : two + one]
    grad_three = total[third_at : third_at + three].T
    return (grad_one, grad_two, grad_three, next_second, next_third, back_second, back_third)


def solution(mesh):
    torus = Mesh(mesh.devices.reshape(8, 2, 4, 4), ("row_0", "row_1", "col_0", "col_1"))
    in_specs = (
        P(ROW, COL, None, None),
        P(ROW, COL, None, None),
        P(ROW, COL, None, None),
        P(ROW, COL, None),
        P(ROW, COL, None),
        P(ROW, COL, None, None),
        P(ROW, COL, None, None),
        P(ROW, COL, None, None),
        P(ROW, COL, None, None),
        P(ROW, COL, None, None),
        P(),
        P(),
        P(),
    )
    out_specs = (
        P(),
        P(),
        P(),
        P(ROW, COL, None, None),
        P(ROW, COL, None, None),
        P(ROW, COL, None, None),
        P(ROW, COL, None, None),
    )
    return jax.shard_map(
        per_device, mesh=torus, in_specs=in_specs, out_specs=out_specs, check_vma=False
    )
```

time: 167 us -> 94.5 us (0.57)
  the two profiles are of different devices: /device:TPU:25 before, /device:TPU:1 now
where the time goes in v1:
time: 94.5 us; the launch traced here: 93.8 us
  starting transfers between devices  39.4 us (42%)
  matrix products  18.9 us (20%)
  waiting for transfers between devices  17.1 us (18%)
  other arithmetic  10.8 us (11%)
  local copies, waits for them, and re-layouts  6.51 us (7%)
  between operations  1.08 us (1%)
    all_to_all x2, starting transfers between devices, copies(): lax.all_to_all(jnp.broadcast_to(piece[None], (size, *piece.shape)), axes,...  19.8 us
    all_to_all x2, waiting for transfers between devices, copies(): lax.all_to_all(jnp.broadcast_to(piece[None], (size, *piece.shape)), axes,...  17.1 us
    ppermute x4, starting transfers between devices, shifted(): return lax.ppermute(block, axis, pairs)  11 us
    all_to_all x1, starting transfers between devices, total_of(): own = summed(lax.all_to_all(pieces, GROUP, 0, 0, tiled=True))  8.6 us
    reduce_sum x1, other arithmetic, per_device(): jnp.sum(local_mask, axis=1).astype(jnp.float32)  4.3 us
    dot_general x1, matrix products, per_device(): jnp.dot(mixed_one.T, upstream_one, preferred_element_type=jnp.float32)  3.62 us
    dot_general x3, matrix products, spread(): summed = jnp.dot(local_bf, values, preferred_element_type=jnp.float32)  2.97 us
    convert_element_type x1, other arithmetic, per_device(): halo_bf = halo_mask.astype(jnp.bfloat16)  2.68 us
  transfers between devices with their start and end apart: 7, of which 2 were waited for; matrix products, arithmetic and copies ran while one was open for 7% of the time, Pallas kernels for 0%

profile of v1, /device:TPU:1, one launch (start us, length us, event | category | flops | bytes accessed | tf_op | source)
XLA Modules:
  0.0 93.8 jit_solution(1294976273671487181)
XLA Ops:
  0.6 2.7 %fusion.86 = (bf16[1,1,1024,512]{3,2,1,0:T(8,128)(2,1)S(1)}, s32[1024]{0:T(1024)S(1)}) fusion(s32[1,1,1024,512]{3,2,1,0:T(8,128)} %param.15), kind=kLoop, calls=%fused_computation.115 | loop fusion | flops 1047552 | bytes 3149824 | tf_op jit(solution)/shard_map/convert_element_type | solution.py:101
  3.3 4.3 %fusion.85 = (s32[1024]{0:T(1024)S(1)}, bf16[1,1,1024,1024]{3,2,1,0:T(8,128)(2,1)S(1)}) fusion(s32[1,1,1024,1024]{3,2,1,0:T(8,128)} %param.14), kind=kLoop, calls=%fused_computation.114 | loop fusion | flops 2096128 | bytes 6295552 | tf_op jit(solution)/shard_map/reduce_sum | solution.py:104
  7.7 1.5 %fusion.8 = f32[1024,602]{0,1:T(8,128)S(1)} fusion(bf16[1,1,1024,1024]{3,2,1,0:T(8,128)(2,1)S(1)} %get-tuple-element.8, bf16[1,1,1024,602]{2,3,1,0:T(8,128)(2,1)S(1)} %copy-done.1), kind=kOutput, calls=%fused_computation.9 | convolution fusion | flops 1262485504 | bytes 5795840 | tf_op jit(solution)/shard_map/dot_general | solution.py:17
  9.2 0.9 multiply_convert_fusion
  10.1 1.7 %multiply_convert_fusion.2 = (bf16[1024,256]{0,1:T(8,128)(2,1)S(1)}, f32[1024,256]{0,1:T(8,128)}) fusion(bf16[1024,602]{0,1:T(8,128)(2,1)S(1)} %multiply_convert_fusion, bf16[602,256]{1,0:T(8,128)(2,1)S(1)} %copy-done.8), kind=kOutput, calls=%fused_computation.71 | convolution fusion | flops 316932096 | bytes 3113984 | tf_op jit(solution)/shard_map/dot_general | solution.py:113
  11.8 0.8 copy-done.12
  12.6 0.7 fusion.40
  13.4 0.5 fusion.44
  14.8 0.7 fusion.37
  17.6 0.7 fusion.34
  18.7 0.8 fusion.47
  19.5 1.0 %convolution_convert_fusion.3 = bf16[256,256]{1,0:T(8,128)(2,1)} fusion(bf16[1024,256]{0,1:T(8,128)(2,1)S(1)} %fusion.44, bf16[1024,256]{0,1:T(8,128)(2,1)S(1)} %fusion.47), kind=kOutput, calls=%fused_computation.49 | convolution fusion | flops 134283264 | bytes 1179648 | tf_op jit(solution)/shard_map/dot_general | solution.py:131
  20.9 1.7 %fusion.31 = f32[1024,256]{0,1:T(8,128)} fusion(bf16[1024,256]{0,1:T(8,128)(2,1)S(1)} %fusion.48, bf16[1,1,1024,1024]{3,2,1,0:T(8,128)(2,1)S(1)} %get-tuple-element.8), kind=kOutput, calls=%fused_computation.31 | convolution fusion | flops 537395200 | bytes 3670016 | tf_op jit(solution)/shard_map/dot_general | solution.py:26
  22.5 3.6 %fusion.51 = bf16[602,256]{1,0:T(8,128)(2,1)} fusion(bf16[1024,602]{0,1:T(8,128)(2,1)S(1)} %multiply_convert_fusion, f32[1024,256]{0,1:T(8,128)} %fusion.31, f32[1024,256]{0,1:T(8,128)} %get-tuple-element.34, s32[512]{0:T(512)S(1)} %bitcast.170, bf16[1,1,512,256]{3,2,1,0:T(8,128)(2,1)} %param.21), kind=kOutput, calls=%fused_computation.44 | convolution fusion | flops 587356672 | bytes 3902464 | tf_op jit(solution)/shard_map/dot_general | solution.py:136
  26.2 1.8 %fusion.76 = bf16[1024,256]{1,0:T(8,128)(2,1)} fusion(bf16[41,256]{1,0:T(8,128)(2,1)S(1)} %convolution_convert_fusion.4, bf16[602,256]{1,0:T(8,128)(2,1)} %fusion.51, bf16[256,256]{1,0:T(8,128)(2,1)} %convolution_convert_fusion.3), kind=kLoop, calls=%fused_computation.78 | loop fusion | flops 3145728 | bytes 984576 | tf_op jit(solution)/shard_map/concatenate | solution.py:145
  28.0 8.6 %all-to-all-start = ((bf16[32,32,256]{2,1,0:T(8,128)(2,1)}), bf16[32,32,256]{2,1,0:T(8,128)(2,1)S(1)}, u32[]{:S(2)}, u32[]{:S(2)}) async-start(bf16[32,32,256]{2,1,0:T(8,128)(2,1)} %bitcast.14), calls=%async_computation | async-start | bytes 1048576 | tf_op jit(solution)/shard_map/all_to_all | solution.py:58
  36.6 2.0 %convolution_convert_fusion = bf16[512,512]{1,0:T(8,128)(2,1)S(1)} fusion(bf16[1024,256]{0,1:T(8,128)(2,1)} %copy-done.13, bf16[1024,256]{0,1:T(8,128)(2,1)} %copy-done.12, s32[512]{0:T(512)S(1)} %bitcast.171), kind=kOutput, calls=%fused_computation.41 | convolution fusion | flops 540278784 | bytes 1574912 | tf_op jit(solution)/shard_map/dot_general | solution.py:138
  40.1 3.8 %collective-permute-start = (bf16[4,128,256]{2,1,0:T(8,128)(2,1)S(1)}, bf16[4,128,256]{2,1,0:T(8,128)(2,1)S(1)}, u32[]{:S(2)}, u32[]{:S(2)}) collective-permute-start(bf16[4,128,256]{2,1,0:T(8,128)(2,1)S(1)} %get-tuple-element.11), channel_id=1, source_target_pairs={{0,16},{16,32},{32,48},{48,64},{64,80},{80,96},{96,112},{112,128},... | collective-permute-start | bytes 786440 | tf_op jit(solution)/shard_map/ppermute | solution.py:66
  43.9 1.3 %collective-permute-start.3 = (bf16[4,128,256]{2,1,0:T(8,128)(2,1)S(1)}, bf16[4,128,256]{2,1,0:T(8,128)(2,1)S(1)}, u32[]{:S(2)}, u32[]{:S(2)}) collective-permute-start(bf16[4,128,256]{2,1,0:T(8,128)(2,1)S(1)} %get-tuple-element.12), channel_id=1, source_target_pairs={{1,0},{2,1},{3,2},{4,3},{5,4},{6,5},{7,6},{8,7},{9,8},{10,9},{11,1... | collective-permute-start | bytes 786440 | tf_op jit(solution)/shard_map/ppermute | solution.py:66
  45.2 4.0 %collective-permute-start.2 = (bf16[4,128,256]{2,1,0:T(8,128)(2,1)S(1)}, bf16[4,128,256]{2,1,0:T(8,128)(2,1)S(1)}, u32[]{:S(2)}, u32[]{:S(2)}) collective-permute-start(bf16[4,128,256]{2,1,0:T(8,128)(2,1)S(1)} %get-tuple-element.13), channel_id=1, source_target_pairs={{0,1},{1,2},{2,3},{3,4},{4,5},{5,6},{6,7},{7,8},{8,9},{9,10},{10,1... | collective-permute-start | bytes 786440 | tf_op jit(solution)/shard_map/ppermute | solution.py:66
  49.2 1.9 %collective-permute-start.1 = (bf16[4,128,256]{2,1,0:T(8,128)(2,1)S(1)}, bf16[4,128,256]{2,1,0:T(8,128)(2,1)S(1)}, u32[]{:S(2)}, u32[]{:S(2)}) collective-permute-start(bf16[4,128,256]{2,1,0:T(8,128)(2,1)S(1)} %get-tuple-element.14), channel_id=1, source_target_pairs={{16,0},{32,16},{48,32},{64,48},{80,64},{96,80},{112,96},{128,112},... | collective-permute-start | bytes 786440 | tf_op jit(solution)/shard_map/ppermute | solution.py:66
  51.3 0.7 broadcast_in_dim.12
  52.0 7.3 %all-to-all-start.1 = ((bf16[8,32,256]{2,1,0:T(8,128)(2,1)}), bf16[8,32,256]{2,1,0:T(8,128)(2,1)S(1)}, u32[]{:S(2)}, u32[]{:S(2)}) async-start(bf16[8,32,256]{2,1,0:T(8,128)(2,1)} %broadcast_in_dim.12), calls=%async_computation.1 | async-start | bytes 262144 | tf_op jit(solution)/shard_map/all_to_all | solution.py:48
  59.3 7.9 %all-to-all-done.1 = bf16[8,32,256]{2,1,0:T(8,128)(2,1)S(1)} async-done(((bf16[8,32,256]{2,1,0:T(8,128)(2,1)}), bf16[8,32,256]{2,1,0:T(8,128)(2,1)S(1)}, u32[]{:S(2)}, u32[]{:S(2)}) %all-to-all-start.1) | async-done | bytes 131104 | tf_op jit(solution)/shard_map/all_to_all | solution.py:48
  67.3 0.9 broadcast_in_dim.13
  68.1 12.5 %all-to-all-start.2 = ((bf16[32,32,256]{2,1,0:T(8,128)(2,1)}), bf16[32,32,256]{2,1,0:T(8,128)(2,1)S(1)}, u32[]{:S(2)}, u32[]{:S(2)}) async-start(bf16[32,32,256]{2,1,0:T(8,128)(2,1)} %broadcast_in_dim.13), calls=%async_computation.2 | async-start | bytes 1048576 | tf_op jit(solution)/shard_map/all_to_all | solution.py:48
  80.7 0.8 maximum_bitcast_fusion.2
  81.5 0.8 maximum_bitcast_fusion
  82.3 9.2 %all-to-all-done.2 = bf16[32,32,256]{2,1,0:T(8,128)(2,1)S(1)} async-done(((bf16[32,32,256]{2,1,0:T(8,128)(2,1)}), bf16[32,32,256]{2,1,0:T(8,128)(2,1)S(1)}, u32[]{:S(2)}, u32[]{:S(2)}) %all-to-all-start.2) | async-done | bytes 524320 | tf_op jit(solution)/shard_map/all_to_all | solution.py:48
  91.6 0.6 slice_bitcast_fusion.20
  92.2 0.9 slice.104
  93.1 0.7 slice.105
  (53 shorter events, 5.3 us)
Async XLA Ops:
  0.6 8.5 %copy-start = (bf16[1,1,512,602]{2,3,1,0:T(8,128)(2,1)S(1)}, bf16[1,1,512,602]{2,3,1,0:T(8,128)(2,1)}, u32[]{:S(2)}) copy-start(bf16[1,1,512,602]{2,3,1,0:T(8,128)(2,1)} %param.18) | copy-start | bytes 1849348
  3.3 4.3 %copy-start.1 = (bf16[1,1,1024,602]{2,3,1,0:T(8,128)(2,1)S(1)}, bf16[1,1,1024,602]{2,3,1,0:T(8,128)(2,1)}, u32[]{:S(2)}) copy-start(bf16[1,1,1024,602]{2,3,1,0:T(8,128)(2,1)} %param.13) | copy-start | bytes 3698692
  9.2 1.0 %copy-start.8 = (bf16[602,256]{1,0:T(8,128)(2,1)S(1)}, bf16[602,256]{1,0:T(8,128)(2,1)}, u32[]{:S(2)}) copy-start(bf16[602,256]{1,0:T(8,128)(2,1)} %param.23) | copy-start | bytes 924676
  11.8 0.8 copy-start.12
  11.8 1.5 %copy-start.4 = (bf16[1,1,512,256]{3,2,1,0:T(8,128)(2,1)S(1)}, bf16[1,1,512,256]{3,2,1,0:T(8,128)(2,1)}, u32[]{:S(2)}) copy-start(bf16[1,1,512,256]{3,2,1,0:T(8,128)(2,1)} %param.19) | copy-start | bytes 786436
  13.4 0.9 copy-start.6
  14.8 1.7 %copy-start.13 = (bf16[1024,256]{0,1:T(8,128)(2,1)}, bf16[1024,256]{0,1:T(8,128)(2,1)S(1)}, u32[]{:S(2)}) copy-start(bf16[1024,256]{0,1:T(8,128)(2,1)S(1)} %get-tuple-element.35) | copy-start | bytes 1572868
  14.8 1.1 %copy-start.5 = (bf16[1,1,512,256]{3,2,1,0:T(8,128)(2,1)S(1)}, bf16[1,1,512,256]{3,2,1,0:T(8,128)(2,1)}, u32[]{:S(2)}) copy-start(bf16[1,1,512,256]{3,2,1,0:T(8,128)(2,1)} %param.20) | copy-start | bytes 786436
  15.9 0.7 copy-start.7
  15.9 1.0 %copy-start.10 = (s32[1,1,1024]{2,1,0:T(1,128)S(1)}, s32[1,1,1024]{2,1,0:T(1,128)}, u32[]{:S(2)}) copy-start(s32[1,1,1024]{2,1,0:T(1,128)} %param.17) | copy-start | bytes 12292
  17.5 2.0 %copy-start.2 = (bf16[1024,256]{0,1:T(8,128)(2,1)}, bf16[1024,256]{0,1:T(8,128)(2,1)S(1)}, u32[]{:S(2)}) copy-start(bf16[1024,256]{0,1:T(8,128)(2,1)S(1)} %fusion.43) | copy-start | bytes 1572868
  17.5 1.1 %copy-start.9 = (bf16[1,1,512,256]{3,2,1,0:T(8,128)(2,1)S(1)}, bf16[1,1,512,256]{3,2,1,0:T(8,128)(2,1)}, u32[]{:S(2)}) copy-start(bf16[1,1,512,256]{3,2,1,0:T(8,128)(2,1)} %param.22) | copy-start | bytes 786436
  17.5 1.1 %copy-start.11 = (s32[1,1,512]{2,1,0:T(1,128)S(1)}, s32[1,1,512]{2,1,0:T(1,128)}, u32[]{:S(2)}) copy-start(s32[1,1,512]{2,1,0:T(1,128)} %param.16) | copy-start | bytes 6148
  28.0 23.2 %all-to-all-start = ((bf16[32,32,256]{2,1,0:T(8,128)(2,1)}), bf16[32,32,256]{2,1,0:T(8,128)(2,1)S(1)}, u32[]{:S(2)}, u32[]{:S(2)}) async-start(bf16[32,32,256]{2,1,0:T(8,128)(2,1)} %bitcast.14), calls=%async_computation | async-start | bytes 1048576 | tf_op jit(solution)/shard_map/all_to_all | solution.py:58
  36.6 2.0 %copy-start.3 = (bf16[1024,256]{0,1:T(8,128)(2,1)S(1)}, bf16[1024,256]{0,1:T(8,128)(2,1)}, u32[]{:S(2)}) copy-start(bf16[1024,256]{0,1:T(8,128)(2,1)} %copy-done.2) | copy-start | bytes 1572868
  40.1 11.1 %collective-permute-start = (bf16[4,128,256]{2,1,0:T(8,128)(2,1)S(1)}, bf16[4,128,256]{2,1,0:T(8,128)(2,1)S(1)}, u32[]{:S(2)}, u32[]{:S(2)}) collective-permute-start(bf16[4,128,256]{2,1,0:T(8,128)(2,1)S(1)} %get-tuple-element.11), channel_id=1, source_target_pairs={{0,16},{16,32},{32,48},{48,64},{64,80},{80,96},{96,112},{112,128},... | collective-permute-start | bytes 786440 | tf_op jit(solution)/shard_map/ppermute | solution.py:66
  43.9 15.4 %collective-permute-start.3 = (bf16[4,128,256]{2,1,0:T(8,128)(2,1)S(1)}, bf16[4,128,256]{2,1,0:T(8,128)(2,1)S(1)}, u32[]{:S(2)}, u32[]{:S(2)}) collective-permute-start(bf16[4,128,256]{2,1,0:T(8,128)(2,1)S(1)} %get-tuple-element.12), channel_id=1, source_target_pairs={{1,0},{2,1},{3,2},{4,3},{5,4},{6,5},{7,6},{8,7},{9,8},{10,9},{11,1... | collective-permute-start | bytes 786440 | tf_op jit(solution)/shard_map/ppermute | solution.py:66
  45.2 35.4 %collective-permute-start.2 = (bf16[4,128,256]{2,1,0:T(8,128)(2,1)S(1)}, bf16[4,128,256]{2,1,0:T(8,128)(2,1)S(1)}, u32[]{:S(2)}, u32[]{:S(2)}) collective-permute-start(bf16[4,128,256]{2,1,0:T(8,128)(2,1)S(1)} %get-tuple-element.13), channel_id=1, source_target_pairs={{0,1},{1,2},{2,3},{3,4},{4,5},{5,6},{6,7},{7,8},{8,9},{9,10},{10,1... | collective-permute-start | bytes 786440 | tf_op jit(solution)/shard_map/ppermute | solution.py:66
  49.2 31.4 %collective-permute-start.1 = (bf16[4,128,256]{2,1,0:T(8,128)(2,1)S(1)}, bf16[4,128,256]{2,1,0:T(8,128)(2,1)S(1)}, u32[]{:S(2)}, u32[]{:S(2)}) collective-permute-start(bf16[4,128,256]{2,1,0:T(8,128)(2,1)S(1)} %get-tuple-element.14), channel_id=1, source_target_pairs={{16,0},{32,16},{48,32},{64,48},{80,64},{96,80},{112,96},{128,112},... | collective-permute-start | bytes 786440 | tf_op jit(solution)/shard_map/ppermute | solution.py:66
  52.0 15.3 %all-to-all-start.1 = ((bf16[8,32,256]{2,1,0:T(8,128)(2,1)}), bf16[8,32,256]{2,1,0:T(8,128)(2,1)S(1)}, u32[]{:S(2)}, u32[]{:S(2)}) async-start(bf16[8,32,256]{2,1,0:T(8,128)(2,1)} %broadcast_in_dim.12), calls=%async_computation.1 | async-start | bytes 262144 | tf_op jit(solution)/shard_map/all_to_all | solution.py:48
  68.1 23.4 %all-to-all-start.2 = ((bf16[32,32,256]{2,1,0:T(8,128)(2,1)}), bf16[32,32,256]{2,1,0:T(8,128)(2,1)S(1)}, u32[]{:S(2)}, u32[]{:S(2)}) async-start(bf16[32,32,256]{2,1,0:T(8,128)(2,1)} %broadcast_in_dim.13), calls=%async_computation.2 | async-start | bytes 1048576 | tf_op jit(solution)/shard_map/all_to_all | solution.py:48

commit v2 on v1

v2 whole, which is shorter than its diff:
```python
import jax
import jax.numpy as jnp
from jax import lax
from jax.experimental import pallas as pl
from jax.experimental.pallas import tpu as pltpu
from jax.sharding import Mesh
from jax.sharding import PartitionSpec as P

ROW = ("row_0", "row_1")
COL = ("col_0", "col_1")


def dot(a, b, contract=(1, 0)):
    dims = (((contract[0],), (contract[1],)), ((), ()))
    return lax.dot_general(a, b, dims, preferred_element_type=jnp.float32)


def silu_of(pre):
    return pre / (1.0 + jnp.exp(-pre))


def slope(pre):
    sigma = 1.0 / (1.0 + jnp.exp(-pre))
    return sigma * (1.0 + pre * (1.0 - sigma))


BF = jnp.bfloat16
F32 = jnp.float32
CHUNKS = 4
ROWS = 1024


def step_kernel(
    index_ref, label_ref, features, local_mask, halo_mask, halo_first, halo_second, halo_third,
    return_second, return_third, weight_first, weight_second, weight_third,
    packed_out, above_out, below_out, left_out, right_out,
    feat, local_raw, halo_raw, first, second, third, ret_two, ret_three, w_one, w_two, w_three,
    local, halo, hits, inverse, mixed_one, mixed_two, mixed_three, pre_one, pre_two,
    hidden_one, hidden_two, scaled, packed, sends, in_sem, local_sem, halo_sem, out_sem,
):
    nodes = feat.shape[0]
    rows = nodes // CHUNKS
    bound = hits.shape[1] // 4

    def fetch(source, target, sem):
        copy = pltpu.make_async_copy(source, target, sem)
        copy.start()
        return copy

    def part(ref, c):
        return ref.at[pl.ds(c * rows, rows)]

    got_feat = fetch(features, feat, in_sem.at[0])
    got_first = fetch(halo_first, first, in_sem.at[1])
    got_local, got_halo = [], []
    for c in range(CHUNKS):
        got_local.append(fetch(part(local_mask, c), part(local_raw, c), local_sem.at[c]))
        got_halo.append(fetch(part(halo_mask, c), part(halo_raw, c), halo_sem.at[c]))
    rest = [
        fetch(source, target, in_sem.at[2 + n])
        for n, (source, target) in enumerate(
            (
                (weight_first, w_one), (weight_second, w_two), (halo_second, second),
                (weight_third, w_three), (halo_third, third),
                (return_third, ret_three), (return_second, ret_two),
            )
        )
    ]
    got_w_one, got_w_two, got_second, got_w_three, got_third, got_ret_three, got_ret_two = rest

    hits[...] = (
        lax.broadcasted_iota(jnp.int32, hits.shape, 0) == index_ref[...]
    ).astype(F32).astype(BF)

    got_feat.wait()
    got_first.wait()
    for c in range(CHUNKS):
        at = pl.ds(c * rows, rows)
        got_local[c].wait()
        got_halo[c].wait()
        raw_local = local_raw[at, :].astype(F32)
        raw_halo = halo_raw[at, :].astype(F32)
        local[at, :] = raw_local.astype(BF)
        halo[at, :] = raw_halo.astype(BF)
        degree = (
            1.0 + jnp.sum(raw_local, axis=1, keepdims=True) + jnp.sum(raw_halo, axis=1, keepdims=True)
        )
        inverse[at, :] = 1.0 / degree
        summed = dot(local[at, :], feat[...]) + feat[at, :].astype(F32) + dot(halo[at, :], first[...])
        mixed_one[at, :] = (summed * inverse[at, :]).astype(BF)
        if c == 0:
            got_w_one.wait()
        pre = dot(mixed_one[at, :], w_one[...])
        pre_one[at, :] = pre
        hidden_one[at, :] = silu_of(pre).astype(BF)

    def spread(values, remote, mixed):
        for c in range(CHUNKS):
            at = pl.ds(c * rows, rows)
            summed = dot(local[at, :], values[...]) + values[at, :].astype(F32) + dot(halo[at, :], remote[...])
            mixed[at, :] = (summed * inverse[at, :]).astype(BF)

    got_w_two.wait()
    got_second.wait()
    spread(hidden_one, second, mixed_two)
    pre = dot(mixed_two[...], w_two[...])
    pre_two[...] = pre
    hidden_two[...] = silu_of(pre).astype(BF)

    got_w_three.wait()
    got_third.wait()
    spread(hidden_two, third, mixed_three)
    logits = dot(mixed_three[...], w_three[...])
    expo = jnp.exp(logits)
    probs = expo / jnp.sum(expo, axis=1, keepdims=True)
    wide = 128
    target = jnp.transpose(
        (lax.broadcasted_iota(jnp.int32, (wide, nodes), 0) == label_ref[...]).astype(F32)
    )[:, : logits.shape[1]]
    up_three = ((probs - target) / nodes).astype(BF)

    out_refs = (above_out, below_out, left_out, right_out)

    def place(array, n):
        for k in range(4):
            sends[k, n] = array[k * bound : (k + 1) * bound].astype(BF)

    def retract(up, weight, returned):
        scaled[...] = (dot(up, weight, (1, 1)) * inverse[...]).astype(BF)
        carried = dot(local[...], scaled[...], (0, 0)) + scaled[...].astype(F32)
        return carried + dot(hits[...], returned[...])

    got_ret_three.wait()
    got_ret_two.wait()
    two = w_two.shape[0]
    one = w_one.shape[0]
    three = w_three.shape[1]
    third_at = two + one + (-one) % 8
    packed[pl.ds(two + one // 16 * 16, ROWS - two - one // 16 * 16), :] = jnp.zeros(
        (ROWS - two - one // 16 * 16, packed.shape[1]), BF
    )
    packed[pl.ds(third_at, three), :] = dot(up_three, mixed_three[...], (0, 0)).astype(BF)
    carried = retract(up_three, w_three[...], ret_three)
    place(dot(halo[...], scaled[...], (0, 0)), 3)
    up_two = (carried * slope(pre_two[...])).astype(BF)
    packed[pl.ds(0, two), :] = dot(mixed_two[...], up_two, (0, 0)).astype(BF)
    carried = retract(up_two, w_two[...], ret_two)
    up_one = (carried * slope(pre_one[...])).astype(BF)
    packed[pl.ds(two, one), :] = dot(mixed_one[...], up_one, (0, 0)).astype(BF)
    out = [fetch(packed, packed_out, out_sem.at[4])]
    place(dot(halo[...], scaled[...], (0, 0)), 2)
    place(dot(hits[...], hidden_one[...], (0, 0)), 0)
    place(dot(hits[...], hidden_two[...], (0, 0)), 1)
    out += [fetch(sends.at[k], out_refs[k], out_sem.at[k]) for k in range(4)]
    for copy in out:
        copy.wait()


def step(index, labels, *arrays):
    (features, local_mask, halo_mask, halo_first, halo_second, halo_third,
     return_second, return_third, weight_first, weight_second, weight_third) = arrays
    nodes, wide = features.shape
    slots, hidden = halo_second.shape
    v = pltpu.VMEM
    scratch = [v(a.shape, a.dtype) for a in arrays]
    scratch += [
        v((nodes, nodes), BF), v((nodes, slots), BF), v((nodes, slots), BF), v((nodes, 1), F32),
        v((nodes, wide), BF), v((nodes, hidden), BF), v((nodes, hidden), BF),
        v((nodes, hidden), F32), v((nodes, hidden), F32),
        v((nodes, hidden), BF), v((nodes, hidden), BF), v((nodes, hidden), BF),
        v((ROWS, hidden), BF), v((4, 4, slots // 4, hidden), BF),
        pltpu.SemaphoreType.DMA((9,)), pltpu.SemaphoreType.DMA((CHUNKS,)),
        pltpu.SemaphoreType.DMA((CHUNKS,)), pltpu.SemaphoreType.DMA((5,)),
    ]
    block = jax.ShapeDtypeStruct((4, slots // 4, hidden), BF)
    return pl.pallas_call(
        step_kernel,
        out_shape=[jax.ShapeDtypeStruct((ROWS, hidden), BF)] + [block] * 4,
        in_specs=[pl.BlockSpec(memory_space=pltpu.VMEM)] * 2 + [pl.BlockSpec(memory_space=pl.ANY)] * len(arrays),
        out_specs=[pl.BlockSpec(memory_space=pl.ANY)] * 5,
        scratch_shapes=scratch,
        compiler_params=pltpu.CompilerParams(vmem_limit_bytes=50 * 2**20),
        cost_estimate=pl.CostEstimate(flops=8_000_000_000, bytes_accessed=12_000_000, transcendentals=1_000_000),
        name="step",
    )(index, labels, *arrays)


GROUP = ("row_1", "col_0", "col_1")
FAR = ("row_0",)


def shares(axes):
    size = 1
    for axis in axes:
        size *= lax.axis_size(axis)
    return size


def copies(piece, axes):
    size = shares(axes)
    return lax.all_to_all(jnp.broadcast_to(piece[None], (size, *piece.shape)), axes, 0, 0, tiled=True)


def summed(pieces):
    return jnp.sum(pieces.astype(jnp.float32), axis=0).astype(jnp.bfloat16)


def total_of(packed):
    size = shares(GROUP)
    pieces = packed.reshape(size, packed.shape[0] // size, packed.shape[1])
    own = summed(lax.all_to_all(pieces, GROUP, 0, 0, tiled=True))
    own = summed(copies(own, FAR))
    return copies(own, GROUP).reshape(packed.shape)


def shifted(block, axis, step):
    size = lax.axis_size(axis)
    pairs = [(i, i + step) for i in range(size) if 0 <= i + step < size]
    return lax.ppermute(block, axis, pairs)


def traded(above, below, left, right):
    got = [shifted(below, ROW, 1), shifted(above, ROW, -1), shifted(right, COL, 1), shifted(left, COL, -1)]
    return [jnp.concatenate([g[n] for g in got], axis=0)[None, None] for n in range(4)]


def per_device(
    features,
    local_mask,
    halo_mask,
    boundary_index,
    labels,
    halo_first,
    halo_second,
    halo_third,
    return_second,
    return_third,
    weight_first,
    weight_second,
    weight_third,
):
    packed, *blocks = step(
        boundary_index[0],
        labels[0],
        features[0, 0],
        local_mask[0, 0],
        halo_mask[0, 0],
        halo_first[0, 0],
        halo_second[0, 0],
        halo_third[0, 0],
        return_second[0, 0],
        return_third[0, 0],
        weight_first,
        weight_second,
        weight_third,
    )
    next_second, next_third, back_second, back_third = traded(*blocks)
    one, two, three = weight_first.shape[0], weight_second.shape[0], weight_third.shape[1]
    third_at = two + one + (-one) % 8
    total = total_of(packed).astype(jnp.float32)
    grad_two = total[:two]
    grad_one = total[two : two + one]
    grad_three = total[third_at : third_at + three].T
    return (grad_one, grad_two, grad_three, next_second, next_third, back_second, back_third)


def solution(mesh):
    torus = Mesh(mesh.devices.reshape(8, 2, 4, 4), ("row_0", "row_1", "col_0", "col_1"))
    in_specs = (
        P(ROW, COL, None, None),
        P(ROW, COL, None, None),
        P(ROW, COL, None, None),
        P(ROW, COL, None),
        P(ROW, COL, None),
        P(ROW, COL, None, None),
        P(ROW, COL, None, None),
        P(ROW, COL, None, None),
        P(ROW, COL, None, None),
        P(ROW, COL, None, None),
        P(),
        P(),
        P(),
    )
    out_specs = (
        P(),
        P(),
        P(),
        P(ROW, COL, None, None),
        P(ROW, COL, None, None),
        P(ROW, COL, None, None),
        P(ROW, COL, None, None),
    )
    return jax.shard_map(
        per_device, mesh=torus, in_specs=in_specs, out_specs=out_specs, check_vma=False
    )
```

time: 94.5 us -> 82.3 us (0.87)
  matrix products: 18.9 us -> 0 us
  Pallas kernels: 0 us -> 15.1 us
  other arithmetic: 10.8 us -> 1.87 us
  local copies, waits for them, and re-layouts: 6.51 us -> 8.61 us
  starting transfers between devices: 39.4 us -> 37.7 us
    dot_general x20 -> x0, matrix products: 18.9 us -> none  [the longest x1 3.62 us: per_device(): jnp.dot(mixed_one.T, upstream_one, preferred_element_type=jnp.float32)]
    pallas_call x0 -> x1, Pallas kernels: none -> 15.1 us  [step(): pl.pallas_call(step_kernel, out_shape=[jax.ShapeDtypeStruct((ROWS, hidden...]
    reduce_sum x1 -> x0, other arithmetic: 4.3 us -> none  [per_device(): jnp.sum(local_mask, axis=1).astype(jnp.float32)]
    convert_element_type x1 -> x0, other arithmetic: 2.68 us -> none  [per_device(): halo_bf = halo_mask.astype(jnp.bfloat16)]
    unnamed x28 -> x19, local copies, waits for them, and re-layouts: 2.3 us -> 4.8 us
    concatenate x1 -> x0, other arithmetic: 1.82 us -> none  [per_device(): jnp.concatenate([grad_two.astype(jnp.bfloat16), jnp.pad(grad_one.astype(j...]
    all_to_all x2, starting transfers between devices: 19.8 us -> 18.8 us  [copies(): lax.all_to_all(jnp.broadcast_to(piece[None], (size, *piece.shape)), axes,...]
  transfers between devices with their start and end apart: 7 -> 7, of which waited for: 2 -> 3; matrix products, arithmetic and copies ran while one was open for 7% -> 4% of each run, Pallas kernels for 0% -> 0%
where the time goes in v2:
time: 82.3 us; the launch traced here: 81.7 us
  starting transfers between devices  37.7 us (46%)
  waiting for transfers between devices  17.6 us (21%)
  Pallas kernels  15.1 us (18%)
  local copies, waits for them, and re-layouts  8.61 us (10%)
  other arithmetic  1.87 us (2%)
  between operations  0.88 us (1%)
    all_to_all x2, starting transfers between devices, copies(): lax.all_to_all(jnp.broadcast_to(piece[None], (size, *piece.shape)), axes,...  18.8 us
    all_to_all x2, waiting for transfers between devices, copies(): lax.all_to_all(jnp.broadcast_to(piece[None], (size, *piece.shape)), axes,...  17.1 us
    pallas_call x1, Pallas kernels, step(): pl.pallas_call(step_kernel, out_shape=[jax.ShapeDtypeStruct((ROWS, hidden...  15.1 us
    ppermute x4, starting transfers between devices, shifted(): return lax.ppermute(block, axis, pairs)  10.3 us
    all_to_all x1, starting transfers between devices, total_of(): own = summed(lax.all_to_all(pieces, GROUP, 0, 0, tiled=True))  8.6 us
    unnamed x19, local copies, waits for them, and re-layouts  4.8 us
    broadcast_in_dim x2, other arithmetic, traded(): jnp.concatenate([g[n] for g in got], axis=0)[None, None]  1.65 us
  transfers between devices with their start and end apart: 7, of which 3 were waited for; matrix products, arithmetic and copies ran while one was open for 4% of the time, Pallas kernels for 0%

profile of v2, /device:TPU:1, one launch (start us, length us, event | category | flops | bytes accessed | tf_op | source)
XLA Modules:
  0.0 81.7 jit_solution(5502178778949638971)
XLA Ops:
  0.6 0.0 copy-start.5
  0.6 0.0 copy-start
  0.7 0.0 copy-start.4
  0.7 0.0 copy-start.3
  0.7 0.0 copy-start.2
  0.7 1.0 %copy.25.weight_third = bf16[256,41]{1,0:T(8,128)(2,1)S(1)} copy(bf16[256,41]{0,1:T(8,128)(2,1)} %param.25) | data formatting | bytes 41984 | tf_op args[12]
  1.7 1.4 %copy.24 = bf16[1,1,512,602]{3,2,1,0:T(8,128)(2,1)S(1)} copy(bf16[1,1,512,602]{2,3,1,0:T(8,128)(2,1)} %param.18) | data formatting | bytes 1232896 | tf_op args[5]
  3.1 2.4 %copy.23 = bf16[1,1,1024,602]{3,2,1,0:T(8,128)(2,1)} copy(bf16[1,1,1024,602]{2,3,1,0:T(8,128)(2,1)} %param.13) | data formatting | bytes 2465792 | tf_op args[0]
  5.5 15.1 %step.1 = (bf16[1024,256]{1,0:T(8,128)(2,1)}, bf16[4,128,256]{2,1,0:T(8,128)(2,1)S(1)}, bf16[4,128,256]{2,1,0:T(8,128)(2,1)S(1)}, bf16[4,128,256]{2,1,0:T(8,128)(2,1)S(1)}, bf16[4,128,256]{2,1,0:T(8,128)(2,1)S(1)}) custom-call(s32[1,512]{1,0:T(1,128)S(1)} %bitcast.61, s32[1,1024]{1,0:T(1,128)S(1)} %bitcast.60, bf16[1024,602]{1,0:T(8,128)(2,1)} %bitcast.64, ...), custom_call_target="tpu_custom_call" | custom-call | flops 8000000000 | bytes 12000000 | tf_op jit(solution)/shard_map/step/pallas_call | solution.py:176
  20.7 8.6 %all-to-all-start = ((bf16[32,32,256]{2,1,0:T(8,128)(2,1)}), bf16[32,32,256]{2,1,0:T(8,128)(2,1)S(1)}, u32[]{:S(2)}, u32[]{:S(2)}) async-start(bf16[32,32,256]{2,1,0:T(8,128)(2,1)} %bitcast.10), calls=%async_computation | async-start | bytes 1048576 | tf_op jit(solution)/shard_map/all_to_all | solution.py:211
  29.3 3.6 %collective-permute-start = (bf16[4,128,256]{2,1,0:T(8,128)(2,1)S(1)}, bf16[4,128,256]{2,1,0:T(8,128)(2,1)S(1)}, u32[]{:S(2)}, u32[]{:S(2)}) collective-permute-start(bf16[4,128,256]{2,1,0:T(8,128)(2,1)S(1)} %get-tuple-element.13), channel_id=1, source_target_pairs={{0,16},{16,32},{32,48},{48,64},{64,80},{80,96},{96,112},{112,128},... | collective-permute-start | bytes 786440 | tf_op jit(solution)/shard_map/ppermute | solution.py:219
  32.9 1.9 %collective-permute-start.1 = (bf16[4,128,256]{2,1,0:T(8,128)(2,1)S(1)}, bf16[4,128,256]{2,1,0:T(8,128)(2,1)S(1)}, u32[]{:S(2)}, u32[]{:S(2)}) collective-permute-start(bf16[4,128,256]{2,1,0:T(8,128)(2,1)S(1)} %get-tuple-element.14), channel_id=1, source_target_pairs={{16,0},{32,16},{48,32},{64,48},{80,64},{96,80},{112,96},{128,112},... | collective-permute-start | bytes 786440 | tf_op jit(solution)/shard_map/ppermute | solution.py:219
  34.8 3.4 %collective-permute-start.2 = (bf16[4,128,256]{2,1,0:T(8,128)(2,1)S(1)}, bf16[4,128,256]{2,1,0:T(8,128)(2,1)S(1)}, u32[]{:S(2)}, u32[]{:S(2)}) collective-permute-start(bf16[4,128,256]{2,1,0:T(8,128)(2,1)S(1)} %get-tuple-element.15), channel_id=1, source_target_pairs={{0,1},{1,2},{2,3},{3,4},{4,5},{5,6},{6,7},{7,8},{8,9},{9,10},{10,1... | collective-permute-start | bytes 786440 | tf_op jit(solution)/shard_map/ppermute | solution.py:219
  38.3 1.3 %collective-permute-start.3 = (bf16[4,128,256]{2,1,0:T(8,128)(2,1)S(1)}, bf16[4,128,256]{2,1,0:T(8,128)(2,1)S(1)}, u32[]{:S(2)}, u32[]{:S(2)}) collective-permute-start(bf16[4,128,256]{2,1,0:T(8,128)(2,1)S(1)} %get-tuple-element.16), channel_id=1, source_target_pairs={{1,0},{2,1},{3,2},{4,3},{5,4},{6,5},{7,6},{8,7},{9,8},{10,9},{11,1... | collective-permute-start | bytes 786440 | tf_op jit(solution)/shard_map/ppermute | solution.py:219
  39.6 0.0 collective-permute-done
  39.6 0.5 all-to-all-done
  40.1 0.1 reduce_sum.24
  40.2 0.7 broadcast_in_dim.24
  40.9 8.2 %all-to-all-start.1 = ((bf16[8,32,256]{2,1,0:T(8,128)(2,1)}), bf16[8,32,256]{2,1,0:T(8,128)(2,1)S(1)}, u32[]{:S(2)}, u32[]{:S(2)}) async-start(bf16[8,32,256]{2,1,0:T(8,128)(2,1)} %broadcast_in_dim.24), calls=%async_computation.1 | async-start | bytes 262144 | tf_op jit(solution)/shard_map/all_to_all | solution.py:201
  49.1 0.0 collective-permute-done.1
  49.1 7.9 %all-to-all-done.1 = bf16[8,32,256]{2,1,0:T(8,128)(2,1)S(1)} async-done(((bf16[8,32,256]{2,1,0:T(8,128)(2,1)}), bf16[8,32,256]{2,1,0:T(8,128)(2,1)S(1)}, u32[]{:S(2)}, u32[]{:S(2)}) %all-to-all-start.1) | async-done | bytes 131104 | tf_op jit(solution)/shard_map/all_to_all | solution.py:201
  57.1 0.9 %broadcast_in_dim.25 = bf16[32,32,256]{2,1,0:T(8,128)(2,1)} broadcast(bf16[32,256]{1,0:T(8,128)(2,1)S(1)} %reduce_sum.25), dimensions={1,2} | broadcast | bytes 540672 | tf_op jit(solution)/shard_map/broadcast_in_dim | solution.py:201
  57.9 10.6 %all-to-all-start.2 = ((bf16[32,32,256]{2,1,0:T(8,128)(2,1)}), bf16[32,32,256]{2,1,0:T(8,128)(2,1)S(1)}, u32[]{:S(2)}, u32[]{:S(2)}) async-start(bf16[32,32,256]{2,1,0:T(8,128)(2,1)} %broadcast_in_dim.25), calls=%async_computation.2 | async-start | bytes 1048576 | tf_op jit(solution)/shard_map/all_to_all | solution.py:201
  68.5 0.0 collective-permute-done.2
  68.5 0.0 collective-permute-done.3
  68.6 0.8 %maximum_bitcast_fusion.2 = (bf16[1,1,512,256]{3,2,1,0:T(8,128)(2,1)}, bf16[1,1,512,256]{3,2,1,0:T(8,128)(2,1)}) fusion(bf16[128,256]{1,0:T(8,128)(2,1)S(1)} %get-tuple-element.30, bf16[128,256]{1,0:T(8,128)(2,1)S(1)} %get-tuple-element.26, bf16[128,256]{1,0:T(8,128)(2,1)S(1)} %get-tuple-element.22, bf16[128,256]{1,0:T(8,128)(2,1)S(1)} %get-tuple-element.18, ...), kind=kLoop, calls=%fused_computation.2 | loop fusion | flops 2097152 | bytes 1048576 | tf_op jit(solution)/shard_map/broadcast_in_dim | solution.py:224
  69.4 0.8 %maximum_bitcast_fusion = (bf16[1,1,512,256]{3,2,1,0:T(8,128)(2,1)}, bf16[1,1,512,256]{3,2,1,0:T(8,128)(2,1)}) fusion(bf16[128,256]{1,0:T(8,128)(2,1)S(1)} %get-tuple-element.32, bf16[128,256]{1,0:T(8,128)(2,1)S(1)} %get-tuple-element.28, bf16[128,256]{1,0:T(8,128)(2,1)S(1)} %get-tuple-element.24, bf16[128,256]{1,0:T(8,128)(2,1)S(1)} %get-tuple-element.20, ...), kind=kLoop, calls=%fused_computation | loop fusion | flops 2097152 | bytes 1048576 | tf_op jit(solution)/shard_map/broadcast_in_dim | solution.py:224
  70.2 9.2 %all-to-all-done.2 = bf16[32,32,256]{2,1,0:T(8,128)(2,1)S(1)} async-done(((bf16[32,32,256]{2,1,0:T(8,128)(2,1)}), bf16[32,32,256]{2,1,0:T(8,128)(2,1)S(1)}, u32[]{:S(2)}, u32[]{:S(2)}) %all-to-all-start.2) | async-done | bytes 524320 | tf_op jit(solution)/shard_map/all_to_all | solution.py:201
  79.4 0.1 convert_element_type.10
  79.5 0.6 slice_bitcast_fusion.16
  80.1 0.9 %slice.80 = f32[602,256]{1,0:T(8,128)} slice(f32[1024,256]{1,0:T(8,128)S(1)} %bitcast.63), slice={[256:858], [0:256]} | slice | bytes 1232896 | tf_op jit(solution)/shard_map/slice | solution.py:262
  81.0 0.7 slice.81
  (16 shorter events, 0.1 us)
Async XLA Ops:
  0.6 4.9 %copy-start.5 = (bf16[256,256]{1,0:T(8,128)(2,1)S(1)}, bf16[256,256]{1,0:T(8,128)(2,1)}, u32[]{:S(2)}) copy-start(bf16[256,256]{1,0:T(8,128)(2,1)} %weight_second.1) | copy-start | bytes 393220
  0.6 4.8 %copy-start = (bf16[602,256]{1,0:T(8,128)(2,1)S(1)}, bf16[602,256]{1,0:T(8,128)(2,1)}, u32[]{:S(2)}) copy-start(bf16[602,256]{1,0:T(8,128)(2,1)} %weight_first.1) | copy-start | bytes 924676
  0.7 4.8 %copy-start.4 = (bf16[1,1,512,256]{3,2,1,0:T(8,128)(2,1)S(1)}, bf16[1,1,512,256]{3,2,1,0:T(8,128)(2,1)}, u32[]{:S(2)}) copy-start(bf16[1,1,512,256]{3,2,1,0:T(8,128)(2,1)} %param.22) | copy-start | bytes 786436
  0.7 4.8 %copy-start.3 = (bf16[1,1,512,256]{3,2,1,0:T(8,128)(2,1)S(1)}, bf16[1,1,512,256]{3,2,1,0:T(8,128)(2,1)}, u32[]{:S(2)}) copy-start(bf16[1,1,512,256]{3,2,1,0:T(8,128)(2,1)} %param.21) | copy-start | bytes 786436
  0.7 4.8 %copy-start.2 = (bf16[1,1,512,256]{3,2,1,0:T(8,128)(2,1)S(1)}, bf16[1,1,512,256]{3,2,1,0:T(8,128)(2,1)}, u32[]{:S(2)}) copy-start(bf16[1,1,512,256]{3,2,1,0:T(8,128)(2,1)} %param.20) | copy-start | bytes 786436
  0.7 4.8 %copy-start.1 = (bf16[1,1,512,256]{3,2,1,0:T(8,128)(2,1)S(1)}, bf16[1,1,512,256]{3,2,1,0:T(8,128)(2,1)}, u32[]{:S(2)}) copy-start(bf16[1,1,512,256]{3,2,1,0:T(8,128)(2,1)} %param.19) | copy-start | bytes 786436
  0.7 4.8 %copy-start.6 = (s32[1,1,1024]{2,1,0:T(1,128)S(1)}, s32[1,1,1024]{2,1,0:T(1,128)}, u32[]{:S(2)}) copy-start(s32[1,1,1024]{2,1,0:T(1,128)} %param.17) | copy-start | bytes 12292
  0.7 4.8 %copy-start.7 = (s32[1,1,512]{2,1,0:T(1,128)S(1)}, s32[1,1,512]{2,1,0:T(1,128)}, u32[]{:S(2)}) copy-start(s32[1,1,512]{2,1,0:T(1,128)} %param.16) | copy-start | bytes 6148
  20.7 19.5 %all-to-all-start = ((bf16[32,32,256]{2,1,0:T(8,128)(2,1)}), bf16[32,32,256]{2,1,0:T(8,128)(2,1)S(1)}, u32[]{:S(2)}, u32[]{:S(2)}) async-start(bf16[32,32,256]{2,1,0:T(8,128)(2,1)} %bitcast.10), calls=%async_computation | async-start | bytes 1048576 | tf_op jit(solution)/shard_map/all_to_all | solution.py:211
  29.3 10.3 %collective-permute-start = (bf16[4,128,256]{2,1,0:T(8,128)(2,1)S(1)}, bf16[4,128,256]{2,1,0:T(8,128)(2,1)S(1)}, u32[]{:S(2)}, u32[]{:S(2)}) collective-permute-start(bf16[4,128,256]{2,1,0:T(8,128)(2,1)S(1)} %get-tuple-element.13), channel_id=1, source_target_pairs={{0,16},{16,32},{32,48},{48,64},{64,80},{80,96},{96,112},{112,128},... | collective-permute-start | bytes 786440 | tf_op jit(solution)/shard_map/ppermute | solution.py:219
  32.9 16.2 %collective-permute-start.1 = (bf16[4,128,256]{2,1,0:T(8,128)(2,1)S(1)}, bf16[4,128,256]{2,1,0:T(8,128)(2,1)S(1)}, u32[]{:S(2)}, u32[]{:S(2)}) collective-permute-start(bf16[4,128,256]{2,1,0:T(8,128)(2,1)S(1)} %get-tuple-element.14), channel_id=1, source_target_pairs={{16,0},{32,16},{48,32},{64,48},{80,64},{96,80},{112,96},{128,112},... | collective-permute-start | bytes 786440 | tf_op jit(solution)/shard_map/ppermute | solution.py:219
  34.8 33.7 %collective-permute-start.2 = (bf16[4,128,256]{2,1,0:T(8,128)(2,1)S(1)}, bf16[4,128,256]{2,1,0:T(8,128)(2,1)S(1)}, u32[]{:S(2)}, u32[]{:S(2)}) collective-permute-start(bf16[4,128,256]{2,1,0:T(8,128)(2,1)S(1)} %get-tuple-element.15), channel_id=1, source_target_pairs={{0,1},{1,2},{2,3},{3,4},{4,5},{5,6},{6,7},{7,8},{8,9},{9,10},{10,1... | collective-permute-start | bytes 786440 | tf_op jit(solution)/shard_map/ppermute | solution.py:219
  38.3 30.3 %collective-permute-start.3 = (bf16[4,128,256]{2,1,0:T(8,128)(2,1)S(1)}, bf16[4,128,256]{2,1,0:T(8,128)(2,1)S(1)}, u32[]{:S(2)}, u32[]{:S(2)}) collective-permute-start(bf16[4,128,256]{2,1,0:T(8,128)(2,1)S(1)} %get-tuple-element.16), channel_id=1, source_target_pairs={{1,0},{2,1},{3,2},{4,3},{5,4},{6,5},{7,6},{8,7},{9,8},{10,9},{11,1... | collective-permute-start | bytes 786440 | tf_op jit(solution)/shard_map/ppermute | solution.py:219
  40.9 16.1 %all-to-all-start.1 = ((bf16[8,32,256]{2,1,0:T(8,128)(2,1)}), bf16[8,32,256]{2,1,0:T(8,128)(2,1)S(1)}, u32[]{:S(2)}, u32[]{:S(2)}) async-start(bf16[8,32,256]{2,1,0:T(8,128)(2,1)} %broadcast_in_dim.24), calls=%async_computation.1 | async-start | bytes 262144 | tf_op jit(solution)/shard_map/all_to_all | solution.py:201
  57.9 21.5 %all-to-all-start.2 = ((bf16[32,32,256]{2,1,0:T(8,128)(2,1)}), bf16[32,32,256]{2,1,0:T(8,128)(2,1)S(1)}, u32[]{:S(2)}, u32[]{:S(2)}) async-start(bf16[32,32,256]{2,1,0:T(8,128)(2,1)} %broadcast_in_dim.25), calls=%async_computation.2 | async-start | bytes 1048576 | tf_op jit(solution)/shard_map/all_to_all | solution.py:201

commit v3 on v2

--- a/solution.py
+++ b/solution.py
@@ -6,6 +6,7 @@
 from jax.sharding import Mesh
 from jax.sharding import PartitionSpec as P
 
+
 ROW = ("row_0", "row_1")
 COL = ("col_0", "col_1")
 
@@ -30,15 +31,19 @@
 ROWS = 1024
 
 
+def padded_up(size):
+    return size + (-size) % 128
+
+
 def step_kernel(
     index_ref, label_ref, features, local_mask, halo_mask, halo_first, halo_second, halo_third,
     return_second, return_third, weight_first, weight_second, weight_third,
     packed_out, above_out, below_out, left_out, right_out,
-    feat, local_raw, halo_raw, first, second, third, ret_two, ret_three, w_one, w_two, w_three,
+    feat_t, local_raw, halo_raw, first_t, second, third, ret_two, ret_three, w_one, w_two, w_three,
     local, halo, hits, inverse, mixed_one, mixed_two, mixed_three, pre_one, pre_two,
-    hidden_one, hidden_two, scaled, packed, sends, in_sem, local_sem, halo_sem, out_sem,
+    hidden_one, hidden_two, scaled, packed, sends, feat, first, in_sem, local_sem, halo_sem, out_sem,
 ):
-    nodes = feat.shape[0]
+    nodes, wide = feat.shape
     rows = nodes // CHUNKS
     bound = hits.shape[1] // 4
 
@@ -50,8 +55,8 @@
     def part(ref, c):
         return ref.at[pl.ds(c * rows, rows)]
 
-    got_feat = fetch(features, feat, in_sem.at[0])
-    got_first = fetch(halo_first, first, in_sem.at[1])
+    got_feat = fetch(features, feat_t, in_sem.at[0])
+    got_first = fetch(halo_first, first_t, in_sem.at[1])
     got_local, got_halo = [], []
     for c in range(CHUNKS):
         got_local.append(fetch(part(local_mask, c), part(local_raw, c), local_sem.at[c]))
@@ -73,7 +78,9 @@
     ).astype(F32).astype(BF)
 
     got_feat.wait()
+    feat[...] = jnp.transpose(feat_t[...])
     got_first.wait()
+    first[...] = jnp.transpose(first_t[...])
     for c in range(CHUNKS):
         at = pl.ds(c * rows, rows)
         got_local[c].wait()
@@ -110,12 +117,11 @@
     got_w_three.wait()
     got_third.wait()
     spread(hidden_two, third, mixed_three)
-    logits = dot(mixed_three[...], w_three[...])
+    logits = dot(mixed_three[...], w_three[...], (1, 1))
     expo = jnp.exp(logits)
     probs = expo / jnp.sum(expo, axis=1, keepdims=True)
-    wide = 128
     target = jnp.transpose(
-        (lax.broadcasted_iota(jnp.int32, (wide, nodes), 0) == label_ref[...]).astype(F32)
+        (lax.broadcasted_iota(jnp.int32, (128, nodes), 0) == label_ref[...]).astype(F32)
     )[:, : logits.shape[1]]
     up_three = ((probs - target) / nodes).astype(BF)
 
@@ -125,28 +131,26 @@
         for k in range(4):
             sends[k, n] = array[k * bound : (k + 1) * bound].astype(BF)
 
-    def retract(up, weight, returned):
-        scaled[...] = (dot(up, weight, (1, 1)) * inverse[...]).astype(BF)
+    def retract(across, returned):
+        scaled[...] = (across * inverse[...]).astype(BF)
         carried = dot(local[...], scaled[...], (0, 0)) + scaled[...].astype(F32)
         return carried + dot(hits[...], returned[...])
 
     got_ret_three.wait()
     got_ret_two.wait()
     two = w_two.shape[0]
-    one = w_one.shape[0]
-    three = w_three.shape[1]
-    third_at = two + one + (-one) % 8
-    packed[pl.ds(two + one // 16 * 16, ROWS - two - one // 16 * 16), :] = jnp.zeros(
-        (ROWS - two - one // 16 * 16, packed.shape[1]), BF
-    )
+    three = w_three.shape[0]
+    third_at = two + padded_up(wide)
+    tail = two + wide // 16 * 16
+    packed[pl.ds(tail, ROWS - tail), :] = jnp.zeros((ROWS - tail, packed.shape[1]), BF)
     packed[pl.ds(third_at, three), :] = dot(up_three, mixed_three[...], (0, 0)).astype(BF)
-    carried = retract(up_three, w_three[...], ret_three)
+    carried = retract(dot(up_three, w_three[...]), ret_three)
     place(dot(halo[...], scaled[...], (0, 0)), 3)
     up_two = (carried * slope(pre_two[...])).astype(BF)
     packed[pl.ds(0, two), :] = dot(mixed_two[...], up_two, (0, 0)).astype(BF)
-    carried = retract(up_two, w_two[...], ret_two)
+    carried = retract(dot(up_two, w_two[...], (1, 1)), ret_two)
     up_one = (carried * slope(pre_one[...])).astype(BF)
-    packed[pl.ds(two, one), :] = dot(mixed_one[...], up_one, (0, 0)).astype(BF)
+    packed[pl.ds(two, wide), :] = dot(mixed_one[...], up_one, (0, 0)).astype(BF)
     out = [fetch(packed, packed_out, out_sem.at[4])]
     place(dot(halo[...], scaled[...], (0, 0)), 2)
     place(dot(hits[...], hidden_one[...], (0, 0)), 0)
@@ -157,9 +161,10 @@
 
 
 def step(index, labels, *arrays):
-    (features, local_mask, halo_mask, halo_first, halo_second, halo_third,
-     return_second, return_third, weight_first, weight_second, weight_third) = arrays
-    nodes, wide = features.shape
+    (features, _, _, _, halo_second, _,
+     _, _, _, _, _) = arrays
+    depth, nodes = features.shape
+    wide = depth
     slots, hidden = halo_second.shape
     v = pltpu.VMEM
     scratch = [v(a.shape, a.dtype) for a in arrays]
@@ -169,6 +174,7 @@
         v((nodes, hidden), F32), v((nodes, hidden), F32),
         v((nodes, hidden), BF), v((nodes, hidden), BF), v((nodes, hidden), BF),
         v((ROWS, hidden), BF), v((4, 4, slots // 4, hidden), BF),
+        v((nodes, wide), BF), v((slots, wide), BF),
         pltpu.SemaphoreType.DMA((9,)), pltpu.SemaphoreType.DMA((CHUNKS,)),
         pltpu.SemaphoreType.DMA((CHUNKS,)), pltpu.SemaphoreType.DMA((5,)),
     ]
@@ -176,10 +182,10 @@
     return pl.pallas_call(
         step_kernel,
         out_shape=[jax.ShapeDtypeStruct((ROWS, hidden), BF)] + [block] * 4,
-        in_specs=[pl.BlockSpec(memory_space=pltpu.VMEM)] * 2 + [pl.BlockSpec(memory_space=pl.ANY)] * len(arrays),
+        in_specs=[pl.BlockSpec(memory_space=pltpu.VMEM)] * 2 + [pl.BlockSpec(memory_space=pltpu.HBM)] * len(arrays),
         out_specs=[pl.BlockSpec(memory_space=pl.ANY)] * 5,
         scratch_shapes=scratch,
-        compiler_params=pltpu.CompilerParams(vmem_limit_bytes=50 * 2**20),
+        compiler_params=pltpu.CompilerParams(vmem_limit_bytes=66_000_000),
         cost_estimate=pl.CostEstimate(flops=8_000_000_000, bytes_accessed=12_000_000, transcendentals=1_000_000),
         name="step",
     )(index, labels, *arrays)
@@ -205,23 +211,23 @@
     return jnp.sum(pieces.astype(jnp.float32), axis=0).astype(jnp.bfloat16)
 
 
-def total_of(packed):
+def total_of(packed, lateral, vertical):
     size = shares(GROUP)
     pieces = packed.reshape(size, packed.shape[0] // size, packed.shape[1])
-    own = summed(lax.all_to_all(pieces, GROUP, 0, 0, tiled=True))
-    own = summed(copies(own, FAR))
-    return copies(own, GROUP).reshape(packed.shape)
+    own = lax.all_to_all(pieces, GROUP, 0, 0, tiled=True)
+    first = lateral()
+    own = summed(own)
+    own = copies(own, FAR)
+    own = summed(own)
+    whole = copies(own, GROUP)
+    last = vertical()
+    return whole.reshape(packed.shape), first, last
 
 
 def shifted(block, axis, step):
     size = lax.axis_size(axis)
     pairs = [(i, i + step) for i in range(size) if 0 <= i + step < size]
     return lax.ppermute(block, axis, pairs)
-
-
-def traded(above, below, left, right):
-    got = [shifted(below, ROW, 1), shifted(above, ROW, -1), shifted(right, COL, 1), shifted(left, COL, -1)]
-    return [jnp.concatenate([g[n] for g in got], axis=0)[None, None] for n in range(4)]
 
 
 def per_device(
@@ -242,22 +248,34 @@
     packed, *blocks = step(
         boundary_index[0],
         labels[0],
-        features[0, 0],
+        features[0, 0].T,
         local_mask[0, 0],
         halo_mask[0, 0],
-        halo_first[0, 0],
+        halo_first[0, 0].T,
         halo_second[0, 0],
         halo_third[0, 0],
         return_second[0, 0],
         return_third[0, 0],
         weight_first,
         weight_second,
-        weight_third,
+        weight_third.T,
     )
-    next_second, next_third, back_second, back_third = traded(*blocks)
+    above, below, left, right = blocks
+
+    def lateral():
+        return [shifted(right, COL, 1), shifted(left, COL, -1)]
+
+    def vertical():
+        return [shifted(below, ROW, 1), shifted(above, ROW, -1)]
+
     one, two, three = weight_first.shape[0], weight_second.shape[0], weight_third.shape[1]
-    third_at = two + one + (-one) % 8
-    total = total_of(packed).astype(jnp.float32)
+    third_at = two + padded_up(one)
+    total, lateral_got, vertical_got = total_of(packed, lateral, vertical)
+    got = vertical_got + lateral_got
+    next_second, next_third, back_second, back_third = [
+        jnp.concatenate([g[n] for g in got], axis=0)[None, None] for n in range(4)
+    ]
+    total = total.astype(jnp.float32)
     grad_two = total[:two]
     grad_one = total[two : two + one]
     grad_three = total[third_at : third_at + three].T

time: 82.3 us -> 79.4 us (0.965)
  local copies, waits for them, and re-layouts: 8.61 us -> 3.82 us
  Pallas kernels: 15.1 us -> 17 us
    unnamed x19 -> x0, local copies, waits for them, and re-layouts: 4.8 us -> none
    pallas_call x1, Pallas kernels: 15.1 us -> 17 us  [step(): pl.pallas_call(step_kernel, out_shape=[jax.ShapeDtypeStruct((ROWS, hidden...]
where the time goes in v3:
time: 79.4 us; the launch traced here: 78.7 us
  starting transfers between devices  37.7 us (47%)
  waiting for transfers between devices  17.6 us (22%)
  Pallas kernels  17 us (21%)
  local copies, waits for them, and re-layouts  3.82 us (5%)
  other arithmetic  1.87 us (2%)
    all_to_all x2, starting transfers between devices, copies(): lax.all_to_all(jnp.broadcast_to(piece[None], (size, *piece.shape)), axes,...  18.8 us
    all_to_all x2, waiting for transfers between devices, copies(): lax.all_to_all(jnp.broadcast_to(piece[None], (size, *piece.shape)), axes,...  17.1 us
    pallas_call x1, Pallas kernels, step(): pl.pallas_call(step_kernel, out_shape=[jax.ShapeDtypeStruct((ROWS, hidden...  17 us
    ppermute x4, starting transfers between devices, shifted(): return lax.ppermute(block, axis, pairs)  10.3 us
    all_to_all x1, starting transfers between devices, total_of(): own = lax.all_to_all(pieces, GROUP, 0, 0, tiled=True)  8.6 us
    broadcast_in_dim x2, other arithmetic, per_device(): jnp.concatenate([g[n] for g in got], axis=0)[None, None]  1.65 us
  transfers between devices with their start and end apart: 7, of which 3 were waited for; matrix products, arithmetic and copies ran while one was open for 4% of the time, Pallas kernels for 0%

profile of v3, /device:TPU:1, one launch (start us, length us, event | category | flops | bytes accessed | tf_op | source)
XLA Modules:
  0.0 78.7 jit_solution(6973502171538781839)
XLA Ops:
  0.6 17.0 %step.1 = (bf16[1024,256]{1,0:T(8,128)(2,1)}, bf16[4,128,256]{2,1,0:T(8,128)(2,1)}, bf16[4,128,256]{2,1,0:T(8,128)(2,1)}, bf16[4,128,256]{2,1,0:T(8,128)(2,1)}, bf16[4,128,256]{2,1,0:T(8,128)(2,1)}) custom-call(s32[1,512]{1,0:T(1,128)} %bitcast.74, s32[1,1024]{1,0:T(1,128)} %bitcast.73, bf16[602,1024]{1,0:T(8,128)(2,1)} %bitcast.66, s32[1024,1024]{1,0:T(8,128)} %bitcast.64, ...), custom_call_target="tpu_custom_call" | custom-call | flops 8000000000 | bytes 12000000 | tf_op jit(solution)/shard_map/step/pallas_call | solution.py:182
  17.6 8.6 %all-to-all-start = ((bf16[32,32,256]{2,1,0:T(8,128)(2,1)}), bf16[32,32,256]{2,1,0:T(8,128)(2,1)S(1)}, u32[]{:S(2)}, u32[]{:S(2)}) async-start(bf16[32,32,256]{2,1,0:T(8,128)(2,1)} %bitcast.62), calls=%async_computation | async-start | bytes 1048576 | tf_op jit(solution)/shard_map/all_to_all | solution.py:217
  26.3 3.7 %collective-permute-start = (bf16[4,128,256]{2,1,0:T(8,128)(2,1)}, bf16[4,128,256]{2,1,0:T(8,128)(2,1)S(1)}, u32[]{:S(2)}, u32[]{:S(2)}) collective-permute-start(bf16[4,128,256]{2,1,0:T(8,128)(2,1)} %get-tuple-element.13), channel_id=1, source_target_pairs={{0,16},{16,32},{32,48},{48,64},{64,80},{80,96},{96,112},{112,128},... | collective-permute-start | bytes 786440 | tf_op jit(solution)/shard_map/ppermute | solution.py:230
  29.9 1.9 %collective-permute-start.1 = (bf16[4,128,256]{2,1,0:T(8,128)(2,1)}, bf16[4,128,256]{2,1,0:T(8,128)(2,1)S(1)}, u32[]{:S(2)}, u32[]{:S(2)}) collective-permute-start(bf16[4,128,256]{2,1,0:T(8,128)(2,1)} %get-tuple-element.14), channel_id=1, source_target_pairs={{16,0},{32,16},{48,32},{64,48},{80,64},{96,80},{112,96},{128,112},... | collective-permute-start | bytes 786440 | tf_op jit(solution)/shard_map/ppermute | solution.py:230
  31.9 3.4 %collective-permute-start.2 = (bf16[4,128,256]{2,1,0:T(8,128)(2,1)}, bf16[4,128,256]{2,1,0:T(8,128)(2,1)S(1)}, u32[]{:S(2)}, u32[]{:S(2)}) collective-permute-start(bf16[4,128,256]{2,1,0:T(8,128)(2,1)} %get-tuple-element.15), channel_id=1, source_target_pairs={{0,1},{1,2},{2,3},{3,4},{4,5},{5,6},{6,7},{7,8},{8,9},{9,10},{10,1... | collective-permute-start | bytes 786440 | tf_op jit(solution)/shard_map/ppermute | solution.py:230
  35.3 1.3 %collective-permute-start.3 = (bf16[4,128,256]{2,1,0:T(8,128)(2,1)}, bf16[4,128,256]{2,1,0:T(8,128)(2,1)S(1)}, u32[]{:S(2)}, u32[]{:S(2)}) collective-permute-start(bf16[4,128,256]{2,1,0:T(8,128)(2,1)} %get-tuple-element.16), channel_id=1, source_target_pairs={{1,0},{2,1},{3,2},{4,3},{5,4},{6,5},{7,6},{8,7},{9,8},{10,9},{11,1... | collective-permute-start | bytes 786440 | tf_op jit(solution)/shard_map/ppermute | solution.py:230
  36.6 0.0 collective-permute-done
  36.6 0.5 all-to-all-done
  37.1 0.1 reduce_sum.24
  37.2 0.7 broadcast_in_dim.24
  37.9 8.2 %all-to-all-start.1 = ((bf16[8,32,256]{2,1,0:T(8,128)(2,1)}), bf16[8,32,256]{2,1,0:T(8,128)(2,1)S(1)}, u32[]{:S(2)}, u32[]{:S(2)}) async-start(bf16[8,32,256]{2,1,0:T(8,128)(2,1)} %broadcast_in_dim.24), calls=%async_computation.1 | async-start | bytes 262144 | tf_op jit(solution)/shard_map/all_to_all | solution.py:207
  46.1 0.0 collective-permute-done.1
  46.1 7.9 %all-to-all-done.1 = bf16[8,32,256]{2,1,0:T(8,128)(2,1)S(1)} async-done(((bf16[8,32,256]{2,1,0:T(8,128)(2,1)}), bf16[8,32,256]{2,1,0:T(8,128)(2,1)S(1)}, u32[]{:S(2)}, u32[]{:S(2)}) %all-to-all-start.1) | async-done | bytes 131104 | tf_op jit(solution)/shard_map/all_to_all | solution.py:207
  54.1 0.9 %broadcast_in_dim.25 = bf16[32,32,256]{2,1,0:T(8,128)(2,1)} broadcast(bf16[32,256]{1,0:T(8,128)(2,1)S(1)} %reduce_sum.25), dimensions={1,2} | broadcast | bytes 540672 | tf_op jit(solution)/shard_map/broadcast_in_dim | solution.py:207
  54.9 10.6 %all-to-all-start.2 = ((bf16[32,32,256]{2,1,0:T(8,128)(2,1)}), bf16[32,32,256]{2,1,0:T(8,128)(2,1)S(1)}, u32[]{:S(2)}, u32[]{:S(2)}) async-start(bf16[32,32,256]{2,1,0:T(8,128)(2,1)} %broadcast_in_dim.25), calls=%async_computation.2 | async-start | bytes 1048576 | tf_op jit(solution)/shard_map/all_to_all | solution.py:207
  65.5 0.0 collective-permute-done.2
  65.5 0.0 collective-permute-done.3
  65.6 0.8 %maximum_bitcast_fusion.2 = (bf16[1,1,512,256]{3,2,1,0:T(8,128)(2,1)}, bf16[1,1,512,256]{3,2,1,0:T(8,128)(2,1)}) fusion(bf16[128,256]{1,0:T(8,128)(2,1)S(1)} %get-tuple-element.30, bf16[128,256]{1,0:T(8,128)(2,1)S(1)} %get-tuple-element.26, bf16[128,256]{1,0:T(8,128)(2,1)S(1)} %get-tuple-element.22, bf16[128,256]{1,0:T(8,128)(2,1)S(1)} %get-tuple-element.18, ...), kind=kLoop, calls=%fused_computation.2 | loop fusion | flops 2097152 | bytes 1048576 | tf_op jit(solution)/shard_map/broadcast_in_dim | solution.py:276
  66.4 0.8 %maximum_bitcast_fusion = (bf16[1,1,512,256]{3,2,1,0:T(8,128)(2,1)}, bf16[1,1,512,256]{3,2,1,0:T(8,128)(2,1)}) fusion(bf16[128,256]{1,0:T(8,128)(2,1)S(1)} %get-tuple-element.32, bf16[128,256]{1,0:T(8,128)(2,1)S(1)} %get-tuple-element.28, bf16[128,256]{1,0:T(8,128)(2,1)S(1)} %get-tuple-element.24, bf16[128,256]{1,0:T(8,128)(2,1)S(1)} %get-tuple-element.20, ...), kind=kLoop, calls=%fused_computation | loop fusion | flops 2097152 | bytes 1048576 | tf_op jit(solution)/shard_map/broadcast_in_dim | solution.py:276
  67.2 9.2 %all-to-all-done.2 = bf16[32,32,256]{2,1,0:T(8,128)(2,1)S(1)} async-done(((bf16[32,32,256]{2,1,0:T(8,128)(2,1)}), bf16[32,32,256]{2,1,0:T(8,128)(2,1)S(1)}, u32[]{:S(2)}, u32[]{:S(2)}) %all-to-all-start.2) | async-done | bytes 524320 | tf_op jit(solution)/shard_map/all_to_all | solution.py:207
  76.4 0.1 convert_element_type.10
  76.5 0.6 slice_bitcast_fusion.16
  77.1 0.9 %slice.80 = f32[602,256]{1,0:T(8,128)} slice(f32[1024,256]{1,0:T(8,128)S(1)} %bitcast.61), slice={[256:858], [0:256]} | slice | bytes 1232896 | tf_op jit(solution)/shard_map/slice | solution.py:280
  78.0 0.7 slice.81
  (5 shorter events, 0.1 us)
Async XLA Ops:
  17.6 19.5 %all-to-all-start = ((bf16[32,32,256]{2,1,0:T(8,128)(2,1)}), bf16[32,32,256]{2,1,0:T(8,128)(2,1)S(1)}, u32[]{:S(2)}, u32[]{:S(2)}) async-start(bf16[32,32,256]{2,1,0:T(8,128)(2,1)} %bitcast.62), calls=%async_computation | async-start | bytes 1048576 | tf_op jit(solution)/shard_map/all_to_all | solution.py:217
  26.3 10.3 %collective-permute-start = (bf16[4,128,256]{2,1,0:T(8,128)(2,1)}, bf16[4,128,256]{2,1,0:T(8,128)(2,1)S(1)}, u32[]{:S(2)}, u32[]{:S(2)}) collective-permute-start(bf16[4,128,256]{2,1,0:T(8,128)(2,1)} %get-tuple-element.13), channel_id=1, source_target_pairs={{0,16},{16,32},{32,48},{48,64},{64,80},{80,96},{96,112},{112,128},... | collective-permute-start | bytes 786440 | tf_op jit(solution)/shard_map/ppermute | solution.py:230
  29.9 16.2 %collective-permute-start.1 = (bf16[4,128,256]{2,1,0:T(8,128)(2,1)}, bf16[4,128,256]{2,1,0:T(8,128)(2,1)S(1)}, u32[]{:S(2)}, u32[]{:S(2)}) collective-permute-start(bf16[4,128,256]{2,1,0:T(8,128)(2,1)} %get-tuple-element.14), channel_id=1, source_target_pairs={{16,0},{32,16},{48,32},{64,48},{80,64},{96,80},{112,96},{128,112},... | collective-permute-start | bytes 786440 | tf_op jit(solution)/shard_map/ppermute | solution.py:230
  31.9 33.7 %collective-permute-start.2 = (bf16[4,128,256]{2,1,0:T(8,128)(2,1)}, bf16[4,128,256]{2,1,0:T(8,128)(2,1)S(1)}, u32[]{:S(2)}, u32[]{:S(2)}) collective-permute-start(bf16[4,128,256]{2,1,0:T(8,128)(2,1)} %get-tuple-element.15), channel_id=1, source_target_pairs={{0,1},{1,2},{2,3},{3,4},{4,5},{5,6},{6,7},{7,8},{8,9},{9,10},{10,1... | collective-permute-start | bytes 786440 | tf_op jit(solution)/shard_map/ppermute | solution.py:230
  35.3 30.3 %collective-permute-start.3 = (bf16[4,128,256]{2,1,0:T(8,128)(2,1)}, bf16[4,128,256]{2,1,0:T(8,128)(2,1)S(1)}, u32[]{:S(2)}, u32[]{:S(2)}) collective-permute-start(bf16[4,128,256]{2,1,0:T(8,128)(2,1)} %get-tuple-element.16), channel_id=1, source_target_pairs={{1,0},{2,1},{3,2},{4,3},{5,4},{6,5},{7,6},{8,7},{9,8},{10,9},{11,1... | collective-permute-start | bytes 786440 | tf_op jit(solution)/shard_map/ppermute | solution.py:230
  37.9 16.1 %all-to-all-start.1 = ((bf16[8,32,256]{2,1,0:T(8,128)(2,1)}), bf16[8,32,256]{2,1,0:T(8,128)(2,1)S(1)}, u32[]{:S(2)}, u32[]{:S(2)}) async-start(bf16[8,32,256]{2,1,0:T(8,128)(2,1)} %broadcast_in_dim.24), calls=%async_computation.1 | async-start | bytes 262144 | tf_op jit(solution)/shard_map/all_to_all | solution.py:207
  54.9 21.5 %all-to-all-start.2 = ((bf16[32,32,256]{2,1,0:T(8,128)(2,1)}), bf16[32,32,256]{2,1,0:T(8,128)(2,1)S(1)}, u32[]{:S(2)}, u32[]{:S(2)}) async-start(bf16[32,32,256]{2,1,0:T(8,128)(2,1)} %broadcast_in_dim.25), calls=%async_computation.2 | async-start | bytes 1048576 | tf_op jit(solution)/shard_map/all_to_all | solution.py:207

commit v4 on v3

--- a/solution.py
+++ b/solution.py
@@ -36,9 +36,9 @@
 
 
 def step_kernel(
-    index_ref, label_ref, features, local_mask, halo_mask, halo_first, halo_second, halo_third,
+    core_ref, index_ref, label_ref, features, local_mask, halo_mask, halo_first, halo_second, halo_third,
     return_second, return_third, weight_first, weight_second, weight_third,
-    packed_out, above_out, below_out, left_out, right_out,
+    keep_out, send_out, above_out, below_out, left_out, right_out,
     feat_t, local_raw, halo_raw, first_t, second, third, ret_two, ret_three, w_one, w_two, w_three,
     local, halo, hits, inverse, mixed_one, mixed_two, mixed_three, pre_one, pre_two,
     hidden_one, hidden_two, scaled, packed, sends, feat, first, in_sem, local_sem, halo_sem, out_sem,
@@ -139,19 +139,26 @@
     got_ret_three.wait()
     got_ret_two.wait()
     two = w_two.shape[0]
-    three = w_three.shape[0]
     third_at = two + padded_up(wide)
     tail = two + wide // 16 * 16
-    packed[pl.ds(tail, ROWS - tail), :] = jnp.zeros((ROWS - tail, packed.shape[1]), BF)
-    packed[pl.ds(third_at, three), :] = dot(up_three, mixed_three[...], (0, 0)).astype(BF)
+    half = packed.shape[2]
+    for h in range(2):
+        packed[h, pl.ds(tail, ROWS - tail), :] = jnp.zeros((ROWS - tail, half), BF)
+
+    def pack(row, grad):
+        for h in range(2):
+            packed[h, pl.ds(row, grad.shape[0]), :] = grad[:, h * half : (h + 1) * half].astype(BF)
+
+    pack(third_at, dot(up_three, mixed_three[...], (0, 0)))
     carried = retract(dot(up_three, w_three[...]), ret_three)
     place(dot(halo[...], scaled[...], (0, 0)), 3)
     up_two = (carried * slope(pre_two[...])).astype(BF)
-    packed[pl.ds(0, two), :] = dot(mixed_two[...], up_two, (0, 0)).astype(BF)
+    pack(0, dot(mixed_two[...], up_two, (0, 0)))
     carried = retract(dot(up_two, w_two[...], (1, 1)), ret_two)
     up_one = (carried * slope(pre_one[...])).astype(BF)
-    packed[pl.ds(two, wide), :] = dot(mixed_one[...], up_one, (0, 0)).astype(BF)
-    out = [fetch(packed, packed_out, out_sem.at[4])]
+    pack(two, dot(mixed_one[...], up_one, (0, 0)))
+    core = core_ref[0]
+    out = [fetch(packed.at[1 - core], send_out, out_sem.at[4]), fetch(packed.at[core], keep_out, out_sem.at[5])]
     place(dot(halo[...], scaled[...], (0, 0)), 2)
     place(dot(hits[...], hidden_one[...], (0, 0)), 0)
     place(dot(hits[...], hidden_two[...], (0, 0)), 1)
@@ -160,7 +167,7 @@
         copy.wait()
 
 
-def step(index, labels, *arrays):
+def step(core, index, labels, *arrays):
     (features, _, _, _, halo_second, _,
      _, _, _, _, _) = arrays
     depth, nodes = features.shape
@@ -173,25 +180,56 @@
         v((nodes, wide), BF), v((nodes, hidden), BF), v((nodes, hidden), BF),
         v((nodes, hidden), F32), v((nodes, hidden), F32),
         v((nodes, hidden), BF), v((nodes, hidden), BF), v((nodes, hidden), BF),
-        v((ROWS, hidden), BF), v((4, 4, slots // 4, hidden), BF),
+        v((2, ROWS, hidden // 2), BF), v((4, 4, slots // 4, hidden), BF),
         v((nodes, wide), BF), v((slots, wide), BF),
         pltpu.SemaphoreType.DMA((9,)), pltpu.SemaphoreType.DMA((CHUNKS,)),
-        pltpu.SemaphoreType.DMA((CHUNKS,)), pltpu.SemaphoreType.DMA((5,)),
+        pltpu.SemaphoreType.DMA((CHUNKS,)), pltpu.SemaphoreType.DMA((6,)),
     ]
-    block = jax.ShapeDtypeStruct((4, slots // 4, hidden), BF)
+    block = v((4, slots // 4, hidden), BF)
     return pl.pallas_call(
         step_kernel,
-        out_shape=[jax.ShapeDtypeStruct((ROWS, hidden), BF)] + [block] * 4,
-        in_specs=[pl.BlockSpec(memory_space=pltpu.VMEM)] * 2 + [pl.BlockSpec(memory_space=pltpu.HBM)] * len(arrays),
-        out_specs=[pl.BlockSpec(memory_space=pl.ANY)] * 5,
+        out_shape=[pltpu.VMEM((ROWS, hidden // 2), BF)] * 2 + [block] * 4,
+        in_specs=[pl.BlockSpec(memory_space=pltpu.SMEM)]
+        + [pl.BlockSpec(memory_space=pltpu.VMEM)] * 2
+        + [pl.BlockSpec(memory_space=pltpu.HBM)] * len(arrays),
+        out_specs=[pl.BlockSpec(memory_space=pl.ANY)] * 6,
         scratch_shapes=scratch,
-        compiler_params=pltpu.CompilerParams(vmem_limit_bytes=66_000_000),
+        compiler_params=pltpu.CompilerParams(vmem_limit_bytes=62_000_000),
         cost_estimate=pl.CostEstimate(flops=8_000_000_000, bytes_accessed=12_000_000, transcendentals=1_000_000),
         name="step",
-    )(index, labels, *arrays)
-
-
-GROUP = ("row_1", "col_0", "col_1")
+    )(core, index, labels, *arrays)
+
+
+def unpack_kernel(core_ref, mine, other, one_out, two_out, three_out):
+    own_left = core_ref[0] == 0
+    half = mine.shape[1]
+
+    def rows_of(row, count):
+        a, b = mine[pl.ds(row, count), :].astype(F32), other[pl.ds(row, count), :].astype(F32)
+        return jnp.where(own_left, a, b), jnp.where(own_left, b, a)
+
+    row = 0
+    for out in (two_out, one_out, three_out):
+        for h, part in enumerate(rows_of(row, out.shape[0])):
+            out[:, h * half : (h + 1) * half] = part
+        row += out.shape[0] if out is two_out else padded_up(out.shape[0])
+
+
+def unpack(core, mine, other, one, two, three):
+    wide = mine.shape[1] * 2
+    return pl.pallas_call(
+        unpack_kernel,
+        out_shape=[jax.ShapeDtypeStruct((n, wide), F32) for n in (one, two, three)],
+        in_specs=[pl.BlockSpec(memory_space=pltpu.SMEM)] + [pl.BlockSpec(memory_space=pltpu.VMEM)] * 2,
+        out_specs=[pl.BlockSpec(memory_space=pltpu.VMEM)] * 3,
+        cost_estimate=pl.CostEstimate(flops=1_000_000, bytes_accessed=1_500_000, transcendentals=0),
+        compiler_params=pltpu.CompilerParams(vmem_limit_bytes=8 * 2**20),
+        name="unpack",
+    )(core, mine, other)
+
+
+PAIR = "row_1"
+GROUP = COL
 FAR = ("row_0",)
 
 
@@ -211,17 +249,29 @@
     return jnp.sum(pieces.astype(jnp.float32), axis=0).astype(jnp.bfloat16)
 
 
-def total_of(packed, lateral, vertical):
+def swapped(half):
+    return lax.ppermute(half, PAIR, [(0, 1), (1, 0)])
+
+
+def joined(got):
+    return [jnp.concatenate([g[n] for g in got], axis=0)[None, None] for n in range(4)]
+
+
+def total_of(keep, send, beside_in, beside_far):
     size = shares(GROUP)
-    pieces = packed.reshape(size, packed.shape[0] // size, packed.shape[1])
+    other = swapped(send)
+    own = (keep.astype(F32) + other.astype(F32)).astype(BF)
+    pieces = own.reshape(size, own.shape[0] // size, own.shape[1])
     own = lax.all_to_all(pieces, GROUP, 0, 0, tiled=True)
-    first = lateral()
+    first = beside_in()
     own = summed(own)
     own = copies(own, FAR)
+    last = beside_far()
     own = summed(own)
-    whole = copies(own, GROUP)
-    last = vertical()
-    return whole.reshape(packed.shape), first, last
+    mine = copies(own, GROUP).reshape(keep.shape)
+    mine, *outs = lax.optimization_barrier((mine, *joined(first + last)))
+    other = swapped(mine)
+    return mine, other, outs
 
 
 def shifted(block, axis, step):
@@ -245,7 +295,9 @@
     weight_second,
     weight_third,
 ):
-    packed, *blocks = step(
+    core = lax.axis_index(PAIR).astype(jnp.int32).reshape(1)
+    keep, send, *blocks = step(
+        core,
         boundary_index[0],
         labels[0],
         features[0, 0].T,
@@ -262,23 +314,17 @@
     )
     above, below, left, right = blocks
 
-    def lateral():
-        return [shifted(right, COL, 1), shifted(left, COL, -1)]
-
-    def vertical():
-        return [shifted(below, ROW, 1), shifted(above, ROW, -1)]
+    def beside_in():
+        return [shifted(below, ROW, 1), shifted(above, ROW, -1), shifted(right, COL, 1)]
+
+    def beside_far():
+        return [shifted(left, COL, -1)]
 
     one, two, three = weight_first.shape[0], weight_second.shape[0], weight_third.shape[1]
-    third_at = two + padded_up(one)
-    total, lateral_got, vertical_got = total_of(packed, lateral, vertical)
-    got = vertical_got + lateral_got
-    next_second, next_third, back_second, back_third = [
-        jnp.concatenate([g[n] for g in got], axis=0)[None, None] for n in range(4)
-    ]
-    total = total.astype(jnp.float32)
-    grad_two = total[:two]
-    grad_one = total[two : two + one]
-    grad_three = total[third_at : third_at + three].T
+    mine, other, outs = total_of(keep, send, beside_in, beside_far)
+    next_second, next_third, back_second, back_third = outs
+    grad_one, grad_two, grad_three = unpack(core, mine, other, one, two, three)
+    grad_three = grad_three.T
     return (grad_one, grad_two, grad_three, next_second, next_third, back_second, back_third)
 
 

time: 79.4 us -> 81.4 us (1.025)
  waiting for transfers between devices: 17.6 us -> 22.9 us
  local copies, waits for them, and re-layouts: 3.82 us -> 1.51 us
  starting transfers between devices: 37.7 us -> 35.8 us
    ppermute x0 -> x2, starting transfers between devices: none -> 9.82 us  [swapped(): return lax.ppermute(half, PAIR, [(0, 1), (1, 0)])]
    all_to_all x2, starting transfers between devices: 18.8 us -> 10.3 us  [copies(): lax.all_to_all(jnp.broadcast_to(piece[None], (size, *piece.shape)), axes,...]
    all_to_all x1, waiting for transfers between devices: 0.52 us -> 8.18 us  [total_of(): own = lax.all_to_all(pieces, GROUP, 0, 0, tiled=True)]
    all_to_all x2, waiting for transfers between devices: 17.1 us -> 13.6 us  [copies(): lax.all_to_all(jnp.broadcast_to(piece[None], (size, *piece.shape)), axes,...]
    ppermute x4, starting transfers between devices: 10.3 us -> 8.14 us  [shifted(): return lax.ppermute(block, axis, pairs)]
    slice x2 -> x0, local copies, waits for them, and re-layouts: 1.59 us -> none  [the longest x1 0.87 us: per_device(): grad_one = total[two:two + one]]
    ppermute x0 -> x2, waiting for transfers between devices: none -> 1.16 us  [swapped(): return lax.ppermute(half, PAIR, [(0, 1), (1, 0)])]
    all_to_all x1, starting transfers between devices: 8.6 us -> 7.53 us  [total_of(): own = lax.all_to_all(pieces, GROUP, 0, 0, tiled=True)]
  transfers between devices with their start and end apart: 7 -> 9, of which waited for: 3 -> 4; matrix products, arithmetic and copies ran while one was open for 4% -> 4% of each run, Pallas kernels for 0% -> 0%
where the time goes in v4:
time: 81.4 us; the launch traced here: 80.8 us
  starting transfers between devices  35.8 us (44%)
  waiting for transfers between devices  22.9 us (28%)
  Pallas kernels  17.3 us (21%)
  other arithmetic  2.49 us (3%)
  local copies, waits for them, and re-layouts  1.51 us (2%)
    pallas_call x1, Pallas kernels, step(): pl.pallas_call(step_kernel, out_shape=[pltpu.VMEM((ROWS, hidden // 2), BF...  16.3 us
    all_to_all x2, waiting for transfers between devices, copies(): lax.all_to_all(jnp.broadcast_to(piece[None], (size, *piece.shape)), axes,...  13.6 us
    all_to_all x2, starting transfers between devices, copies(): lax.all_to_all(jnp.broadcast_to(piece[None], (size, *piece.shape)), axes,...  10.3 us
    ppermute x2, starting transfers between devices, swapped(): return lax.ppermute(half, PAIR, [(0, 1), (1, 0)])  9.82 us
    all_to_all x1, waiting for transfers between devices, total_of(): own = lax.all_to_all(pieces, GROUP, 0, 0, tiled=True)  8.18 us
    ppermute x4, starting transfers between devices, shifted(): return lax.ppermute(block, axis, pairs)  8.14 us
    all_to_all x1, starting transfers between devices, total_of(): own = lax.all_to_all(pieces, GROUP, 0, 0, tiled=True)  7.53 us
    broadcast_in_dim x2, other arithmetic, joined(): jnp.concatenate([g[n] for g in got], axis=0)[None, None]  1.65 us
  transfers between devices with their start and end apart: 9, of which 4 were waited for; matrix products, arithmetic and copies ran while one was open for 4% of the time, Pallas kernels for 0%

profile of v4, /device:TPU:1, one launch (start us, length us, event | category | flops | bytes accessed | tf_op | source)
XLA Modules:
  0.0 80.8 jit_solution(17686268270613655924)
XLA Ops:
  0.6 16.3 %step.1 = (bf16[1024,128]{1,0:T(8,128)(2,1)S(1)}, bf16[1024,128]{1,0:T(8,128)(2,1)S(1)}, bf16[4,128,256]{2,1,0:T(8,128)(2,1)S(1)}, bf16[4,128,256]{2,1,0:T(8,128...) custom-call(s32[1]{0:T(128)} %bitcast.core_ref, s32[1,512]{1,0:T(1,128)} %bitcast.72, ...), custom_call_target="tpu_custom_call" | custom-call | flops 8000000000 | bytes 12000000 | tf_op jit(solution)/shard_map/step/pallas_call | solution.py:189
  17.0 3.3 %collective-permute-start = (bf16[1024,128]{1,0:T(8,128)(2,1)S(1)}, bf16[1024,128]{1,0:T(8,128)(2,1)S(1)}, u32[]{:S(2)}, u32[]{:S(2)}) collective-permute-start(bf16[1024,128]{1,0:T(8,128)(2,1)S(1)} %get-tuple-element.22), channel_id=1, source_target_pairs={{0,16},{16,0},{1,17},{17,1},{2,18},{18,2},{3,19},{19,3},{4,20},{20... | collective-permute-start | bytes 786440 | tf_op jit(solution)/shard_map/ppermute | solution.py:253
  20.3 1.9 %collective-permute-start.1 = (bf16[4,128,256]{2,1,0:T(8,128)(2,1)S(1)}, bf16[4,128,256]{2,1,0:T(8,128)(2,1)S(1)}, u32[]{:S(2)}, u32[]{:S(2)}) collective-permute-start(bf16[4,128,256]{2,1,0:T(8,128)(2,1)S(1)} %get-tuple-element.23), channel_id=1, source_target_pairs={{0,16},{16,32},{32,48},{48,64},{64,80},{80,96},{96,112},{112,128},... | collective-permute-start | bytes 786440 | tf_op jit(solution)/shard_map/ppermute | solution.py:280
  22.2 2.4 %collective-permute-start.2 = (bf16[4,128,256]{2,1,0:T(8,128)(2,1)S(1)}, bf16[4,128,256]{2,1,0:T(8,128)(2,1)S(1)}, u32[]{:S(2)}, u32[]{:S(2)}) collective-permute-start(bf16[4,128,256]{2,1,0:T(8,128)(2,1)S(1)} %get-tuple-element.24), channel_id=1, source_target_pairs={{16,0},{32,16},{48,32},{64,48},{80,64},{96,80},{112,96},{128,112},... | collective-permute-start | bytes 786440 | tf_op jit(solution)/shard_map/ppermute | solution.py:280
  24.6 2.5 %collective-permute-start.3 = (bf16[4,128,256]{2,1,0:T(8,128)(2,1)S(1)}, bf16[4,128,256]{2,1,0:T(8,128)(2,1)S(1)}, u32[]{:S(2)}, u32[]{:S(2)}) collective-permute-start(bf16[4,128,256]{2,1,0:T(8,128)(2,1)S(1)} %get-tuple-element.25), channel_id=1, source_target_pairs={{0,1},{1,2},{2,3},{3,4},{4,5},{5,6},{6,7},{7,8},{8,9},{9,10},{10,1... | collective-permute-start | bytes 786440 | tf_op jit(solution)/shard_map/ppermute | solution.py:280
  27.1 1.3 %collective-permute-start.4 = (bf16[4,128,256]{2,1,0:T(8,128)(2,1)S(1)}, bf16[4,128,256]{2,1,0:T(8,128)(2,1)S(1)}, u32[]{:S(2)}, u32[]{:S(2)}) collective-permute-start(bf16[4,128,256]{2,1,0:T(8,128)(2,1)S(1)} %get-tuple-element.26), channel_id=1, source_target_pairs={{1,0},{2,1},{3,2},{4,3},{5,4},{6,5},{7,6},{8,7},{9,8},{10,9},{11,1... | collective-permute-start | bytes 786440 | tf_op jit(solution)/shard_map/ppermute | solution.py:280
  28.4 0.0 collective-permute-done
  28.5 0.8 add_convert_fusion
  29.2 7.5 %all-to-all-start = ((bf16[16,64,128]{2,1,0:T(8,128)(2,1)}), bf16[16,64,128]{2,1,0:T(8,128)(2,1)S(1)}, u32[]{:S(2)}, u32[]{:S(2)}) async-start(bf16[16,64,128]{2,1,0:T(8,128)(2,1)} %bitcast.14), calls=%async_computation | async-start | bytes 524288 | tf_op jit(solution)/shard_map/all_to_all | solution.py:265
  36.8 0.0 collective-permute-done.1
  36.8 0.0 collective-permute-done.2
  36.8 0.0 collective-permute-done.3
  36.9 8.2 %all-to-all-done = bf16[16,64,128]{2,1,0:T(8,128)(2,1)S(1)} async-done(((bf16[16,64,128]{2,1,0:T(8,128)(2,1)}), bf16[16,64,128]{2,1,0:T(8,128)(2,1)S(1)}, u32[]{:S(2)}, u32[]{:S(2)}) %all-to-all-start) | async-done | bytes 262176 | tf_op jit(solution)/shard_map/all_to_all | solution.py:265
  45.1 0.7 broadcast_in_dim.24
  45.8 6.5 %all-to-all-start.1 = ((bf16[8,64,128]{2,1,0:T(8,128)(2,1)}), bf16[8,64,128]{2,1,0:T(8,128)(2,1)S(1)}, u32[]{:S(2)}, u32[]{:S(2)}) async-start(bf16[8,64,128]{2,1,0:T(8,128)(2,1)} %broadcast_in_dim.24), calls=%async_computation.1 | async-start | bytes 262144 | tf_op jit(solution)/shard_map/all_to_all | solution.py:245
  52.3 0.0 collective-permute-done.4
  52.3 7.9 %all-to-all-done.1 = bf16[8,64,128]{2,1,0:T(8,128)(2,1)S(1)} async-done(((bf16[8,64,128]{2,1,0:T(8,128)(2,1)}), bf16[8,64,128]{2,1,0:T(8,128)(2,1)S(1)}, u32[]{:S(2)}, u32[]{:S(2)}) %all-to-all-start.1) | async-done | bytes 131104 | tf_op jit(solution)/shard_map/all_to_all | solution.py:245
  60.3 0.8 broadcast_in_dim.25
  61.0 3.8 %all-to-all-start.2 = ((bf16[16,64,128]{2,1,0:T(8,128)(2,1)}), bf16[16,64,128]{2,1,0:T(8,128)(2,1)S(1)}, u32[]{:S(2)}, u32[]{:S(2)}) async-start(bf16[16,64,128]{2,1,0:T(8,128)(2,1)} %broadcast_in_dim.25), calls=%async_computation.2 | async-start | bytes 524288 | tf_op jit(solution)/shard_map/all_to_all | solution.py:245
  64.8 0.8 %maximum_bitcast_fusion.2 = (bf16[1,1,512,256]{3,2,1,0:T(8,128)(2,1)}, bf16[1,1,512,256]{3,2,1,0:T(8,128)(2,1)}) fusion(bf16[128,256]{1,0:T(8,128)(2,1)S(1)} %get-tuple-element.48, bf16[128,256]{1,0:T(8,128)(2,1)S(1)} %get-tuple-element.44, bf16[128,256]{1,0:T(8,128)(2,1)S(1)} %get-tuple-element.40, bf16[128,256]{1,0:T(8,128)(2,1)S(1)} %get-tuple-element.36, ...), kind=kLoop, calls=%fused_computation.3 | loop fusion | flops 2097152 | bytes 1048576 | tf_op jit(solution)/shard_map/broadcast_in_dim | solution.py:257
  65.7 0.8 %maximum_bitcast_fusion = (bf16[1,1,512,256]{3,2,1,0:T(8,128)(2,1)}, bf16[1,1,512,256]{3,2,1,0:T(8,128)(2,1)}) fusion(bf16[128,256]{1,0:T(8,128)(2,1)S(1)} %get-tuple-element.50, bf16[128,256]{1,0:T(8,128)(2,1)S(1)} %get-tuple-element.46, bf16[128,256]{1,0:T(8,128)(2,1)S(1)} %get-tuple-element.42, bf16[128,256]{1,0:T(8,128)(2,1)S(1)} %get-tuple-element.38, ...), kind=kLoop, calls=%fused_computation.1 | loop fusion | flops 2097152 | bytes 1048576 | tf_op jit(solution)/shard_map/broadcast_in_dim | solution.py:257
  66.5 5.7 %all-to-all-done.2 = bf16[16,64,128]{2,1,0:T(8,128)(2,1)S(1)} async-done(((bf16[16,64,128]{2,1,0:T(8,128)(2,1)}), bf16[16,64,128]{2,1,0:T(8,128)(2,1)S(1)}, u32[]{:S(2)}, u32[]{:S(2)}) %all-to-all-start.2) | async-done | bytes 262176 | tf_op jit(solution)/shard_map/all_to_all | solution.py:245
  72.2 6.5 %collective-permute-start.5 = (bf16[1024,128]{1,0:T(8,128)(2,1)S(1)}, bf16[1024,128]{1,0:T(8,128)(2,1)S(1)}, u32[]{:S(2)}, u32[]{:S(2)}) collective-permute-start(bf16[1024,128]{1,0:T(8,128)(2,1)S(1)} %bitcast.59), channel_id=1, source_target_pairs={{0,16},{16,0},{1,17},{17,1},{2,18},{18,2},{3,19},{19,3},{4,20},{20... | collective-permute-start | bytes 786440 | tf_op jit(solution)/shard_map/ppermute | solution.py:253
  78.7 1.2 %collective-permute-done.5.other = bf16[1024,128]{1,0:T(8,128)(2,1)S(1)} collective-permute-done((bf16[1024,128]{1,0:T(8,128)(2,1)S(1)}, bf16[1024,128]{1,0:T(8,128)(2,1)S(1)}, u32[]{:S(2)}, u32[]{:S(2)}) %collective-permute-start.5) | collective-permute-done | bytes 262176 | tf_op jit(solution)/shard_map/ppermute | solution.py:253
  79.9 0.9 %unpack.1 = (f32[602,256]{1,0:T(8,128)}, f32[256,256]{1,0:T(8,128)}, f32[41,256]{1,0:T(8,128)}) custom-call(s32[1]{0:T(128)} %bitcast.core_ref, bf16[1024,128]{1,0:T(8,128)(2,1)S(1)} %bitcast.60, bf16[1024,128]{1,0:T(8,128)(2,1)S(1)} %collective-permute-done.5.other), custom_call_target="tpu_custom_call" | custom-call | flops 1000000 | bytes 1500000 | tf_op jit(solution)/shard_map/unpack/pallas_call | solution.py:220
  (6 shorter events, 0.1 us)
Async XLA Ops:
  17.0 11.5 %collective-permute-start = (bf16[1024,128]{1,0:T(8,128)(2,1)S(1)}, bf16[1024,128]{1,0:T(8,128)(2,1)S(1)}, u32[]{:S(2)}, u32[]{:S(2)}) collective-permute-start(bf16[1024,128]{1,0:T(8,128)(2,1)S(1)} %get-tuple-element.22), channel_id=1, source_target_pairs={{0,16},{16,0},{1,17},{17,1},{2,18},{18,2},{3,19},{19,3},{4,20},{20... | collective-permute-start | bytes 786440 | tf_op jit(solution)/shard_map/ppermute | solution.py:253
  20.3 16.5 %collective-permute-start.1 = (bf16[4,128,256]{2,1,0:T(8,128)(2,1)S(1)}, bf16[4,128,256]{2,1,0:T(8,128)(2,1)S(1)}, u32[]{:S(2)}, u32[]{:S(2)}) collective-permute-start(bf16[4,128,256]{2,1,0:T(8,128)(2,1)S(1)} %get-tuple-element.23), channel_id=1, source_target_pairs={{0,16},{16,32},{32,48},{48,64},{64,80},{80,96},{96,112},{112,128},... | collective-permute-start | bytes 786440 | tf_op jit(solution)/shard_map/ppermute | solution.py:280
  22.2 14.6 %collective-permute-start.2 = (bf16[4,128,256]{2,1,0:T(8,128)(2,1)S(1)}, bf16[4,128,256]{2,1,0:T(8,128)(2,1)S(1)}, u32[]{:S(2)}, u32[]{:S(2)}) collective-permute-start(bf16[4,128,256]{2,1,0:T(8,128)(2,1)S(1)} %get-tuple-element.24), channel_id=1, source_target_pairs={{16,0},{32,16},{48,32},{64,48},{80,64},{96,80},{112,96},{128,112},... | collective-permute-start | bytes 786440 | tf_op jit(solution)/shard_map/ppermute | solution.py:280
  24.6 12.2 %collective-permute-start.3 = (bf16[4,128,256]{2,1,0:T(8,128)(2,1)S(1)}, bf16[4,128,256]{2,1,0:T(8,128)(2,1)S(1)}, u32[]{:S(2)}, u32[]{:S(2)}) collective-permute-start(bf16[4,128,256]{2,1,0:T(8,128)(2,1)S(1)} %get-tuple-element.25), channel_id=1, source_target_pairs={{0,1},{1,2},{2,3},{3,4},{4,5},{5,6},{6,7},{7,8},{8,9},{9,10},{10,1... | collective-permute-start | bytes 786440 | tf_op jit(solution)/shard_map/ppermute | solution.py:280
  27.1 25.2 %collective-permute-start.4 = (bf16[4,128,256]{2,1,0:T(8,128)(2,1)S(1)}, bf16[4,128,256]{2,1,0:T(8,128)(2,1)S(1)}, u32[]{:S(2)}, u32[]{:S(2)}) collective-permute-start(bf16[4,128,256]{2,1,0:T(8,128)(2,1)S(1)} %get-tuple-element.26), channel_id=1, source_target_pairs={{1,0},{2,1},{3,2},{4,3},{5,4},{6,5},{7,6},{8,7},{9,8},{10,9},{11,1... | collective-permute-start | bytes 786440 | tf_op jit(solution)/shard_map/ppermute | solution.py:280
  29.2 15.8 %all-to-all-start = ((bf16[16,64,128]{2,1,0:T(8,128)(2,1)}), bf16[16,64,128]{2,1,0:T(8,128)(2,1)S(1)}, u32[]{:S(2)}, u32[]{:S(2)}) async-start(bf16[16,64,128]{2,1,0:T(8,128)(2,1)} %bitcast.14), calls=%async_computation | async-start | bytes 524288 | tf_op jit(solution)/shard_map/all_to_all | solution.py:265
  45.8 14.4 %all-to-all-start.1 = ((bf16[8,64,128]{2,1,0:T(8,128)(2,1)}), bf16[8,64,128]{2,1,0:T(8,128)(2,1)S(1)}, u32[]{:S(2)}, u32[]{:S(2)}) async-start(bf16[8,64,128]{2,1,0:T(8,128)(2,1)} %broadcast_in_dim.24), calls=%async_computation.1 | async-start | bytes 262144 | tf_op jit(solution)/shard_map/all_to_all | solution.py:245
  61.0 11.2 %all-to-all-start.2 = ((bf16[16,64,128]{2,1,0:T(8,128)(2,1)}), bf16[16,64,128]{2,1,0:T(8,128)(2,1)S(1)}, u32[]{:S(2)}, u32[]{:S(2)}) async-start(bf16[16,64,128]{2,1,0:T(8,128)(2,1)} %broadcast_in_dim.25), calls=%async_computation.2 | async-start | bytes 524288 | tf_op jit(solution)/shard_map/all_to_all | solution.py:245
  72.2 7.7 %collective-permute-start.5 = (bf16[1024,128]{1,0:T(8,128)(2,1)S(1)}, bf16[1024,128]{1,0:T(8,128)(2,1)S(1)}, u32[]{:S(2)}, u32[]{:S(2)}) collective-permute-start(bf16[1024,128]{1,0:T(8,128)(2,1)S(1)} %bitcast.59), channel_id=1, source_target_pairs={{0,16},{16,0},{1,17},{17,1},{2,18},{18,2},{3,19},{19,3},{4,20},{20... | collective-permute-start | bytes 786440 | tf_op jit(solution)/shard_map/ppermute | solution.py:253

commit v5 on v4

--- a/solution.py
+++ b/solution.py
@@ -38,10 +38,10 @@
 def step_kernel(
     core_ref, index_ref, label_ref, features, local_mask, halo_mask, halo_first, halo_second, halo_third,
     return_second, return_third, weight_first, weight_second, weight_third,
-    keep_out, send_out, above_out, below_out, left_out, right_out,
+    keep_out, pair_out, far_out, left_out, right_out,
     feat_t, local_raw, halo_raw, first_t, second, third, ret_two, ret_three, w_one, w_two, w_three,
     local, halo, hits, inverse, mixed_one, mixed_two, mixed_three, pre_one, pre_two,
-    hidden_one, hidden_two, scaled, packed, sends, feat, first, in_sem, local_sem, halo_sem, out_sem,
+    hidden_one, hidden_two, scaled, packed, upright, sends, feat, first, in_sem, local_sem, halo_sem, out_sem,
 ):
     nodes, wide = feat.shape
     rows = nodes // CHUNKS
@@ -125,11 +125,15 @@
     )[:, : logits.shape[1]]
     up_three = ((probs - target) / nodes).astype(BF)
 
-    out_refs = (above_out, below_out, left_out, right_out)
+    half = packed.shape[2]
 
     def place(array, n):
-        for k in range(4):
-            sends[k, n] = array[k * bound : (k + 1) * bound].astype(BF)
+        for k in range(2):
+            for h in range(2):
+                upright[k, pl.ds((2 * n + h) * bound, bound), :] = array[
+                    k * bound : (k + 1) * bound, h * half : (h + 1) * half
+                ].astype(BF)
+            sends[k, n] = array[(2 + k) * bound : (3 + k) * bound].astype(BF)
 
     def retract(across, returned):
         scaled[...] = (across * inverse[...]).astype(BF)
@@ -141,7 +145,6 @@
     two = w_two.shape[0]
     third_at = two + padded_up(wide)
     tail = two + wide // 16 * 16
-    half = packed.shape[2]
     for h in range(2):
         packed[h, pl.ds(tail, ROWS - tail), :] = jnp.zeros((ROWS - tail, half), BF)
 
@@ -158,11 +161,16 @@
     up_one = (carried * slope(pre_one[...])).astype(BF)
     pack(two, dot(mixed_one[...], up_one, (0, 0)))
     core = core_ref[0]
-    out = [fetch(packed.at[1 - core], send_out, out_sem.at[4]), fetch(packed.at[core], keep_out, out_sem.at[5])]
+    out = [fetch(packed.at[1 - core], pair_out.at[0], out_sem.at[4]), fetch(packed.at[core], keep_out, out_sem.at[5])]
     place(dot(halo[...], scaled[...], (0, 0)), 2)
     place(dot(hits[...], hidden_one[...], (0, 0)), 0)
     place(dot(hits[...], hidden_two[...], (0, 0)), 1)
-    out += [fetch(sends.at[k], out_refs[k], out_sem.at[k]) for k in range(4)]
+    out += [
+        fetch(upright.at[1 - core], pair_out.at[1], out_sem.at[0]),
+        fetch(upright.at[core], far_out, out_sem.at[1]),
+        fetch(sends.at[0], left_out, out_sem.at[2]),
+        fetch(sends.at[1], right_out, out_sem.at[3]),
+    ]
     for copy in out:
         copy.wait()
 
@@ -180,19 +188,21 @@
         v((nodes, wide), BF), v((nodes, hidden), BF), v((nodes, hidden), BF),
         v((nodes, hidden), F32), v((nodes, hidden), F32),
         v((nodes, hidden), BF), v((nodes, hidden), BF), v((nodes, hidden), BF),
-        v((2, ROWS, hidden // 2), BF), v((4, 4, slots // 4, hidden), BF),
+        v((2, ROWS, hidden // 2), BF), v((2, 2 * slots, hidden // 2), BF),
+        v((2, 4, slots // 4, hidden), BF),
         v((nodes, wide), BF), v((slots, wide), BF),
         pltpu.SemaphoreType.DMA((9,)), pltpu.SemaphoreType.DMA((CHUNKS,)),
         pltpu.SemaphoreType.DMA((CHUNKS,)), pltpu.SemaphoreType.DMA((6,)),
     ]
+    half = v((ROWS, hidden // 2), BF)
     block = v((4, slots // 4, hidden), BF)
     return pl.pallas_call(
         step_kernel,
-        out_shape=[pltpu.VMEM((ROWS, hidden // 2), BF)] * 2 + [block] * 4,
+        out_shape=[half, v((2, ROWS, hidden // 2), BF), half, block, block],
         in_specs=[pl.BlockSpec(memory_space=pltpu.SMEM)]
         + [pl.BlockSpec(memory_space=pltpu.VMEM)] * 2
         + [pl.BlockSpec(memory_space=pltpu.HBM)] * len(arrays),
-        out_specs=[pl.BlockSpec(memory_space=pl.ANY)] * 6,
+        out_specs=[pl.BlockSpec(memory_space=pl.ANY)] * 5,
         scratch_shapes=scratch,
         compiler_params=pltpu.CompilerParams(vmem_limit_bytes=62_000_000),
         cost_estimate=pl.CostEstimate(flops=8_000_000_000, bytes_accessed=12_000_000, transcendentals=1_000_000),
@@ -200,6 +210,50 @@
     )(core, index, labels, *arrays)
 
 
+def small(kernel, out_shape, *arrays):
+    scalars = sum(a.ndim == 1 for a in arrays)
+    return pl.pallas_call(
+        kernel,
+        out_shape=out_shape,
+        in_specs=[pl.BlockSpec(memory_space=pltpu.SMEM)] * scalars
+        + [pl.BlockSpec(memory_space=pltpu.VMEM)] * (len(arrays) - scalars),
+        out_specs=jax.tree.map(lambda _: pl.BlockSpec(memory_space=pltpu.VMEM), out_shape),
+        compiler_params=pltpu.CompilerParams(vmem_limit_bytes=8 * 2**20),
+        cost_estimate=pl.CostEstimate(flops=500_000, bytes_accessed=1_000_000, transcendentals=0),
+    )(*arrays)
+
+
+def add_kernel(keep, pair, out):
+    out[...] = (keep[...].astype(F32) + pair[0].astype(F32)).astype(BF)
+
+
+def sum_kernel(pieces, out):
+    total = pieces[0].astype(F32)
+    for n in range(1, pieces.shape[0]):
+        total = total + pieces[n].astype(F32)
+    total = total.astype(BF)
+    for n in range(out.shape[0]):
+        out[n] = total
+
+
+def repeated_sum(pieces, count):
+    return small(sum_kernel, pltpu.VMEM((count, *pieces.shape[1:]), BF), pieces)
+
+
+def join_kernel(core_ref, pair, far, right, left, *outs):
+    upper = core_ref[0] == 0
+    bound, half = right.shape[1], pair.shape[2]
+    for n, out in enumerate(outs):
+        for h in range(2):
+            at = pl.ds((2 * n + h) * bound, bound)
+            cols = slice(h * half, (h + 1) * half)
+            near, away = pair[1, at, :], far[at, :]
+            out[0:bound, cols] = jnp.where(upper, away, near)
+            out[bound : 2 * bound, cols] = jnp.where(upper, near, away)
+        out[2 * bound : 3 * bound, :] = right[n]
+        out[3 * bound : 4 * bound, :] = left[n]
+
+
 def unpack_kernel(core_ref, mine, other, one_out, two_out, three_out):
     own_left = core_ref[0] == 0
     half = mine.shape[1]
@@ -217,15 +271,8 @@
 
 def unpack(core, mine, other, one, two, three):
     wide = mine.shape[1] * 2
-    return pl.pallas_call(
-        unpack_kernel,
-        out_shape=[jax.ShapeDtypeStruct((n, wide), F32) for n in (one, two, three)],
-        in_specs=[pl.BlockSpec(memory_space=pltpu.SMEM)] + [pl.BlockSpec(memory_space=pltpu.VMEM)] * 2,
-        out_specs=[pl.BlockSpec(memory_space=pltpu.VMEM)] * 3,
-        cost_estimate=pl.CostEstimate(flops=1_000_000, bytes_accessed=1_500_000, transcendentals=0),
-        compiler_params=pltpu.CompilerParams(vmem_limit_bytes=8 * 2**20),
-        name="unpack",
-    )(core, mine, other)
+    shapes = [jax.ShapeDtypeStruct((n, wide), F32) for n in (one, two, three)]
+    return small(unpack_kernel, shapes, core, mine, other)
 
 
 PAIR = "row_1"
@@ -240,44 +287,44 @@
     return size
 
 
-def copies(piece, axes):
-    size = shares(axes)
-    return lax.all_to_all(jnp.broadcast_to(piece[None], (size, *piece.shape)), axes, 0, 0, tiled=True)
-
-
-def summed(pieces):
-    return jnp.sum(pieces.astype(jnp.float32), axis=0).astype(jnp.bfloat16)
+def exchanged(pieces, axes):
+    return lax.all_to_all(pieces, axes, 0, 0, tiled=True)
 
 
 def swapped(half):
     return lax.ppermute(half, PAIR, [(0, 1), (1, 0)])
 
 
-def joined(got):
-    return [jnp.concatenate([g[n] for g in got], axis=0)[None, None] for n in range(4)]
-
-
-def total_of(keep, send, beside_in, beside_far):
+def total_of(core, keep, pair, beside_in, beside_far):
     size = shares(GROUP)
-    other = swapped(send)
-    own = (keep.astype(F32) + other.astype(F32)).astype(BF)
+    pair = swapped(pair)
+    own = small(add_kernel, pltpu.VMEM(keep.shape, BF), keep, pair)
     pieces = own.reshape(size, own.shape[0] // size, own.shape[1])
-    own = lax.all_to_all(pieces, GROUP, 0, 0, tiled=True)
-    first = beside_in()
-    own = summed(own)
-    own = copies(own, FAR)
-    last = beside_far()
-    own = summed(own)
-    mine = copies(own, GROUP).reshape(keep.shape)
-    mine, *outs = lax.optimization_barrier((mine, *joined(first + last)))
+    pieces = exchanged(pieces, GROUP)
+    far, right = beside_in()
+    own = repeated_sum(pieces, shares(FAR))
+    pieces = exchanged(own, FAR)
+    left = beside_far()
+    own = repeated_sum(pieces, size)
+    mine = exchanged(own, GROUP).reshape(keep.shape)
+    _, bound, half = right.shape
+    outs = [jax.ShapeDtypeStruct((4 * bound, half), BF)] * 4
+    outs = small(join_kernel, outs, core, pair, far, right, left)
+    mine, *outs = lax.optimization_barrier((mine, *outs))
     other = swapped(mine)
-    return mine, other, outs
+    return mine, other, [out[None, None] for out in outs]
 
 
 def shifted(block, axis, step):
     size = lax.axis_size(axis)
     pairs = [(i, i + step) for i in range(size) if 0 <= i + step < size]
     return lax.ppermute(block, axis, pairs)
+
+
+def across_chips(block):
+    size = lax.axis_size(ROW)
+    up = [(i, i + 1) for i in range(1, size - 1, 2)]
+    return lax.ppermute(block, ROW, up + [(j, i) for i, j in up])
 
 
 def per_device(
@@ -296,7 +343,7 @@
     weight_third,
 ):
     core = lax.axis_index(PAIR).astype(jnp.int32).reshape(1)
-    keep, send, *blocks = step(
+    keep, pair, far, left, right = step(
         core,
         boundary_index[0],
         labels[0],
@@ -312,16 +359,15 @@
         weight_second,
         weight_third.T,
     )
-    above, below, left, right = blocks
 
     def beside_in():
-        return [shifted(below, ROW, 1), shifted(above, ROW, -1), shifted(right, COL, 1)]
+        return across_chips(far), shifted(right, COL, 1)
 
     def beside_far():
-        return [shifted(left, COL, -1)]
+        return shifted(left, COL, -1)
 
     one, two, three = weight_first.shape[0], weight_second.shape[0], weight_third.shape[1]
-    mine, other, outs = total_of(keep, send, beside_in, beside_far)
+    mine, other, outs = total_of(core, keep, pair, beside_in, beside_far)
     next_second, next_third, back_second, back_third = outs
     grad_one, grad_two, grad_three = unpack(core, mine, other, one, two, three)
     grad_three = grad_three.T

time: 81.4 us -> 71.7 us (0.88)
  blocking collectives: 0 us -> 12.4 us
  waiting for transfers between devices: 22.9 us -> 10.8 us
  starting transfers between devices: 35.8 us -> 27.4 us
  Pallas kernels: 17.3 us -> 19.8 us
  other arithmetic: 2.49 us -> 0 us
  local copies, waits for them, and re-layouts: 1.51 us -> 0 us
    all_to_all x3 -> x2, waiting for transfers between devices: 21.7 us -> 8.11 us  [exchanged(): return lax.all_to_all(pieces, axes, 0, 0, tiled=True)]
    all_to_all x0 -> x1, blocking collectives: none -> 12.4 us  [exchanged(): return lax.all_to_all(pieces, axes, 0, 0, tiled=True)]
    ppermute x2, starting transfers between devices: 9.82 us -> 3.7 us  [swapped(): return lax.ppermute(half, PAIR, [(0, 1), (1, 0)])]
    ppermute x0 -> x1, starting transfers between devices: none -> 5.7 us  [across_chips(): return lax.ppermute(block, ROW, up + [(j, i) for i, j in up])]
    ppermute x4 -> x2, starting transfers between devices: 8.14 us -> 3.38 us  [shifted(): return lax.ppermute(block, axis, pairs)]
    all_to_all x3 -> x2, starting transfers between devices: 17.9 us -> 14.6 us  [exchanged(): return lax.all_to_all(pieces, axes, 0, 0, tiled=True)]
    pallas_call x2 -> x6, Pallas kernels: 17.3 us -> 19.8 us  [the longest x1 16.3 us: step(): pl.pallas_call(step_kernel, out_shape=[half, v((2, ROWS, hidden // 2), BF...]
    broadcast_in_dim x2 -> x0, other arithmetic: 1.65 us -> none  [joined(): jnp.concatenate([g[n] for g in got], axis=0)[None, None]]
  transfers between devices with their start and end apart: 9 -> 7, of which waited for: 4 -> 3; matrix products, arithmetic and copies ran while one was open for 4% -> 0% of each run, Pallas kernels for 0% -> 3%
where the time goes in v5:
time: 71.7 us; the launch traced here: 71.2 us
  starting transfers between devices  27.4 us (38%)
  Pallas kernels  19.8 us (28%)
  blocking collectives  12.4 us (17%)
  waiting for transfers between devices  10.8 us (15%)
  between operations  0.72 us (1%)
    pallas_call x1, Pallas kernels, step(): pl.pallas_call(step_kernel, out_shape=[half, v((2, ROWS, hidden // 2), BF...  16.3 us
    all_to_all x2, starting transfers between devices, exchanged(): return lax.all_to_all(pieces, axes, 0, 0, tiled=True)  14.6 us
    all_to_all x1, blocking collectives, exchanged(): return lax.all_to_all(pieces, axes, 0, 0, tiled=True)  12.4 us
    all_to_all x2, waiting for transfers between devices, exchanged(): return lax.all_to_all(pieces, axes, 0, 0, tiled=True)  8.11 us
    ppermute x1, starting transfers between devices, across_chips(): return lax.ppermute(block, ROW, up + [(j, i) for i, j in up])  5.7 us
    ppermute x2, starting transfers between devices, swapped(): return lax.ppermute(half, PAIR, [(0, 1), (1, 0)])  3.7 us
    pallas_call x5, Pallas kernels, small(): pl.pallas_call(kernel, out_shape=out_shape, in_specs=[pl.BlockSpec(memory...  3.53 us
    ppermute x2, starting transfers between devices, shifted(): return lax.ppermute(block, axis, pairs)  3.38 us
  transfers between devices with their start and end apart: 7, of which 3 were waited for; matrix products, arithmetic and copies ran while one was open for 0% of the time, Pallas kernels for 3%

profile of v5, /device:TPU:1, one launch (start us, length us, event | category | flops | bytes accessed | tf_op | source)
XLA Modules:
  0.0 71.2 jit_solution(6988979539447575308)
XLA Ops:
  0.6 16.3 %step.1 = (bf16[1024,128]{1,0:T(8,128)(2,1)S(1)}, bf16[2,1024,128]{2,1,0:T(8,128)(2,1)S(1)}, bf16[1024,128]{1,0:T(8,128)(2,1)S(1)}, bf16[4,128,256]{2,1,0:T(8,128)(2,1)S(1)}, bf16[4,128,256]{2,1,0:T(8,128)(2,1)S(1)}) custom-call(s32[1]{0:T(128)} %bitcast.core_ref, s32[1,512]{1,0:T(1,128)} %bitcast.41, s32[1,1024]{1,0:T(1,128)} %bitcast.40, ...), custom_call_target="tpu_custom_call" | custom-call | flops 8000000000 | bytes 12000000 | tf_op jit(solution)/shard_map/step/pallas_call | solution.py:199
  17.0 3.3 %collective-permute-start = (bf16[2,1024,128]{2,1,0:T(8,128)(2,1)S(1)}, bf16[2,1024,128]{2,1,0:T(8,128)(2,1)S(1)}, u32[]{:S(2)}, u32[]{:S(2)}) collective-permute-start(bf16[2,1024,128]{2,1,0:T(8,128)(2,1)S(1)} %get-tuple-element.25), channel_id=1, source_target_pairs={{0,16},{16,0},{1,17},{17,1},{2,18},{18,2},{3,19},{19,3},{4,20},{20... | collective-permute-start | bytes 1572872 | tf_op jit(solution)/shard_map/ppermute | solution.py:295
  20.3 1.5 %collective-permute-done.pair = bf16[2,1024,128]{2,1,0:T(8,128)(2,1)S(1)} collective-permute-done((bf16[2,1024,128]{2,1,0:T(8,128)(2,1)S(1)}, bf16[2,1024,128]{2,1,0:T(8,128)(2,1)S(1)}, u32[]{:S(2)}, u32[]{:S(2)}) %collective-permute-start) | collective-permute-done | bytes 524320 | tf_op jit(solution)/shard_map/ppermute | solution.py:295
  21.8 0.1 shard_map.180
  21.9 12.4 %all_to_all.15.pieces = bf16[16,64,128]{2,1,0:T(8,128)(2,1)S(1)} all-to-all(bf16[16,64,128]{2,1,0:T(8,128)(2,1)S(1)} %bitcast.25), channel_id=1, replica_groups=mesh['row_0'=8,'row_1'=2,'col_0'=4,'col_1'=4] {'col_0','col_1'}, dimensions={0} | all-to-all | bytes 524288 | tf_op jit(solution)/shard_map/all_to_all | solution.py:291
  34.3 0.7 shard_map.181
  35.0 8.2 %all-to-all-start.1 = ((bf16[8,64,128]{2,1,0:T(8,128)(2,1)}), bf16[8,64,128]{2,1,0:T(8,128)(2,1)S(1)}, u32[]{:S(2)}, u32[]{:S(2)}) async-start(bf16[8,64,128]{2,1,0:T(8,128)(2,1)} %shard_map.181), calls=%async_computation.1 | async-start | bytes 262144 | tf_op jit(solution)/shard_map/all_to_all | solution.py:291
  43.2 5.7 %collective-permute-start.1 = (bf16[1024,128]{1,0:T(8,128)(2,1)S(1)}, bf16[1024,128]{1,0:T(8,128)(2,1)S(1)}, u32[]{:S(2)}, u32[]{:S(2)}) collective-permute-start(bf16[1024,128]{1,0:T(8,128)(2,1)S(1)} %get-tuple-element.26), channel_id=1, source_target_pairs={{16,32},{48,64},{80,96},{112,128},{144,160},{176,192},{208,224},{3... | collective-permute-start | bytes 786440 | tf_op jit(solution)/shard_map/ppermute | solution.py:327
  48.9 2.1 %collective-permute-start.2 = (bf16[4,128,256]{2,1,0:T(8,128)(2,1)S(1)}, bf16[4,128,256]{2,1,0:T(8,128)(2,1)S(1)}, u32[]{:S(2)}, u32[]{:S(2)}) collective-permute-start(bf16[4,128,256]{2,1,0:T(8,128)(2,1)S(1)} %get-tuple-element.27), channel_id=1, source_target_pairs={{0,1},{1,2},{2,3},{3,4},{4,5},{5,6},{6,7},{7,8},{8,9},{9,10},{10,1... | collective-permute-start | bytes 786440 | tf_op jit(solution)/shard_map/ppermute | solution.py:321
  51.0 1.3 %collective-permute-start.3 = (bf16[4,128,256]{2,1,0:T(8,128)(2,1)S(1)}, bf16[4,128,256]{2,1,0:T(8,128)(2,1)S(1)}, u32[]{:S(2)}, u32[]{:S(2)}) collective-permute-start(bf16[4,128,256]{2,1,0:T(8,128)(2,1)S(1)} %get-tuple-element.28), channel_id=1, source_target_pairs={{1,0},{2,1},{3,2},{4,3},{5,4},{6,5},{7,6},{8,7},{9,8},{10,9},{11,1... | collective-permute-start | bytes 786440 | tf_op jit(solution)/shard_map/ppermute | solution.py:321
  52.3 0.0 all-to-all-done.1.pieces
  52.3 0.7 %shard_map.182 = bf16[16,64,128]{2,1,0:T(8,128)(2,1)} custom-call(bf16[8,64,128]{2,1,0:T(8,128)(2,1)S(1)} %all-to-all-done.1.pieces), custom_call_target="tpu_custom_call" | custom-call | flops 500000 | bytes 1000000 | tf_op jit(solution)/shard_map/pallas_call | solution.py:215
  53.0 6.4 %all-to-all-start.2 = ((bf16[16,64,128]{2,1,0:T(8,128)(2,1)}), bf16[16,64,128]{2,1,0:T(8,128)(2,1)S(1)}, u32[]{:S(2)}, u32[]{:S(2)}) async-start(bf16[16,64,128]{2,1,0:T(8,128)(2,1)} %shard_map.182), calls=%async_computation.2 | async-start | bytes 524288 | tf_op jit(solution)/shard_map/all_to_all | solution.py:291
  59.5 0.0 collective-permute-done.1.far
  59.5 0.0 collective-permute-done.2.right
  59.5 0.0 collective-permute-done.3.left
  59.5 1.1 %shard_map.183 = (bf16[512,256]{1,0:T(8,128)(2,1)}, bf16[512,256]{1,0:T(8,128)(2,1)}, bf16[512,256]{1,0:T(8,128)(2,1)}, bf16[512,256]{1,0:T(8,128)(2,1)}) custom-call(s32[1]{0:T(128)} %bitcast.core_ref, bf16[2,1024,128]{2,1,0:T(8,128)(2,1)S(1)} %collective-permute-done.pair, bf16[1024,128]{1,0:T(8,128)(2,1)S(1)} %collective-permute-done.1.far, ...), custom_call_target="tpu_custom_call" | custom-call | flops 500000 | bytes 1000000 | tf_op jit(solution)/shard_map/pallas_call | solution.py:215
  60.6 8.1 %all-to-all-done.2 = bf16[16,64,128]{2,1,0:T(8,128)(2,1)S(1)} async-done(((bf16[16,64,128]{2,1,0:T(8,128)(2,1)}), bf16[16,64,128]{2,1,0:T(8,128)(2,1)S(1)}, u32[]{:S(2)}, u32[]{:S(2)}) %all-to-all-start.2) | async-done | bytes 262176 | tf_op jit(solution)/shard_map/all_to_all | solution.py:291
  68.7 0.4 collective-permute-start.4
  69.1 1.2 %collective-permute-done.4.other = bf16[1024,128]{1,0:T(8,128)(2,1)S(1)} collective-permute-done((bf16[1024,128]{1,0:T(8,128)(2,1)S(1)}, bf16[1024,128]{1,0:T(8,128)(2,1)S(1)}, u32[]{:S(2)}, u32[]{:S(2)}) %collective-permute-start.4) | collective-permute-done | bytes 262176 | tf_op jit(solution)/shard_map/ppermute | solution.py:295
  70.3 0.9 %shard_map.184 = (f32[602,256]{1,0:T(8,128)}, f32[256,256]{1,0:T(8,128)}, f32[41,256]{1,0:T(8,128)}) custom-call(s32[1]{0:T(128)} %bitcast.core_ref, bf16[1024,128]{1,0:T(8,128)(2,1)S(1)} %bitcast.24, bf16[1024,128]{1,0:T(8,128)(2,1)S(1)} %collective-permute-done.4.other), custom_call_target="tpu_custom_call" | custom-call | flops 500000 | bytes 1000000 | tf_op jit(solution)/shard_map/pallas_call | solution.py:215
Async XLA Ops:
  17.0 4.8 %collective-permute-start = (bf16[2,1024,128]{2,1,0:T(8,128)(2,1)S(1)}, bf16[2,1024,128]{2,1,0:T(8,128)(2,1)S(1)}, u32[]{:S(2)}, u32[]{:S(2)}) collective-permute-start(bf16[2,1024,128]{2,1,0:T(8,128)(2,1)S(1)} %get-tuple-element.25), channel_id=1, source_target_pairs={{0,16},{16,0},{1,17},{17,1},{2,18},{18,2},{3,19},{19,3},{4,20},{20... | collective-permute-start | bytes 1572872 | tf_op jit(solution)/shard_map/ppermute | solution.py:295
  35.0 17.3 %all-to-all-start.1 = ((bf16[8,64,128]{2,1,0:T(8,128)(2,1)}), bf16[8,64,128]{2,1,0:T(8,128)(2,1)S(1)}, u32[]{:S(2)}, u32[]{:S(2)}) async-start(bf16[8,64,128]{2,1,0:T(8,128)(2,1)} %shard_map.181), calls=%async_computation.1 | async-start | bytes 262144 | tf_op jit(solution)/shard_map/all_to_all | solution.py:291
  43.2 16.3 %collective-permute-start.1 = (bf16[1024,128]{1,0:T(8,128)(2,1)S(1)}, bf16[1024,128]{1,0:T(8,128)(2,1)S(1)}, u32[]{:S(2)}, u32[]{:S(2)}) collective-permute-start(bf16[1024,128]{1,0:T(8,128)(2,1)S(1)} %get-tuple-element.26), channel_id=1, source_target_pairs={{16,32},{48,64},{80,96},{112,128},{144,160},{176,192},{208,224},{3... | collective-permute-start | bytes 786440 | tf_op jit(solution)/shard_map/ppermute | solution.py:327
  48.9 10.6 %collective-permute-start.2 = (bf16[4,128,256]{2,1,0:T(8,128)(2,1)S(1)}, bf16[4,128,256]{2,1,0:T(8,128)(2,1)S(1)}, u32[]{:S(2)}, u32[]{:S(2)}) collective-permute-start(bf16[4,128,256]{2,1,0:T(8,128)(2,1)S(1)} %get-tuple-element.27), channel_id=1, source_target_pairs={{0,1},{1,2},{2,3},{3,4},{4,5},{5,6},{6,7},{7,8},{8,9},{9,10},{10,1... | collective-permute-start | bytes 786440 | tf_op jit(solution)/shard_map/ppermute | solution.py:321
  51.0 8.5 %collective-permute-start.3 = (bf16[4,128,256]{2,1,0:T(8,128)(2,1)S(1)}, bf16[4,128,256]{2,1,0:T(8,128)(2,1)S(1)}, u32[]{:S(2)}, u32[]{:S(2)}) collective-permute-start(bf16[4,128,256]{2,1,0:T(8,128)(2,1)S(1)} %get-tuple-element.28), channel_id=1, source_target_pairs={{1,0},{2,1},{3,2},{4,3},{5,4},{6,5},{7,6},{8,7},{9,8},{10,9},{11,1... | collective-permute-start | bytes 786440 | tf_op jit(solution)/shard_map/ppermute | solution.py:321
  53.0 15.6 %all-to-all-start.2 = ((bf16[16,64,128]{2,1,0:T(8,128)(2,1)}), bf16[16,64,128]{2,1,0:T(8,128)(2,1)S(1)}, u32[]{:S(2)}, u32[]{:S(2)}) async-start(bf16[16,64,128]{2,1,0:T(8,128)(2,1)} %shard_map.182), calls=%async_computation.2 | async-start | bytes 524288 | tf_op jit(solution)/shard_map/all_to_all | solution.py:291
  68.7 1.6 %collective-permute-start.4 = (bf16[1024,128]{1,0:T(8,128)(2,1)S(1)}, bf16[1024,128]{1,0:T(8,128)(2,1)S(1)}, u32[]{:S(2)}, u32[]{:S(2)}) collective-permute-start(bf16[1024,128]{1,0:T(8,128)(2,1)S(1)} %bitcast.23), channel_id=1, source_target_pairs={{0,16},{16,0},{1,17},{17,1},{2,18},{18,2},{3,19},{19,3},{4,20},{20... | collective-permute-start | bytes 786440 | tf_op jit(solution)/shard_map/ppermute | solution.py:295

commit v6 on v5

--- a/solution.py
+++ b/solution.py
@@ -101,6 +101,18 @@
         pre_one[at, :] = pre
         hidden_one[at, :] = silu_of(pre).astype(BF)
 
+    half = packed.shape[2]
+    core = core_ref[0]
+    out = []
+
+    def place(array, n):
+        for k in range(2):
+            for h in range(2):
+                upright[k, pl.ds((2 * n + h) * bound, bound), :] = array[
+                    k * bound : (k + 1) * bound, h * half : (h + 1) * half
+                ].astype(BF)
+            sends[k, n] = array[(2 + k) * bound : (3 + k) * bound].astype(BF)
+
     def spread(values, remote, mixed):
         for c in range(CHUNKS):
             at = pl.ds(c * rows, rows)
@@ -125,16 +137,6 @@
     )[:, : logits.shape[1]]
     up_three = ((probs - target) / nodes).astype(BF)
 
-    half = packed.shape[2]
-
-    def place(array, n):
-        for k in range(2):
-            for h in range(2):
-                upright[k, pl.ds((2 * n + h) * bound, bound), :] = array[
-                    k * bound : (k + 1) * bound, h * half : (h + 1) * half
-                ].astype(BF)
-            sends[k, n] = array[(2 + k) * bound : (3 + k) * bound].astype(BF)
-
     def retract(across, returned):
         scaled[...] = (across * inverse[...]).astype(BF)
         carried = dot(local[...], scaled[...], (0, 0)) + scaled[...].astype(F32)
@@ -155,16 +157,16 @@
     pack(third_at, dot(up_three, mixed_three[...], (0, 0)))
     carried = retract(dot(up_three, w_three[...]), ret_three)
     place(dot(halo[...], scaled[...], (0, 0)), 3)
+    place(dot(hits[...], hidden_one[...], (0, 0)), 0)
+    place(dot(hits[...], hidden_two[...], (0, 0)), 1)
     up_two = (carried * slope(pre_two[...])).astype(BF)
     pack(0, dot(mixed_two[...], up_two, (0, 0)))
     carried = retract(dot(up_two, w_two[...], (1, 1)), ret_two)
     up_one = (carried * slope(pre_one[...])).astype(BF)
     pack(two, dot(mixed_one[...], up_one, (0, 0)))
-    core = core_ref[0]
-    out = [fetch(packed.at[1 - core], pair_out.at[0], out_sem.at[4]), fetch(packed.at[core], keep_out, out_sem.at[5])]
     place(dot(halo[...], scaled[...], (0, 0)), 2)
-    place(dot(hits[...], hidden_one[...], (0, 0)), 0)
-    place(dot(hits[...], hidden_two[...], (0, 0)), 1)
+    out.append(fetch(packed.at[1 - core], pair_out.at[0], out_sem.at[4]))
+    out.append(fetch(packed.at[core], keep_out, out_sem.at[5]))
     out += [
         fetch(upright.at[1 - core], pair_out.at[1], out_sem.at[0]),
         fetch(upright.at[core], far_out, out_sem.at[1]),
@@ -301,17 +303,16 @@
     own = small(add_kernel, pltpu.VMEM(keep.shape, BF), keep, pair)
     pieces = own.reshape(size, own.shape[0] // size, own.shape[1])
     pieces = exchanged(pieces, GROUP)
-    far, right = beside_in()
+    far = beside_in()
     own = repeated_sum(pieces, shares(FAR))
     pieces = exchanged(own, FAR)
-    left = beside_far()
+    right, left = beside_far()
     own = repeated_sum(pieces, size)
     mine = exchanged(own, GROUP).reshape(keep.shape)
+    other = swapped(mine)
     _, bound, half = right.shape
     outs = [jax.ShapeDtypeStruct((4 * bound, half), BF)] * 4
     outs = small(join_kernel, outs, core, pair, far, right, left)
-    mine, *outs = lax.optimization_barrier((mine, *outs))
-    other = swapped(mine)
     return mine, other, [out[None, None] for out in outs]
 
 
@@ -361,10 +362,10 @@
     )
 
     def beside_in():
-        return across_chips(far), shifted(right, COL, 1)
+        return across_chips(far)
 
     def beside_far():
-        return shifted(left, COL, -1)
+        return shifted(right, COL, 1), shifted(left, COL, -1)
 
     one, two, three = weight_first.shape[0], weight_second.shape[0], weight_third.shape[1]
     mine, other, outs = total_of(core, keep, pair, beside_in, beside_far)

time: 71.7 us -> 75.3 us (1.050); the launches traced: 71.2 us -> 73.9 us
  blocking collectives: 12.4 us -> 28.4 us
  starting transfers between devices: 27.4 us -> 18.6 us
  waiting for transfers between devices: 10.8 us -> 7.98 us
  Pallas kernels: 19.8 us -> 18.2 us
    all_to_all x1 -> x2, blocking collectives: 12.4 us -> 28.4 us  [exchanged(): return lax.all_to_all(pieces, axes, 0, 0, tiled=True)]
    all_to_all x2 -> x1, starting transfers between devices: 14.6 us -> 3.63 us  [exchanged(): return lax.all_to_all(pieces, axes, 0, 0, tiled=True)]
    all_to_all x2 -> x1, waiting for transfers between devices: 8.11 us -> 0.01 us  [exchanged(): return lax.all_to_all(pieces, axes, 0, 0, tiled=True)]
    ppermute x2, waiting for transfers between devices: 0.01 us -> 6.44 us  [shifted(): return lax.ppermute(block, axis, pairs)]
    ppermute x2, starting transfers between devices: 3.38 us -> 4.85 us  [shifted(): return lax.ppermute(block, axis, pairs)]
    ppermute x2, waiting for transfers between devices: 2.7 us -> 1.54 us  [swapped(): return lax.ppermute(half, PAIR, [(0, 1), (1, 0)])]
    ppermute x2, starting transfers between devices: 3.7 us -> 4.81 us  [swapped(): return lax.ppermute(half, PAIR, [(0, 1), (1, 0)])]
    pallas_call x1, Pallas kernels: 16.3 us -> 15.4 us  [step(): pl.pallas_call(step_kernel, out_shape=[half, v((2, ROWS, hidden // 2), BF...]
  transfers between devices with their start and end apart: 7 -> 6, of which waited for: 3 -> 3; matrix products, arithmetic and copies ran while one was open for 0% -> 0% of each run, Pallas kernels for 3% -> 1%
where the time goes in v6:
time: 75.3 us; the launch traced here: 73.9 us
  blocking collectives  28.4 us (38%)
  starting transfers between devices  18.6 us (25%)
  Pallas kernels  18.2 us (24%)
  waiting for transfers between devices  7.98 us (11%)
    all_to_all x2, blocking collectives, exchanged(): return lax.all_to_all(pieces, axes, 0, 0, tiled=True)  28.4 us
    pallas_call x1, Pallas kernels, step(): pl.pallas_call(step_kernel, out_shape=[half, v((2, ROWS, hidden // 2), BF...  15.4 us
    ppermute x2, waiting for transfers between devices, shifted(): return lax.ppermute(block, axis, pairs)  6.44 us
    ppermute x1, starting transfers between devices, across_chips(): return lax.ppermute(block, ROW, up + [(j, i) for i, j in up])  5.3 us
    ppermute x2, starting transfers between devices, shifted(): return lax.ppermute(block, axis, pairs)  4.85 us
    ppermute x2, starting transfers between devices, swapped(): return lax.ppermute(half, PAIR, [(0, 1), (1, 0)])  4.81 us
    all_to_all x1, starting transfers between devices, exchanged(): return lax.all_to_all(pieces, axes, 0, 0, tiled=True)  3.63 us
    pallas_call x5, Pallas kernels, small(): pl.pallas_call(kernel, out_shape=out_shape, in_specs=[pl.BlockSpec(memory...  2.87 us
  transfers between devices with their start and end apart: 6, of which 3 were waited for; matrix products, arithmetic and copies ran while one was open for 0% of the time, Pallas kernels for 1%

profile of v6, /device:TPU:1, one launch (start us, length us, event | category | flops | bytes accessed | tf_op | source)
XLA Modules:
  0.0 73.9 jit_solution(3050492928901488462)
XLA Ops:
  0.6 15.4 %step.1 = (bf16[1024,128]{1,0:T(8,128)(2,1)S(1)}, bf16[2,1024,128]{2,1,0:T(8,128)(2,1)S(1)}, bf16[1024,128]{1,0:T(8,128)(2,1)S(1)}, bf16[4,128,256]{2,1,0:T(8,128)(2,1)S(1)}, bf16[4,128,256]{2,1,0:T(8,128)(2,1)S(1)}) custom-call(s32[1]{0:T(128)} %bitcast.core_ref, s32[1,512]{1,0:T(1,128)} %bitcast.41, s32[1,1024]{1,0:T(1,128)} %bitcast.40, ...), custom_call_target="tpu_custom_call" | custom-call | flops 8000000000 | bytes 12000000 | tf_op jit(solution)/shard_map/step/pallas_call | solution.py:201
  16.0 3.3 %collective-permute-start = (bf16[2,1024,128]{2,1,0:T(8,128)(2,1)S(1)}, bf16[2,1024,128]{2,1,0:T(8,128)(2,1)S(1)}, u32[]{:S(2)}, u32[]{:S(2)}) collective-permute-start(bf16[2,1024,128]{2,1,0:T(8,128)(2,1)S(1)} %get-tuple-element.20), channel_id=1, source_target_pairs={{0,16},{16,0},{1,17},{17,1},{2,18},{18,2},{3,19},{19,3},{4,20},{20... | collective-permute-start | bytes 1572872 | tf_op jit(solution)/shard_map/ppermute | solution.py:297
  19.3 1.5 %collective-permute-done.pair = bf16[2,1024,128]{2,1,0:T(8,128)(2,1)S(1)} collective-permute-done((bf16[2,1024,128]{2,1,0:T(8,128)(2,1)S(1)}, bf16[2,1024,128]{2,1,0:T(8,128)(2,1)S(1)}, u32[]{:S(2)}, u32[]{:S(2)}) %collective-permute-start) | collective-permute-done | bytes 524320 | tf_op jit(solution)/shard_map/ppermute | solution.py:297
  20.8 0.1 shard_map.180
  20.9 12.4 %all_to_all.15.pieces = bf16[16,64,128]{2,1,0:T(8,128)(2,1)S(1)} all-to-all(bf16[16,64,128]{2,1,0:T(8,128)(2,1)S(1)} %bitcast.25), channel_id=1, replica_groups=mesh['row_0'=8,'row_1'=2,'col_0'=4,'col_1'=4] {'col_0','col_1'}, dimensions={0} | all-to-all | bytes 524288 | tf_op jit(solution)/shard_map/all_to_all | solution.py:293
  33.4 16.0 %all_to_all.16.pieces = bf16[8,64,128]{2,1,0:T(8,128)(2,1)S(1)} all-to-all(bf16[8,64,128]{2,1,0:T(8,128)(2,1)S(1)} %shard_map.181), channel_id=1, replica_groups=mesh['row_0'=8,'row_1'=2,'col_0'=4,'col_1'=4] {'row_0'}, dimensions={0} | all-to-all | bytes 262144 | tf_op jit(solution)/shard_map/all_to_all | solution.py:293
  49.4 0.7 shard_map.182
  50.1 3.6 %all-to-all-start.2 = ((bf16[16,64,128]{2,1,0:T(8,128)(2,1)}), bf16[16,64,128]{2,1,0:T(8,128)(2,1)S(1)}, u32[]{:S(2)}, u32[]{:S(2)}) async-start(bf16[16,64,128]{2,1,0:T(8,128)(2,1)} %shard_map.182), calls=%async_computation.2 | async-start | bytes 524288 | tf_op jit(solution)/shard_map/all_to_all | solution.py:293
  53.7 5.3 %collective-permute-start.2 = (bf16[1024,128]{1,0:T(8,128)(2,1)S(1)}, bf16[1024,128]{1,0:T(8,128)(2,1)S(1)}, u32[]{:S(2)}, u32[]{:S(2)}) collective-permute-start(bf16[1024,128]{1,0:T(8,128)(2,1)S(1)} %get-tuple-element.24), channel_id=1, source_target_pairs={{16,32},{48,64},{80,96},{112,128},{144,160},{176,192},{208,224},{3... | collective-permute-start | bytes 786440 | tf_op jit(solution)/shard_map/ppermute | solution.py:328
  59.1 3.6 %collective-permute-start.3 = (bf16[4,128,256]{2,1,0:T(8,128)(2,1)S(1)}, bf16[4,128,256]{2,1,0:T(8,128)(2,1)S(1)}, u32[]{:S(2)}, u32[]{:S(2)}) collective-permute-start(bf16[4,128,256]{2,1,0:T(8,128)(2,1)S(1)} %get-tuple-element.25), channel_id=1, source_target_pairs={{0,1},{1,2},{2,3},{3,4},{4,5},{5,6},{6,7},{7,8},{8,9},{9,10},{10,1... | collective-permute-start | bytes 786440 | tf_op jit(solution)/shard_map/ppermute | solution.py:322
  62.6 1.3 %collective-permute-start.4 = (bf16[4,128,256]{2,1,0:T(8,128)(2,1)S(1)}, bf16[4,128,256]{2,1,0:T(8,128)(2,1)S(1)}, u32[]{:S(2)}, u32[]{:S(2)}) collective-permute-start(bf16[4,128,256]{2,1,0:T(8,128)(2,1)S(1)} %get-tuple-element.26), channel_id=1, source_target_pairs={{1,0},{2,1},{3,2},{4,3},{5,4},{6,5},{7,6},{8,7},{9,8},{10,9},{11,1... | collective-permute-start | bytes 786440 | tf_op jit(solution)/shard_map/ppermute | solution.py:322
  63.9 0.0 all-to-all-done.2
  63.9 1.5 %collective-permute-start.1 = (bf16[1024,128]{1,0:T(8,128)(2,1)S(1)}, bf16[1024,128]{1,0:T(8,128)(2,1)S(1)}, u32[]{:S(2)}, u32[]{:S(2)}) collective-permute-start(bf16[1024,128]{1,0:T(8,128)(2,1)S(1)} %bitcast.23), channel_id=1, source_target_pairs={{0,16},{16,0},{1,17},{17,1},{2,18},{18,2},{3,19},{19,3},{4,20},{20... | collective-permute-start | bytes 786440 | tf_op jit(solution)/shard_map/ppermute | solution.py:297
  65.4 0.0 collective-permute-done.2.far
  65.4 2.3 %collective-permute-done.3.right = bf16[4,128,256]{2,1,0:T(8,128)(2,1)S(1)} collective-permute-done((bf16[4,128,256]{2,1,0:T(8,128)(2,1)S(1)}, bf16[4,128,256]{2,1,0:T(8,128)(2,1)S(1)}, u32[]{:S(2)}, u32[]{:S(2)}) %collective-permute-start.3) | collective-permute-done | bytes 262176 | tf_op jit(solution)/shard_map/ppermute | solution.py:322
  67.8 4.1 %collective-permute-done.4.left = bf16[4,128,256]{2,1,0:T(8,128)(2,1)S(1)} collective-permute-done((bf16[4,128,256]{2,1,0:T(8,128)(2,1)S(1)}, bf16[4,128,256]{2,1,0:T(8,128)(2,1)S(1)}, u32[]{:S(2)}, u32[]{:S(2)}) %collective-permute-start.4) | collective-permute-done | bytes 262176 | tf_op jit(solution)/shard_map/ppermute | solution.py:322
  71.9 1.1 %shard_map.184 = (bf16[512,256]{1,0:T(8,128)(2,1)}, bf16[512,256]{1,0:T(8,128)(2,1)}, bf16[512,256]{1,0:T(8,128)(2,1)}, bf16[512,256]{1,0:T(8,128)(2,1)}) custom-call(s32[1]{0:T(128)} %bitcast.core_ref, bf16[2,1024,128]{2,1,0:T(8,128)(2,1)S(1)} %collective-permute-done.pair, bf16[1024,128]{1,0:T(8,128)(2,1)S(1)} %collective-permute-done.2.far, ...), custom_call_target="tpu_custom_call" | custom-call | flops 500000 | bytes 1000000 | tf_op jit(solution)/shard_map/pallas_call | solution.py:217
  73.0 0.0 collective-permute-done.1.other
  73.0 0.9 %shard_map.183 = (f32[602,256]{1,0:T(8,128)}, f32[256,256]{1,0:T(8,128)}, f32[41,256]{1,0:T(8,128)}) custom-call(s32[1]{0:T(128)} %bitcast.core_ref, bf16[1024,128]{1,0:T(8,128)(2,1)S(1)} %bitcast.24, bf16[1024,128]{1,0:T(8,128)(2,1)S(1)} %collective-permute-done.1.other), custom_call_target="tpu_custom_call" | custom-call | flops 500000 | bytes 1000000 | tf_op jit(solution)/shard_map/pallas_call | solution.py:217
  (1 shorter events, 0.0 us)
Async XLA Ops:
  16.0 4.8 %collective-permute-start = (bf16[2,1024,128]{2,1,0:T(8,128)(2,1)S(1)}, bf16[2,1024,128]{2,1,0:T(8,128)(2,1)S(1)}, u32[]{:S(2)}, u32[]{:S(2)}) collective-permute-start(bf16[2,1024,128]{2,1,0:T(8,128)(2,1)S(1)} %get-tuple-element.20), channel_id=1, source_target_pairs={{0,16},{16,0},{1,17},{17,1},{2,18},{18,2},{3,19},{19,3},{4,20},{20... | collective-permute-start | bytes 1572872 | tf_op jit(solution)/shard_map/ppermute | solution.py:297
  50.1 13.8 %all-to-all-start.2 = ((bf16[16,64,128]{2,1,0:T(8,128)(2,1)}), bf16[16,64,128]{2,1,0:T(8,128)(2,1)S(1)}, u32[]{:S(2)}, u32[]{:S(2)}) async-start(bf16[16,64,128]{2,1,0:T(8,128)(2,1)} %shard_map.182), calls=%async_computation.2 | async-start | bytes 524288 | tf_op jit(solution)/shard_map/all_to_all | solution.py:293
  53.7 11.7 %collective-permute-start.2 = (bf16[1024,128]{1,0:T(8,128)(2,1)S(1)}, bf16[1024,128]{1,0:T(8,128)(2,1)S(1)}, u32[]{:S(2)}, u32[]{:S(2)}) collective-permute-start(bf16[1024,128]{1,0:T(8,128)(2,1)S(1)} %get-tuple-element.24), channel_id=1, source_target_pairs={{16,32},{48,64},{80,96},{112,128},{144,160},{176,192},{208,224},{3... | collective-permute-start | bytes 786440 | tf_op jit(solution)/shard_map/ppermute | solution.py:328
  59.1 8.7 %collective-permute-start.3 = (bf16[4,128,256]{2,1,0:T(8,128)(2,1)S(1)}, bf16[4,128,256]{2,1,0:T(8,128)(2,1)S(1)}, u32[]{:S(2)}, u32[]{:S(2)}) collective-permute-start(bf16[4,128,256]{2,1,0:T(8,128)(2,1)S(1)} %get-tuple-element.25), channel_id=1, source_target_pairs={{0,1},{1,2},{2,3},{3,4},{4,5},{5,6},{6,7},{7,8},{8,9},{9,10},{10,1... | collective-permute-start | bytes 786440 | tf_op jit(solution)/shard_map/ppermute | solution.py:322
  62.6 9.3 %collective-permute-start.4 = (bf16[4,128,256]{2,1,0:T(8,128)(2,1)S(1)}, bf16[4,128,256]{2,1,0:T(8,128)(2,1)S(1)}, u32[]{:S(2)}, u32[]{:S(2)}) collective-permute-start(bf16[4,128,256]{2,1,0:T(8,128)(2,1)S(1)} %get-tuple-element.26), channel_id=1, source_target_pairs={{1,0},{2,1},{3,2},{4,3},{5,4},{6,5},{7,6},{8,7},{9,8},{10,9},{11,1... | collective-permute-start | bytes 786440 | tf_op jit(solution)/shard_map/ppermute | solution.py:322
  63.9 9.0 %collective-permute-start.1 = (bf16[1024,128]{1,0:T(8,128)(2,1)S(1)}, bf16[1024,128]{1,0:T(8,128)(2,1)S(1)}, u32[]{:S(2)}, u32[]{:S(2)}) collective-permute-start(bf16[1024,128]{1,0:T(8,128)(2,1)S(1)} %bitcast.23), channel_id=1, source_target_pairs={{0,16},{16,0},{1,17},{17,1},{2,18},{18,2},{3,19},{19,3},{4,20},{20... | collective-permute-start | bytes 786440 | tf_op jit(solution)/shard_map/ppermute | solution.py:297
